TPU v7x, 256 devices: a whole 4x4x8 slice. The times are simulated.
256 devices in a mesh: ctx: 32 (over z, y), help: 8 (over x, core).
Axes of the slice: x: 4, y: 4, z: 8, core: 2. Of those that a mesh axis runs over, the one named last changes fastest.
Arguments:
- query_rows: bfloat16 [1, 32768, 2048], P(None, ('ctx', 'help')), may hold values from -126 to 126
- key_rows: bfloat16 [1, 32768, 2048], P(None, 'ctx'), may hold values from -6.5 to 6.5
- value_rows: bfloat16 [1, 32768, 2048], P(None, 'ctx'), may hold values from -6 to 6
- output_grad: bfloat16 [1, 32768, 2048], P(None, ('ctx', 'help')), may hold values from -96 to 96
- block_choice: int32 [1, 32768, 2], P(None, ('ctx', 'help')), may hold values from 0 to 31, as said below
Outputs:
- query_grad: bfloat16 [1, 32768, 2048], P(None, ('ctx', 'help'))
- key_grad: bfloat16 [1, 32768, 2048], P(None, ('ctx', 'help'))
- value_grad: bfloat16 [1, 32768, 2048], P(None, ('ctx', 'help'))
Inputs may be any that keep to these rules, and one draw needn't show every extreme that they name: `block_choice`: an entry names a block only where it is below the token's own block index; the entries of a token that name blocks name different blocks. In each aligned run of 128 rows of one sequence (the rows of one device) no block is named more than 8 times, and the devices of a sequence's third block name each of its first two blocks exactly 8 times. Blocks early in a sequence are named by the tokens of more blocks than late ones.
All inputs are finite; a program needn't handle non-finite values.
Results may differ from a plain program's by a relative error of at most 0.01.
Values may be sent and summed in bfloat16 or wider, within the bound.
No kernel may reach another device: no remote copies, remote signals or barrier semaphores. Data moves between devices by JAX's collectives and lax.ppermute only.
A program may use at most 192 MiB of HBM per device.

v0:
```python
import functools

import jax
import jax.numpy as jnp
from jax import lax
from jax.experimental import pallas as pl
from jax.experimental.pallas import tpu as pltpu
from jax.sharding import PartitionSpec as P

HEAD_DIM = 128
CAPACITY = 8
NEGATIVE = -1e30
LOG2E = 1.4426950408889634
LN2 = 0.6931471805599453
SCALING = HEAD_DIM ** (-0.5)
INFO = 16
TILE = 256
F32 = jnp.float32
BF16 = jnp.bfloat16


def iota(shape, dim):
    return lax.broadcasted_iota(jnp.int32, shape, dim)


def dot(a, b, ca, cb, precision=None):
    return lax.dot_general(
        a, b, (((ca,), (cb,)), ((), ())), precision=precision, preferred_element_type=F32
    )


def params(**kw):
    return pltpu.CompilerParams(**kw)


def pack_kernel(blocks, helpers, pos, choice, query, grad, sent, picker_out, *own):
    rows = query.shape[0]
    width = query.shape[1] // helpers
    center = pos[0]
    helper = pos[1]
    slots = blocks * CAPACITY
    targets = []
    matches = []
    block_ids = iota((blocks, rows), 0)
    for r in range(2):
        c = choice[r : r + 1, :]
        t = jnp.where(c < center, center - 1 - c, -1)
        targets.append(t)
        matches.append(block_ids == t)
    counts = jnp.where(matches[0], 1.0, 0.0) + jnp.where(matches[1], 1.0, 0.0)
    before = jnp.where(iota((rows, rows), 0) < iota((rows, rows), 1), 1.0, 0.0).astype(BF16)
    earlier = dot(counts.astype(BF16), before, 1, 0)
    picker = jnp.zeros((slots, rows), F32)
    places = []
    for r in range(2):
        p = jnp.sum(jnp.where(matches[r], earlier, 0.0), axis=0, keepdims=True)
        places.append(p)
        code = jnp.where(targets[r] >= 0, targets[r] * CAPACITY + p.astype(jnp.int32), -1)
        picker = picker + jnp.where(iota((slots, rows), 0) == code, 1.0, 0.0)
    picker_out[...] = picker.T.astype(BF16)
    low = picker.astype(BF16)
    for d in range(helpers):
        for n, source in enumerate((query, grad)):
            got = dot(low, source[:, d * width : (d + 1) * width], 1, 0)
            sent[:, d, :, n * width : (n + 1) * width] = got.reshape(
                blocks, CAPACITY, width
            ).astype(BF16)
    info = jnp.concatenate([t.astype(F32) for t in targets] + places, axis=1)
    info = jnp.broadcast_to(info, (INFO, info.shape[1])).astype(BF16)
    for k in range(helpers):
        cols = pl.ds(pl.multiple_of((helper ^ k) * width, width), width)
        own[k][0:rows, 0:width] = query[:, cols]
        own[k][0:rows, width : 2 * width] = grad[:, cols]
        own[k][rows : rows + INFO, :] = info


def tile_rows(own, helper, start, count, rows, cols):
    parts = [own[helper ^ g, 0:rows, cols] for g in range(start // rows, (start + count) // rows)]
    return jnp.concatenate(parts, axis=0)


def head_cols(head, heads, which):
    at = (which * heads + head) * HEAD_DIM
    return slice(at, at + HEAD_DIM)


def diagonal():
    return iota((TILE, TILE), 0) <= iota((TILE, TILE), 1)


def statistics_of(scores, products):
    highest = jnp.max(scores, axis=0, keepdims=True)
    weights = jnp.exp2(scores - highest)
    total = jnp.sum(weights, axis=0, keepdims=True)
    crossed = jnp.sum(weights * products, axis=0, keepdims=True)
    return highest + jnp.log(total) * LOG2E, crossed / total


def own_statistics_kernel(heads, helpers, pos, own, key, value, out):
    helper = pos[1]
    rows = own.shape[1] - INFO
    length = key.shape[0]
    keep = diagonal()
    for head in range(heads):
        hc = slice(head * HEAD_DIM, (head + 1) * HEAD_DIM)
        for start in range(0, length, TILE):
            end = start + TILE
            q = tile_rows(own, helper, start, TILE, rows, head_cols(head, heads, 0))
            g = tile_rows(own, helper, start, TILE, rows, head_cols(head, heads, 1))
            scores = dot(key[0:end, hc], q, 1, 1) * (SCALING * LOG2E)
            products = dot(value[0:end, hc], g, 1, 1)
            last = jnp.where(keep, scores[start:end], NEGATIVE)
            scores = jnp.concatenate([scores[0:start], last], axis=0) if start else last
            log_sum, mean = statistics_of(scores, products)
            out[2 * head : 2 * head + 1, start:end] = log_sum
            out[2 * head + 1 : 2 * head + 2, start:end] = mean
    for n in range(4):
        parts = [
            own[helper ^ g, rows : rows + INFO, n * rows : (n + 1) * rows].astype(F32)[0:1]
            for g in range(helpers)
        ]
        out[2 * heads + n : 2 * heads + n + 1, :] = jnp.concatenate(parts, axis=1)


def routed_statistics_kernel(heads, group, pos, rows, key, value, out):
    for head in range(heads):
        hc = slice(head * HEAD_DIM, (head + 1) * HEAD_DIM)
        scores = dot(key[:, hc], rows[:, head_cols(head, heads, 0)], 1, 1) * (SCALING * LOG2E)
        products = dot(value[:, hc], rows[:, head_cols(head, heads, 1)], 1, 1)
        log_sum, mean = statistics_of(scores, products)
        for a in range(TILE // group):
            cut = slice(a * group, (a + 1) * group)
            out[a, head : head + 1, 0:group] = log_sum[:, cut]
            out[a, head : head + 1, group : 2 * group] = mean[:, cut]


def combine_kernel(heads, helpers, stats, got, totals, slots):
    length = stats.shape[1]
    blocks = got.shape[0]
    group = got.shape[2] // 2
    rows = length // helpers
    exact = lax.Precision.HIGHEST
    slot = iota((group, length), 0)
    in_group = (slot // CAPACITY) == (iota((group, length), 1) // rows)
    slot_place = (slot % CAPACITY).astype(F32)
    block_ids = iota((blocks, length), 0).astype(F32)
    hots = []
    masks = []
    present = []
    for r in range(2):
        t = stats[2 * heads + r : 2 * heads + r + 1, :]
        p = stats[2 * heads + 2 + r : 2 * heads + 3 + r, :]
        present.append(t >= 0.0)
        hots.append(jnp.where(block_ids == t, 1.0, 0.0))
        masks.append(in_group & (slot_place == p) & (t >= 0.0))
    for head in range(heads):
        part = got[:, head, :]
        logs = [stats[2 * head : 2 * head + 1, :]]
        means = [stats[2 * head + 1 : 2 * head + 2, :]]
        for r in range(2):
            spread = dot(part, hots[r], 0, 0, exact)
            log_r = jnp.sum(jnp.where(masks[r], spread[0:group], 0.0), axis=0, keepdims=True)
            mean_r = jnp.sum(
                jnp.where(masks[r], spread[group : 2 * group], 0.0), axis=0, keepdims=True
            )
            logs.append(jnp.where(present[r], log_r, NEGATIVE))
            means.append(mean_r)
        top = jnp.maximum(jnp.maximum(logs[0], logs[1]), logs[2])
        shares = [jnp.exp2(v - top) for v in logs]
        norm = shares[0] + shares[1] + shares[2]
        log_total = top + jnp.log(norm) * LOG2E
        center = (shares[0] * means[0] + shares[1] * means[1] + shares[2] * means[2]) / norm
        totals[2 * head : 2 * head + 1, :] = log_total
        totals[2 * head + 1 : 2 * head + 2, :] = center
        result = jnp.zeros((blocks, 2 * group), F32)
        for r in range(2):
            both = jnp.concatenate(
                [jnp.where(masks[r], log_total, 0.0), jnp.where(masks[r], center, 0.0)], axis=0
            )
            result = result + dot(hots[r], both, 1, 1, exact)
        slots[:, head, :] = result


def own_gradients_kernel(heads, pos, own, key, value, totals, query_out, key_out, value_out):
    helper = pos[1]
    rows = own.shape[1] - INFO
    length = key.shape[0]
    keep = diagonal()
    for head in range(heads):
        hc = slice(head * HEAD_DIM, (head + 1) * HEAD_DIM)
        turned = key[:, hc].T
        for start in reversed(range(0, length, TILE)):
            end = start + TILE
            q = tile_rows(own, helper, start, TILE, rows, head_cols(head, heads, 0))
            g = tile_rows(own, helper, start, TILE, rows, head_cols(head, heads, 1))
            log_total = totals[2 * head : 2 * head + 1, start:end]
            center = totals[2 * head + 1 : 2 * head + 2, start:end]
            scores = dot(key[0:end, hc], q, 1, 1) * (SCALING * LOG2E)
            products = dot(value[0:end, hc], g, 1, 1)
            last = jnp.where(keep, scores[start:end], NEGATIVE)
            scores = jnp.concatenate([scores[0:start], last], axis=0) if start else last
            probs = jnp.exp2(scores - log_total)
            mixed = (probs * (products - center)).astype(BF16)
            value_new = dot(probs.astype(BF16), g, 1, 0)
            key_new = dot(mixed, q, 1, 0)
            if end == length:
                value_out[:, hc] = value_new
                key_out[:, hc] = key_new
            else:
                value_out[0:end, hc] += value_new
                key_out[0:end, hc] += key_new
            query_new = (dot(turned[:, 0:end], mixed, 1, 0) * SCALING).T
            for n in range(TILE // rows):
                query_out[helper ^ (start // rows + n), :, hc] = query_new[
                    n * rows : (n + 1) * rows
                ].astype(BF16)


def slot_row(slots, head, which, group):
    cut = slice(which * group, (which + 1) * group)
    return jnp.concatenate([slots[a, head : head + 1, cut] for a in range(TILE // group)], axis=1)


def routed_mixed(heads, group, head, rows, key, value, slots):
    hc = slice(head * HEAD_DIM, (head + 1) * HEAD_DIM)
    scores = dot(key[:, hc], rows[:, head_cols(head, heads, 0)], 1, 1) * (SCALING * LOG2E)
    products = dot(value[:, hc], rows[:, head_cols(head, heads, 1)], 1, 1)
    probs = jnp.exp2(scores - slot_row(slots, head, 0, group))
    mixed = (probs * (products - slot_row(slots, head, 1, group))).astype(BF16)
    return probs, mixed


def routed_query_kernel(heads, group, pos, rows, key, value, slots, out, turned):
    @pl.when(pl.program_id(0) == 0)
    def _():
        for head in range(heads):
            turned[head] = key[:, head * HEAD_DIM : (head + 1) * HEAD_DIM].T

    for head in range(heads):
        hc = slice(head * HEAD_DIM, (head + 1) * HEAD_DIM)
        _, mixed = routed_mixed(heads, group, head, rows, key, value, slots)
        out[:, hc] = (dot(turned[head], mixed, 1, 0) * SCALING).T.astype(BF16)


def routed_block_kernel(
    heads, group, helpers, pos, rows, key, value, slots, key_own, value_own, query_own, *rest
):
    pieces = rest[:helpers]
    key_acc, value_acc = rest[helpers:]
    step = pl.program_id(0)

    @pl.when(step == 0)
    def _():
        key_acc[...] = key_own[...]
        value_acc[...] = value_own[...]

    for head in range(heads):
        hc = slice(head * HEAD_DIM, (head + 1) * HEAD_DIM)
        probs, mixed = routed_mixed(heads, group, head, rows, key, value, slots)
        value_acc[:, hc] += dot(probs.astype(BF16), rows[:, head_cols(head, heads, 1)], 1, 0)
        key_acc[:, hc] += dot(mixed, rows[:, head_cols(head, heads, 0)], 1, 0)

    @pl.when(step == pl.num_programs(0) - 1)
    def _():
        width = key_acc.shape[1]
        share = key_acc.shape[0] // helpers
        for k in range(helpers):
            at = pl.ds(pl.multiple_of((pos[1] ^ k) * share, share), share)
            pieces[k][:, 0:width] = query_own[k]
            pieces[k][:, width : 2 * width] = (key_acc[at, :] * SCALING).astype(BF16)
            pieces[k][:, 2 * width : 3 * width] = value_acc[at, :].astype(BF16)


def place_kernel(helpers, pos, *refs):
    pieces = refs[:helpers]
    key_out, value_out = refs[helpers:]
    width = key_out.shape[1] // helpers
    for k in range(helpers):
        cols = pl.ds(pl.multiple_of((pos[1] ^ k) * width, width), width)
        key_out[:, cols] = pieces[k][:, width : 2 * width]
        value_out[:, cols] = pieces[k][:, 2 * width : 3 * width]


def finish_kernel(helpers, pos, picker, returned, *refs):
    pieces = refs[:helpers]
    out = refs[helpers]
    width = out.shape[1] // helpers
    slots = picker.shape[1]
    for k in range(helpers):
        d = pos[1] ^ k
        cols = pl.ds(pl.multiple_of(d * width, width), width)
        terms = returned[:, d].astype(F32).reshape(slots, width).astype(BF16)
        out[:, cols] = (dot(picker[...], terms, 1, 0) + pieces[k][:, 0:width].astype(F32)).astype(
            BF16
        )


def exchange(pieces, helpers):
    received = [pieces[0]]
    for k in range(1, helpers):
        received.append(lax.ppermute(pieces[k], "help", [(i, i ^ k) for i in range(helpers)]))
    return received


def whole(shape):
    return pl.BlockSpec(shape, lambda *_: (0,) * len(shape))


def per_device(query_rows, key_rows, value_rows, output_grad, block_choice):
    blocks = lax.axis_size("ctx")
    helpers = lax.axis_size("help")
    position = jnp.stack([lax.axis_index("ctx"), lax.axis_index("help")]).astype(jnp.int32)
    _, rows, features = query_rows.shape
    length = key_rows.shape[1]
    width = features // helpers
    heads = width // HEAD_DIM
    group = helpers * CAPACITY
    slots = blocks * CAPACITY
    total = blocks * group
    steps = total // TILE
    query, grad = query_rows[0], output_grad[0]
    key, value = key_rows[0], value_rows[0]
    choice = jnp.transpose(block_choice[0])
    shape = jax.ShapeDtypeStruct

    def call(kernel, out_shape, in_specs, out_specs, grid=(1,), scratch=(), name=None):
        return pl.pallas_call(
            kernel,
            out_shape=out_shape,
            grid_spec=pltpu.PrefetchScalarGridSpec(
                num_scalar_prefetch=1,
                grid=grid,
                in_specs=in_specs,
                out_specs=out_specs,
                scratch_shapes=scratch,
            ),
            name=name,
        )

    piece = shape((rows + INFO, 2 * width), BF16)
    packed = call(
        functools.partial(pack_kernel, blocks, helpers),
        [
            shape((blocks, helpers, CAPACITY, 2 * width), BF16),
            shape((rows, slots), BF16),
        ]
        + [piece] * helpers,
        [whole((2, rows)), whole((rows, features)), whole((rows, features))],
        [whole((blocks, helpers, CAPACITY, 2 * width)), whole((rows, slots))]
        + [whole(piece.shape)] * helpers,
        name="pack",
    )(position, choice, query, grad)
    sent, picker, pieces = packed[0], packed[1], packed[2:]

    own = jnp.stack(exchange(pieces, helpers))
    with jax.named_scope("dispatch"):
        routed = lax.all_to_all(
            sent.reshape(blocks * helpers, CAPACITY, 2 * width),
            ("ctx", "help"),
            split_axis=0,
            concat_axis=0,
            tiled=True,
        ).reshape(total, 2 * width)

    block_spec = pl.BlockSpec((length, width), lambda i, pos: (0, pos[1]))
    own_spec = whole((helpers, rows + INFO, 2 * width))
    stats = call(
        functools.partial(own_statistics_kernel, heads, helpers),
        shape((2 * heads + 4, length), F32),
        [own_spec, block_spec, block_spec],
        whole((2 * heads + 4, length)),
        name="own_statistics",
    )(position, own, key, value)

    row_spec = pl.BlockSpec((TILE, 2 * width), lambda i, pos: (i, 0))
    slot_spec = pl.BlockSpec((TILE // group, heads, 2 * group), lambda i, pos: (i, 0, 0))
    slot_shape = shape((blocks, heads, 2 * group), F32)
    parts = call(
        functools.partial(routed_statistics_kernel, heads, group),
        slot_shape,
        [row_spec, block_spec, block_spec],
        slot_spec,
        grid=(steps,),
        name="routed_statistics",
    )(position, routed, key, value)
    with jax.named_scope("parts"):
        parts = lax.all_to_all(parts, "ctx", split_axis=0, concat_axis=0, tiled=True)

    totals, spread = pl.pallas_call(
        functools.partial(combine_kernel, heads, helpers),
        out_shape=[shape((2 * heads, length), F32), slot_shape],
        name="combine",
    )(stats, parts)
    with jax.named_scope("totals"):
        spread = lax.all_to_all(spread, "ctx", split_axis=0, concat_axis=0, tiled=True)

    query_own, key_own, value_own = call(
        functools.partial(own_gradients_kernel, heads),
        [shape((helpers, rows, width), BF16), shape((length, width), F32), shape((length, width), F32)],
        [own_spec, block_spec, block_spec, whole((2 * heads, length))],
        [whole((helpers, rows, width)), whole((length, width)), whole((length, width))],
        name="own_gradients",
    )(position, own, key, value, totals)

    terms = call(
        functools.partial(routed_query_kernel, heads, group),
        shape((total, width), BF16),
        [row_spec, block_spec, block_spec, slot_spec],
        pl.BlockSpec((TILE, width), lambda i, pos: (i, 0)),
        grid=(steps,),
        scratch=[pltpu.VMEM((heads, HEAD_DIM, length), BF16)],
        name="routed_query",
    )(position, routed, key, value, spread)
    with jax.named_scope("back"):
        returned = lax.all_to_all(
            terms.reshape(blocks * helpers, CAPACITY, width),
            ("ctx", "help"),
            split_axis=0,
            concat_axis=0,
            tiled=True,
        ).reshape(blocks, helpers, CAPACITY, width)

    share = length // helpers
    piece = shape((share, 3 * width), BF16)
    pieces = call(
        functools.partial(routed_block_kernel, heads, group, helpers),
        [piece] * helpers,
        [
            row_spec,
            block_spec,
            block_spec,
            slot_spec,
            whole((length, width)),
            whole((length, width)),
            whole((helpers, rows, width)),
        ],
        [whole(piece.shape)] * helpers,
        grid=(steps,),
        scratch=[pltpu.VMEM((length, width), F32), pltpu.VMEM((length, width), F32)],
        name="routed_block",
    )(position, routed, key, value, spread, key_own, value_own, query_own)
    pieces = exchange(pieces, helpers)

    key_grad, value_grad = call(
        functools.partial(place_kernel, helpers),
        [shape((share, features), BF16)] * 2,
        [whole(piece.shape)] * helpers,
        [whole((share, features))] * 2,
        name="place",
    )(position, *pieces)
    query_grad = call(
        functools.partial(finish_kernel, helpers),
        shape((rows, features), BF16),
        [whole((rows, slots)), whole((blocks, helpers, CAPACITY, width))]
        + [whole(piece.shape)] * helpers,
        whole((rows, features)),
        name="finish",
    )(position, picker, returned, *pieces)
    return query_grad[None], key_grad[None], value_grad[None]


def solution(mesh):
    split = P(None, ("ctx", "help"), None)
    shared = P(None, "ctx", None)
    return jax.shard_map(
        per_device,
        mesh=mesh,
        in_specs=(split, shared, shared, split, split),
        out_specs=(split, split, split),
        check_vma=False,
    )
```

profile of v0, /device:TPU:1, one launch (start us, length us, event | category | flops | bytes accessed | tf_op | source)
XLA Modules:
  0.0 196.2 jit_solution(4219932305872547366)
XLA Ops:
  1.3 4.4 %pack.1 = (bf16[32,8,8,512]{3,2,1,0:T(8,128)(2,1)}, bf16[128,256]{1,0:T(8,128)(2,1)}, bf16[144,512]{1,0:T(8,128)(2,1)}, bf16[144,512]{1,0:T(8,128)(2,1)}, bf16[1...) custom-call(s32[2]{0:T(128)} %pad_add_fusion.pos, ...), custom_call_target="tpu_custom_call" | custom-call | tf_op jit(solution)/shard_map/pack/pallas_call | solution.py:341
  5.7 15.7 %all-to-all-start = ((bf16[256,8,512]{2,1,0:T(8,128)(2,1)}), bf16[256,8,512]{2,1,0:T(8,128)(2,1)S(1)}, u32[]{:S(2)}, u32[]{:S(2)}) async-start(bf16[256,8,512]{2,1,0:T(8,128)(2,1)} %bitcast.47), calls=%async_computation | async-start | bytes 4194304 | tf_op jit(solution)/shard_map/dispatch/all_to_all | solution.py:357
  32.5 6.4 %collective-permute-done.2 = bf16[144,512]{1,0:T(8,128)(2,1)S(1)} collective-permute-done((bf16[144,512]{1,0:T(8,128)(2,1)}, bf16[144,512]{1,0:T(8,128)(2,1)S(1)}, u32[]{:S(2)}, u32[]{:S(2)}) %collective-permute-start.2) | collective-permute-done | bytes 147488 | tf_op jit(solution)/shard_map/ppermute | solution.py:301
  38.9 4.1 %collective-permute-done.3 = bf16[144,512]{1,0:T(8,128)(2,1)S(1)} collective-permute-done((bf16[144,512]{1,0:T(8,128)(2,1)}, bf16[144,512]{1,0:T(8,128)(2,1)S(1)}, u32[]{:S(2)}, u32[]{:S(2)}) %collective-permute-start.3) | collective-permute-done | bytes 147488 | tf_op jit(solution)/shard_map/ppermute | solution.py:301
  43.0 5.9 %collective-permute-done.4 = bf16[144,512]{1,0:T(8,128)(2,1)S(1)} collective-permute-done((bf16[144,512]{1,0:T(8,128)(2,1)}, bf16[144,512]{1,0:T(8,128)(2,1)S(1)}, u32[]{:S(2)}, u32[]{:S(2)}) %collective-permute-start.4) | collective-permute-done | bytes 147488 | tf_op jit(solution)/shard_map/ppermute | solution.py:301
  49.5 24.6 %all-to-all-done = bf16[256,8,512]{2,1,0:T(8,128)(2,1)S(1)} async-done(((bf16[256,8,512]{2,1,0:T(8,128)(2,1)}), bf16[256,8,512]{2,1,0:T(8,128)(2,1)S(1)}, u32[]{:S(2)}, u32[]{:S(2)}) %all-to-all-start) | async-done | bytes 2097184 | tf_op jit(solution)/shard_map/dispatch/all_to_all | solution.py:357
  75.5 12.0 %routed_statistics.1 = f32[32,2,128]{2,1,0:T(2,128)} custom-call(s32[2]{0:T(128)} %pad_add_fusion.pos, bf16[2048,512]{1,0:T(8,128)(2,1)} %bitcast.42, bf16[1024,2048]{1,0:T(8,128)(2,1)} %bitcast.32, bf16[1024,2048]{1,0:T(8,128)(2,1)} %bitcast.37), custom_call_target="tpu_custom_call" | custom-call | tf_op jit(solution)/shard_map/routed_statistics/pallas_call | solution.py:378
  87.5 5.1 %all-to-all-start.1 = ((f32[32,2,128]{2,1,0:T(2,128)}), f32[32,2,128]{2,1,0:T(2,128)S(1)}, u32[]{:S(2)}, u32[]{:S(2)}) async-start(f32[32,2,128]{2,1,0:T(2,128)} %routed_statistics.1), calls=%async_computation.1 | async-start | bytes 65536 | tf_op jit(solution)/shard_map/parts/all_to_all | solution.py:387
  93.7 5.0 %own_statistics.1.stats = f32[8,1024]{1,0:T(8,128)} custom-call(s32[2]{0:T(128)} %pad_add_fusion.pos, bf16[8,144,512]{2,1,0:T(8,128)(2,1)} %copy-done.1, bf16[1024,2048]{1,0:T(8,128)(2,1)} %bitcast.33, bf16[1024,2048]{1,0:T(8,128)(2,1)} %bitcast.38), custom_call_target="tpu_custom_call" | custom-call | tf_op jit(solution)/shard_map/own_statistics/pallas_call | solution.py:367
  98.6 2.5 %all-to-all-done.1.got = f32[32,2,128]{2,1,0:T(2,128)S(1)} async-done(((f32[32,2,128]{2,1,0:T(2,128)}), f32[32,2,128]{2,1,0:T(2,128)S(1)}, u32[]{:S(2)}, u32[]{:S(2)}) %all-to-all-start.1) | async-done | bytes 32800 | tf_op jit(solution)/shard_map/parts/all_to_all | solution.py:387
  101.7 6.3 %combine.1 = (f32[4,1024]{1,0:T(4,128)}, f32[32,2,128]{2,1,0:T(2,128)}) custom-call(f32[8,1024]{1,0:T(8,128)} %own_statistics.1.stats, f32[32,2,128]{2,1,0:T(2,128)} %copy-done.11), custom_call_target="tpu_custom_call" | custom-call | tf_op jit(solution)/shard_map/combine/pallas_call | solution.py:389
  108.0 15.4 %all_to_all.20.slots = f32[32,2,128]{2,1,0:T(2,128)} all-to-all(f32[32,2,128]{2,1,0:T(2,128)} %get-tuple-element.38), channel_id=1, replica_groups=mesh['ctx'=32,'help'=8] {'ctx'}, dimensions={0} | all-to-all | bytes 65536 | tf_op jit(solution)/shard_map/totals/all_to_all | solution.py:395
  123.4 11.9 %routed_query.1 = bf16[2048,256]{1,0:T(8,128)(2,1)} custom-call(s32[2]{0:T(128)} %pad_add_fusion.pos, bf16[2048,512]{1,0:T(8,128)(2,1)} %bitcast.43, bf16[1024,2048]{1,0:T(8,128)(2,1)} %bitcast.34, bf16[1024,2048]{1,0:T(8,128)(2,1)} %bitcast.39, f32[32,2,128]{2,1,0:T(2,128)} %all_to_all.20.slots), custom_call_target="tpu_custom_call" | custom-call | tf_op jit(solution)/shard_map/routed_query/pallas_call | solution.py:405
  135.3 8.2 %all-to-all-start.3 = ((bf16[256,8,256]{2,1,0:T(8,128)(2,1)}), bf16[256,8,256]{2,1,0:T(8,128)(2,1)S(1)}, u32[]{:S(2)}, u32[]{:S(2)}) async-start(bf16[256,8,256]{2,1,0:T(8,128)(2,1)} %bitcast.45), calls=%async_computation.3 | async-start | bytes 2097152 | tf_op jit(solution)/shard_map/back/all_to_all | solution.py:415
  143.5 7.2 %own_gradients.1 = (bf16[8,128,256]{2,1,0:T(8,128)(2,1)}, f32[1024,256]{1,0:T(8,128)}, f32[1024,256]{1,0:T(8,128)}) custom-call(s32[2]{0:T(128)} %pad_add_fusion.pos, bf16[8,144,512]{2,1,0:T(8,128)(2,1)} %copy-done.1, bf16[1024,2048]{1,0:T(8,128)(2,1)} %bitcast.35, bf16[1024,2048]{1,0:T(8,128)(2,1)} %bitcast.40, f32[4,1024]{1,0:T(4,128)} %get-tuple-element.39.totals), custom_call_target="tpu_custom_call" | custom-call | tf_op jit(solution)/shard_map/own_gradients/pallas_call | solution.py:397
  150.7 14.7 %routed_block.1 = (bf16[128,768]{1,0:T(8,128)(2,1)}, bf16[128,768]{1,0:T(8,128)(2,1)}, bf16[128,768]{1,0:T(8,128)(2,1)}, bf16[128,768]{1,0:T(8,128)(2,1)}, bf16[...) custom-call(s32[2]{0:T(128)} %pad_add_fusion.pos, ...), custom_call_target="tpu_custom_call" | custom-call | tf_op jit(solution)/shard_map/routed_block/pallas_call | solution.py:425
  165.4 2.9 %collective-permute-start.10 = (bf16[128,768]{1,0:T(8,128)(2,1)}, bf16[128,768]{1,0:T(8,128)(2,1)S(1)}, u32[]{:S(2)}, u32[]{:S(2)}) collective-permute-start(bf16[128,768]{1,0:T(8,128)(2,1)} %get-tuple-element.47), channel_id=1, source_target_pairs={{0,4},{1,5},{2,6},{3,7},{4,0},{5,1},{6,2},{7,3},{8,12},{9,13},{10,... | collective-permute-start | bytes 589832 | tf_op jit(solution)/shard_map/ppermute | solution.py:301
  168.3 2.8 %collective-permute-start.11 = (bf16[128,768]{1,0:T(8,128)(2,1)}, bf16[128,768]{1,0:T(8,128)(2,1)S(1)}, u32[]{:S(2)}, u32[]{:S(2)}) collective-permute-start(bf16[128,768]{1,0:T(8,128)(2,1)} %get-tuple-element.48), channel_id=1, source_target_pairs={{0,5},{1,4},{2,7},{3,6},{4,1},{5,0},{6,3},{7,2},{8,13},{9,12},{10,... | collective-permute-start | bytes 589832 | tf_op jit(solution)/shard_map/ppermute | solution.py:301
  171.8 2.3 %collective-permute-start.7 = (bf16[128,768]{1,0:T(8,128)(2,1)}, bf16[128,768]{1,0:T(8,128)(2,1)S(1)}, u32[]{:S(2)}, u32[]{:S(2)}) collective-permute-start(bf16[128,768]{1,0:T(8,128)(2,1)} %get-tuple-element.44), channel_id=1, source_target_pairs={{0,1},{1,0},{2,3},{3,2},{4,5},{5,4},{6,7},{7,6},{8,9},{9,8},{10,11... | collective-permute-start | bytes 589832 | tf_op jit(solution)/shard_map/ppermute | solution.py:301
  175.3 3.7 %collective-permute-done.11.refs_5_ = bf16[128,768]{1,0:T(8,128)(2,1)S(1)} collective-permute-done((bf16[128,768]{1,0:T(8,128)(2,1)}, bf16[128,768]{1,0:T(8,128)(2,1)S(1)}, u32[]{:S(2)}, u32[]{:S(2)}) %collective-permute-start.11) | collective-permute-done | bytes 196640 | tf_op jit(solution)/shard_map/ppermute | solution.py:301
  179.8 3.6 %collective-permute-done.12.refs_6_ = bf16[128,768]{1,0:T(8,128)(2,1)S(1)} collective-permute-done((bf16[128,768]{1,0:T(8,128)(2,1)}, bf16[128,768]{1,0:T(8,128)(2,1)S(1)}, u32[]{:S(2)}, u32[]{:S(2)}) %collective-permute-start.12) | collective-permute-done | bytes 196640 | tf_op jit(solution)/shard_map/ppermute | solution.py:301
  183.5 4.2 %collective-permute-done.13.refs_7_ = bf16[128,768]{1,0:T(8,128)(2,1)S(1)} collective-permute-done((bf16[128,768]{1,0:T(8,128)(2,1)}, bf16[128,768]{1,0:T(8,128)(2,1)S(1)}, u32[]{:S(2)}, u32[]{:S(2)}) %collective-permute-start.13) | collective-permute-done | bytes 196640 | tf_op jit(solution)/shard_map/ppermute | solution.py:301
  188.6 3.2 %place.1 = (bf16[128,2048]{1,0:T(8,128)(2,1)}, bf16[128,2048]{1,0:T(8,128)(2,1)}) custom-call(s32[2]{0:T(128)} %pad_add_fusion.pos, bf16[128,768]{1,0:T(8,128)(2,1)} %get-tuple-element.43.refs_0_, bf16[128,768]{1,0:T(8,128)(2,1)} %copy-done.7, bf16[128,768]{1,0:T(8,128)(2,1)} %copy-done.8, bf16[128,768]{1,0:T(8,128)(2,1)} %copy-done.9, ...), custom_call_target="tpu_custom_call" | custom-call | tf_op jit(solution)/shard_map/place/pallas_call | solution.py:444
  192.8 3.5 %finish.1 = bf16[128,2048]{1,0:T(8,128)(2,1)} custom-call(s32[2]{0:T(128)} %pad_add_fusion.pos, bf16[128,256]{1,0:T(8,128)(2,1)} %get-tuple-element.28.picker, bf16[32,8,8,256]{3,2,1,0:T(8,128)(2,1)} %bitcast.46, bf16[128,768]{1,0:T(8,128)(2,1)} %get-tuple-element.43.refs_0_, bf16[128,768]{1,0:T(8,128)(2,1)} %copy-done.7, bf16[128,768]{1,0:T(8,128)(2,1)} %copy-done.8, ...), custom_call_target="tpu_custom_call" | custom-call | tf_op jit(solution)/shard_map/finish/pallas_call | solution.py:451
  (53 shorter events, 20.0 us)
Async XLA Ops:
  5.7 22.9 %copy-start.10 = (bf16[144,512]{1,0:T(8,128)(2,1)S(1)}, bf16[144,512]{1,0:T(8,128)(2,1)}, u32[]{:S(2)}) copy-start(bf16[144,512]{1,0:T(8,128)(2,1)} %get-tuple-element.30) | copy-start | bytes 442372
  5.7 68.5 %all-to-all-start = ((bf16[256,8,512]{2,1,0:T(8,128)(2,1)}), bf16[256,8,512]{2,1,0:T(8,128)(2,1)S(1)}, u32[]{:S(2)}, u32[]{:S(2)}) async-start(bf16[256,8,512]{2,1,0:T(8,128)(2,1)} %bitcast.47), calls=%async_computation | async-start | bytes 4194304 | tf_op jit(solution)/shard_map/dispatch/all_to_all | solution.py:357
  21.4 7.2 %collective-permute-start = (bf16[144,512]{1,0:T(8,128)(2,1)}, bf16[144,512]{1,0:T(8,128)(2,1)S(1)}, u32[]{:S(2)}, u32[]{:S(2)}) collective-permute-start(bf16[144,512]{1,0:T(8,128)(2,1)} %get-tuple-element.31), channel_id=1, source_target_pairs={{0,1},{1,0},{2,3},{3,2},{4,5},{5,4},{6,7},{7,6},{8,9},{9,8},{10,11... | collective-permute-start | bytes 442376 | tf_op jit(solution)/shard_map/ppermute | solution.py:301
  23.6 6.9 %collective-permute-start.1 = (bf16[144,512]{1,0:T(8,128)(2,1)}, bf16[144,512]{1,0:T(8,128)(2,1)S(1)}, u32[]{:S(2)}, u32[]{:S(2)}) collective-permute-start(bf16[144,512]{1,0:T(8,128)(2,1)} %get-tuple-element.32), channel_id=1, source_target_pairs={{0,2},{1,3},{2,0},{3,1},{4,6},{5,7},{6,4},{7,5},{8,10},{9,11},{10,... | collective-permute-start | bytes 442376 | tf_op jit(solution)/shard_map/ppermute | solution.py:301
  23.6 15.3 %collective-permute-start.2 = (bf16[144,512]{1,0:T(8,128)(2,1)}, bf16[144,512]{1,0:T(8,128)(2,1)S(1)}, u32[]{:S(2)}, u32[]{:S(2)}) collective-permute-start(bf16[144,512]{1,0:T(8,128)(2,1)} %get-tuple-element.33), channel_id=1, source_target_pairs={{0,3},{1,2},{2,1},{3,0},{4,7},{5,6},{6,5},{7,4},{8,11},{9,10},{10,... | collective-permute-start | bytes 442376 | tf_op jit(solution)/shard_map/ppermute | solution.py:301
  25.3 17.7 %collective-permute-start.3 = (bf16[144,512]{1,0:T(8,128)(2,1)}, bf16[144,512]{1,0:T(8,128)(2,1)S(1)}, u32[]{:S(2)}, u32[]{:S(2)}) collective-permute-start(bf16[144,512]{1,0:T(8,128)(2,1)} %get-tuple-element.34), channel_id=1, source_target_pairs={{0,4},{1,5},{2,6},{3,7},{4,0},{5,1},{6,2},{7,3},{8,12},{9,13},{10,... | collective-permute-start | bytes 442376 | tf_op jit(solution)/shard_map/ppermute | solution.py:301
  26.4 22.4 %collective-permute-start.4 = (bf16[144,512]{1,0:T(8,128)(2,1)}, bf16[144,512]{1,0:T(8,128)(2,1)S(1)}, u32[]{:S(2)}, u32[]{:S(2)}) collective-permute-start(bf16[144,512]{1,0:T(8,128)(2,1)} %get-tuple-element.35), channel_id=1, source_target_pairs={{0,5},{1,4},{2,7},{3,6},{4,1},{5,0},{6,3},{7,2},{8,13},{9,12},{10,... | collective-permute-start | bytes 442376 | tf_op jit(solution)/shard_map/ppermute | solution.py:301
  28.6 20.9 %collective-permute-start.5 = (bf16[144,512]{1,0:T(8,128)(2,1)}, bf16[144,512]{1,0:T(8,128)(2,1)S(1)}, u32[]{:S(2)}, u32[]{:S(2)}) collective-permute-start(bf16[144,512]{1,0:T(8,128)(2,1)} %get-tuple-element.36), channel_id=1, source_target_pairs={{0,6},{1,7},{2,4},{3,5},{4,2},{5,3},{6,0},{7,1},{8,14},{9,15},{10,... | collective-permute-start | bytes 442376 | tf_op jit(solution)/shard_map/ppermute | solution.py:301
  30.5 62.1 %collective-permute-start.6 = (bf16[144,512]{1,0:T(8,128)(2,1)}, bf16[144,512]{1,0:T(8,128)(2,1)S(1)}, u32[]{:S(2)}, u32[]{:S(2)}) collective-permute-start(bf16[144,512]{1,0:T(8,128)(2,1)} %get-tuple-element.37), channel_id=1, source_target_pairs={{0,7},{1,6},{2,5},{3,4},{4,3},{5,2},{6,1},{7,0},{8,15},{9,14},{10,... | collective-permute-start | bytes 442376 | tf_op jit(solution)/shard_map/ppermute | solution.py:301
  74.2 1.3 copy-start
  87.5 13.6 %all-to-all-start.1 = ((f32[32,2,128]{2,1,0:T(2,128)}), f32[32,2,128]{2,1,0:T(2,128)S(1)}, u32[]{:S(2)}, u32[]{:S(2)}) async-start(f32[32,2,128]{2,1,0:T(2,128)} %routed_statistics.1), calls=%async_computation.1 | async-start | bytes 65536 | tf_op jit(solution)/shard_map/parts/all_to_all | solution.py:387
  92.6 1.0 copy-start.1
  135.3 56.5 %all-to-all-start.3 = ((bf16[256,8,256]{2,1,0:T(8,128)(2,1)}), bf16[256,8,256]{2,1,0:T(8,128)(2,1)S(1)}, u32[]{:S(2)}, u32[]{:S(2)}) async-start(bf16[256,8,256]{2,1,0:T(8,128)(2,1)} %bitcast.45), calls=%async_computation.3 | async-start | bytes 2097152 | tf_op jit(solution)/shard_map/back/all_to_all | solution.py:415
  165.4 8.7 %collective-permute-start.10 = (bf16[128,768]{1,0:T(8,128)(2,1)}, bf16[128,768]{1,0:T(8,128)(2,1)S(1)}, u32[]{:S(2)}, u32[]{:S(2)}) collective-permute-start(bf16[128,768]{1,0:T(8,128)(2,1)} %get-tuple-element.47), channel_id=1, source_target_pairs={{0,4},{1,5},{2,6},{3,7},{4,0},{5,1},{6,2},{7,3},{8,12},{9,13},{10,... | collective-permute-start | bytes 589832 | tf_op jit(solution)/shard_map/ppermute | solution.py:301
  168.3 10.8 %collective-permute-start.11 = (bf16[128,768]{1,0:T(8,128)(2,1)}, bf16[128,768]{1,0:T(8,128)(2,1)S(1)}, u32[]{:S(2)}, u32[]{:S(2)}) collective-permute-start(bf16[128,768]{1,0:T(8,128)(2,1)} %get-tuple-element.48), channel_id=1, source_target_pairs={{0,5},{1,4},{2,7},{3,6},{4,1},{5,0},{6,3},{7,2},{8,13},{9,12},{10,... | collective-permute-start | bytes 589832 | tf_op jit(solution)/shard_map/ppermute | solution.py:301
  171.0 12.4 %collective-permute-start.12 = (bf16[128,768]{1,0:T(8,128)(2,1)}, bf16[128,768]{1,0:T(8,128)(2,1)S(1)}, u32[]{:S(2)}, u32[]{:S(2)}) collective-permute-start(bf16[128,768]{1,0:T(8,128)(2,1)} %get-tuple-element.49), channel_id=1, source_target_pairs={{0,6},{1,7},{2,4},{3,5},{4,2},{5,3},{6,0},{7,1},{8,14},{9,15},{10,... | collective-permute-start | bytes 589832 | tf_op jit(solution)/shard_map/ppermute | solution.py:301
  171.5 16.2 %collective-permute-start.13 = (bf16[128,768]{1,0:T(8,128)(2,1)}, bf16[128,768]{1,0:T(8,128)(2,1)S(1)}, u32[]{:S(2)}, u32[]{:S(2)}) collective-permute-start(bf16[128,768]{1,0:T(8,128)(2,1)} %get-tuple-element.50), channel_id=1, source_target_pairs={{0,7},{1,6},{2,5},{3,4},{4,3},{5,2},{6,1},{7,0},{8,15},{9,14},{10,... | collective-permute-start | bytes 589832 | tf_op jit(solution)/shard_map/ppermute | solution.py:301
  171.8 15.9 %collective-permute-start.7 = (bf16[128,768]{1,0:T(8,128)(2,1)}, bf16[128,768]{1,0:T(8,128)(2,1)S(1)}, u32[]{:S(2)}, u32[]{:S(2)}) collective-permute-start(bf16[128,768]{1,0:T(8,128)(2,1)} %get-tuple-element.44), channel_id=1, source_target_pairs={{0,1},{1,0},{2,3},{3,2},{4,5},{5,4},{6,7},{7,6},{8,9},{9,8},{10,11... | collective-permute-start | bytes 589832 | tf_op jit(solution)/shard_map/ppermute | solution.py:301
  174.1 13.6 %copy-start.3 = (bf16[128,768]{1,0:T(8,128)(2,1)}, bf16[128,768]{1,0:T(8,128)(2,1)S(1)}, u32[]{:S(2)}) copy-start(bf16[128,768]{1,0:T(8,128)(2,1)S(1)} %collective-permute-done.10.refs_4_) | copy-start | bytes 589828
  174.1 13.6 %collective-permute-start.8 = (bf16[128,768]{1,0:T(8,128)(2,1)}, bf16[128,768]{1,0:T(8,128)(2,1)S(1)}, u32[]{:S(2)}, u32[]{:S(2)}) collective-permute-start(bf16[128,768]{1,0:T(8,128)(2,1)} %get-tuple-element.45), channel_id=1, source_target_pairs={{0,2},{1,3},{2,0},{3,1},{4,6},{5,7},{6,4},{7,5},{8,10},{9,11},{10,... | collective-permute-start | bytes 589832 | tf_op jit(solution)/shard_map/ppermute | solution.py:301
  179.1 8.6 %copy-start.4 = (bf16[128,768]{1,0:T(8,128)(2,1)}, bf16[128,768]{1,0:T(8,128)(2,1)S(1)}, u32[]{:S(2)}) copy-start(bf16[128,768]{1,0:T(8,128)(2,1)S(1)} %collective-permute-done.11.refs_5_) | copy-start | bytes 589828
  179.1 8.6 %collective-permute-start.9 = (bf16[128,768]{1,0:T(8,128)(2,1)}, bf16[128,768]{1,0:T(8,128)(2,1)S(1)}, u32[]{:S(2)}, u32[]{:S(2)}) collective-permute-start(bf16[128,768]{1,0:T(8,128)(2,1)} %get-tuple-element.46), channel_id=1, source_target_pairs={{0,3},{1,2},{2,1},{3,0},{4,7},{5,6},{6,5},{7,4},{8,11},{9,10},{10,... | collective-permute-start | bytes 589832 | tf_op jit(solution)/shard_map/ppermute | solution.py:301
  183.5 4.3 %copy-start.5 = (bf16[128,768]{1,0:T(8,128)(2,1)}, bf16[128,768]{1,0:T(8,128)(2,1)S(1)}, u32[]{:S(2)}) copy-start(bf16[128,768]{1,0:T(8,128)(2,1)S(1)} %collective-permute-done.12.refs_6_) | copy-start | bytes 589828
  191.8 1.0 copy-start.2
  (5 other events, 3.8 us)
where the time goes:
time: 197 us; the launch traced here: 196 us
  Pallas kernels  68.1 us (35%)
  waiting for transfers between devices  56.6 us (29%)
  starting transfers between devices  49.7 us (25%)
  blocking collectives  15.4 us (8%)
  local copies, waits for them, and re-layouts  4.9 us (2%)
    ppermute x14, waiting for transfers between devices, exchange(): lax.ppermute(pieces[k], 'help', [(i, i ^ k) for i in range(helpers)])  29.5 us
    all_to_all x1, waiting for transfers between devices, per_device(): lax.all_to_all(sent.reshape(blocks * helpers, CAPACITY, 2 * width), ('ctx...  24.6 us
    ppermute x14, starting transfers between devices, exchange(): lax.ppermute(pieces[k], 'help', [(i, i ^ k) for i in range(helpers)])  20.8 us
    all_to_all x1, starting transfers between devices, per_device(): lax.all_to_all(sent.reshape(blocks * helpers, CAPACITY, 2 * width), ('ctx...  15.7 us
    all_to_all x1, blocking collectives, per_device(): lax.all_to_all(spread, 'ctx', split_axis=0, concat_axis=0, tiled=True)  15.4 us
    pallas_call x1, Pallas kernels, per_device(): call(functools.partial(routed_block_kernel, heads, group, helpers), [piec...  14.7 us
    pallas_call x1, Pallas kernels, per_device(): call(functools.partial(routed_statistics_kernel, heads, group), slot_shap...  12 us
    pallas_call x1, Pallas kernels, per_device(): call(functools.partial(routed_query_kernel, heads, group), shape((total,...  11.9 us
  transfers between devices with their start and end apart: 17, of which 10 were waited for; matrix products, arithmetic and copies ran while one was open for 0% of the time, Pallas kernels for 21%

commit v1 on v0

v1 whole, which is shorter than its diff:
```python
import functools

import jax
import jax.numpy as jnp
from jax import lax
from jax.experimental import pallas as pl
from jax.experimental.pallas import tpu as pltpu
from jax.sharding import PartitionSpec as P

HEAD_DIM = 128
CAPACITY = 8
NEGATIVE = -1e30
LOG2E = 1.4426950408889634
LN2 = 0.6931471805599453
SCALING = HEAD_DIM ** (-0.5)
INFO = 16
TILE = 256
CHUNK = 64
F32 = jnp.float32
BF16 = jnp.bfloat16


def iota(shape, dim):
    return lax.broadcasted_iota(jnp.int32, shape, dim)


def dot(a, b, ca, cb, precision=None):
    return lax.dot_general(
        a, b, (((ca,), (cb,)), ((), ())), precision=precision, preferred_element_type=F32
    )


def params(**kw):
    return pltpu.CompilerParams(**kw)


def pack_kernel(blocks, helpers, pos, choice, query, grad, sent, picker_out, *own):
    rows = query.shape[0]
    width = query.shape[1] // helpers
    center = pos[0]
    helper = pos[1]
    slots = blocks * CAPACITY
    targets = []
    matches = []
    block_ids = iota((blocks, rows), 0)
    for r in range(2):
        c = choice[r : r + 1, :]
        t = jnp.where(c < center, center - 1 - c, -1)
        targets.append(t)
        matches.append(block_ids == t)
    counts = jnp.where(matches[0], 1.0, 0.0) + jnp.where(matches[1], 1.0, 0.0)
    before = jnp.where(iota((rows, rows), 0) < iota((rows, rows), 1), 1.0, 0.0).astype(BF16)
    earlier = dot(counts.astype(BF16), before, 1, 0)
    picker = jnp.zeros((slots, rows), F32)
    places = []
    for r in range(2):
        p = jnp.sum(jnp.where(matches[r], earlier, 0.0), axis=0, keepdims=True)
        places.append(p)
        code = jnp.where(targets[r] >= 0, targets[r] * CAPACITY + p.astype(jnp.int32), -1)
        picker = picker + jnp.where(iota((slots, rows), 0) == code, 1.0, 0.0)
    picker_out[...] = picker.T.astype(BF16)
    low = picker.astype(BF16)
    for d in range(helpers):
        for n, source in enumerate((query, grad)):
            got = dot(low, source[:, d * width : (d + 1) * width], 1, 0)
            sent[d, :, :, n * width : (n + 1) * width] = got.reshape(
                blocks, CAPACITY, width
            ).astype(BF16)
    info = jnp.concatenate([t.astype(F32) for t in targets] + places, axis=1)
    info = jnp.broadcast_to(info, (INFO, info.shape[1])).astype(BF16)
    for k in range(helpers):
        cols = pl.ds(pl.multiple_of((helper ^ k) * width, width), width)
        own[k][0:rows, 0:width] = query[:, cols]
        own[k][0:rows, width : 2 * width] = grad[:, cols]
        own[k][rows : rows + INFO, :] = info


def head_cols(head, heads, which):
    at = (which * heads + head) * HEAD_DIM
    return slice(at, at + HEAD_DIM)


def cols_of(head):
    return slice(head * HEAD_DIM, (head + 1) * HEAD_DIM)


def own_tile(own, helper, start, rows, cols):
    parts = [own[helper ^ g, 0:rows, cols] for g in range(start // rows, (start + TILE) // rows)]
    return jnp.concatenate(parts, axis=0)


def routed_tile(routed, tile, cols):
    helpers, _, capacity, _ = routed.shape
    group = helpers * capacity
    count = TILE // group
    parts = [
        routed[:, tile * count + a, :, cols].astype(F32).reshape(group, HEAD_DIM)
        for a in range(count)
    ]
    return jnp.concatenate(parts, axis=0).astype(BF16)


def statistics_of(key, value, q, g, masked_from):
    scores = dot(key, q, 1, 1)
    products = dot(value, g, 1, 1)
    shape = (8, q.shape[0])
    highest = jnp.full(shape, NEGATIVE, F32)
    total = jnp.zeros(shape, F32)
    crossed = jnp.zeros(shape, F32)
    for at in range(0, key.shape[0], CHUNK):
        part = scores[at : at + CHUNK] * (SCALING * LOG2E)
        if masked_from is not None and at + CHUNK > masked_from:
            keep = iota(part.shape, 0) + (at - masked_from) <= iota(part.shape, 1)
            part = jnp.where(keep, part, NEGATIVE)
        part = part.reshape((CHUNK // 8,) + shape)
        newer = jnp.maximum(highest, jnp.max(part, axis=0))
        weights = jnp.exp2(part - newer)
        if masked_from is not None and at + CHUNK > masked_from:
            weights = jnp.where(keep.reshape(weights.shape), weights, 0.0)
        shrink = jnp.exp2(highest - newer)
        total = total * shrink + jnp.sum(weights, axis=0)
        crossed = crossed * shrink + jnp.sum(
            weights * products[at : at + CHUNK].reshape(part.shape), axis=0
        )
        highest = newer
    top = jnp.max(highest, axis=0, keepdims=True)
    shrink = jnp.exp2(highest - top)
    total = jnp.sum(total * shrink, axis=0, keepdims=True)
    crossed = jnp.sum(crossed * shrink, axis=0, keepdims=True)
    return top + jnp.log(total) * LOG2E, crossed / total


def own_statistics_kernel(heads, helpers, pos, own, key, value, out):
    helper = pos[1]
    rows = own.shape[1] - INFO
    length = key.shape[0]
    for head in range(heads):
        hc = cols_of(head)
        for start in range(0, length, TILE):
            end = start + TILE
            q = own_tile(own, helper, start, rows, head_cols(head, heads, 0))
            g = own_tile(own, helper, start, rows, head_cols(head, heads, 1))
            log_sum, mean = statistics_of(key[0:end, hc], value[0:end, hc], q, g, start)
            out[2 * head : 2 * head + 1, start:end] = log_sum
            out[2 * head + 1 : 2 * head + 2, start:end] = mean
    for n in range(4):
        parts = [
            own[helper ^ g, rows : rows + INFO, n * rows : (n + 1) * rows].astype(F32)[0:1]
            for g in range(helpers)
        ]
        out[2 * heads + n : 2 * heads + n + 1, :] = jnp.concatenate(parts, axis=1)


def routed_statistics_kernel(heads, routed, key, value, out):
    helpers, blocks, capacity, _ = routed.shape
    group = helpers * capacity
    count = TILE // group

    def body(tile, _):
        for head in range(heads):
            hc = cols_of(head)
            q = routed_tile(routed, tile, head_cols(head, heads, 0))
            g = routed_tile(routed, tile, head_cols(head, heads, 1))
            log_sum, mean = statistics_of(key[:, hc], value[:, hc], q, g, None)
            for a in range(count):
                cut = slice(a * group, (a + 1) * group)
                out[tile * count + a, head : head + 1, 0:group] = log_sum[:, cut]
                out[tile * count + a, head : head + 1, group : 2 * group] = mean[:, cut]
        return 0

    lax.fori_loop(0, blocks // count, body, 0)


def thirds(x, axis):
    high = x.astype(BF16)
    rest = x - high.astype(F32)
    middle = rest.astype(BF16)
    low = (rest - middle.astype(F32)).astype(BF16)
    return jnp.concatenate([high, middle, low], axis=axis)


def combine_kernel(heads, helpers, stats, got, totals, slots):
    length = stats.shape[1]
    blocks = got.shape[0]
    group = got.shape[2] // 2
    rows = length // helpers
    wide = 2 * group
    slot = iota((group, length), 0)
    in_group = (slot // CAPACITY) == (iota((group, length), 1) // rows)
    slot_place = (slot % CAPACITY).astype(F32)
    block_ids = iota((blocks, length), 0).astype(F32)
    hots = []
    masks = []
    present = []
    for r in range(2):
        t = stats[2 * heads + r : 2 * heads + r + 1, :]
        p = stats[2 * heads + 2 + r : 2 * heads + 3 + r, :]
        present.append(t >= 0.0)
        hots.append(jnp.where(block_ids == t, 1.0, 0.0).astype(BF16))
        masks.append(in_group & (slot_place == p) & (t >= 0.0))
    for head in range(heads):
        part = thirds(got[:, head, :].T, 1)
        logs = [stats[2 * head : 2 * head + 1, :]]
        means = [stats[2 * head + 1 : 2 * head + 2, :]]
        for r in range(2):
            hot = jnp.concatenate([hots[r]] * 3, axis=0)
            spread = dot(part, hot, 1, 0)
            log_r = jnp.sum(jnp.where(masks[r], spread[0:group], 0.0), axis=0, keepdims=True)
            mean_r = jnp.sum(jnp.where(masks[r], spread[group:wide], 0.0), axis=0, keepdims=True)
            logs.append(jnp.where(present[r], log_r, NEGATIVE))
            means.append(mean_r)
        top = jnp.maximum(jnp.maximum(logs[0], logs[1]), logs[2])
        shares = [jnp.exp2(v - top) for v in logs]
        norm = shares[0] + shares[1] + shares[2]
        log_total = top + jnp.log(norm) * LOG2E
        center = (shares[0] * means[0] + shares[1] * means[1] + shares[2] * means[2]) / norm
        totals[2 * head : 2 * head + 1, :] = log_total
        totals[2 * head + 1 : 2 * head + 2, :] = center
        logs3 = thirds(log_total, 0).astype(F32)
        means3 = thirds(center, 0).astype(F32)
        result = jnp.zeros((blocks, wide), F32)
        for r in range(2):
            for n in range(3):
                both = jnp.concatenate(
                    [
                        jnp.where(masks[r], logs3[n : n + 1], 0.0),
                        jnp.where(masks[r], means3[n : n + 1], 0.0),
                    ],
                    axis=0,
                ).astype(BF16)
                result = result + dot(hots[r], both, 1, 1)
        slots[:, head, :] = result


def mixed_into(mixed, probs, key, value, q, g, log_total, center, masked_from):
    scores = dot(key, q, 1, 1)
    products = dot(value, g, 1, 1)
    for at in range(0, key.shape[0], CHUNK):
        rows = slice(at, at + CHUNK)
        part = scores[rows] * (SCALING * LOG2E)
        if masked_from is not None and at + CHUNK > masked_from:
            keep = iota(part.shape, 0) + (at - masked_from) <= iota(part.shape, 1)
            part = jnp.where(keep, part, NEGATIVE)
        weights = jnp.exp2(part - log_total)
        if probs is not None:
            probs[rows, :] = weights.astype(BF16)
        mixed[rows, :] = (weights * (products[rows] - center)).astype(BF16)


def own_gradients_kernel(
    heads, pos, own, key, value, totals, query_out, key_out, value_out, mixed, probs
):
    helper = pos[1]
    rows = own.shape[1] - INFO
    length = key.shape[0]
    for head in range(heads):
        hc = cols_of(head)
        turned = key[:, hc].T
        for start in reversed(range(0, length, TILE)):
            end = start + TILE
            q = own_tile(own, helper, start, rows, head_cols(head, heads, 0))
            g = own_tile(own, helper, start, rows, head_cols(head, heads, 1))
            log_total = totals[2 * head : 2 * head + 1, start:end]
            center = totals[2 * head + 1 : 2 * head + 2, start:end]
            mixed_into(
                mixed, probs, key[0:end, hc], value[0:end, hc], q, g, log_total, center, start
            )
            value_new = dot(probs[0:end, :], g, 1, 0)
            key_new = dot(mixed[0:end, :], q, 1, 0)
            if end == length:
                value_out[:, hc] = value_new
                key_out[:, hc] = key_new
            else:
                value_out[0:end, hc] += value_new
                key_out[0:end, hc] += key_new
            query_new = (dot(turned[:, 0:end], mixed[0:end, :], 1, 0) * SCALING).T
            for n in range(TILE // rows):
                query_out[helper ^ (start // rows + n), :, hc] = query_new[
                    n * rows : (n + 1) * rows
                ].astype(BF16)


def slot_row(slots, tile, head, which, group):
    cut = slice(which * group, (which + 1) * group)
    count = TILE // group
    return jnp.concatenate(
        [slots[tile * count + a, head : head + 1, cut] for a in range(count)], axis=1
    )


def routed_query_kernel(heads, routed, key, value, slots, out, mixed):
    helpers, blocks, capacity, _ = routed.shape
    group = helpers * capacity
    count = TILE // group
    turned = [key[:, cols_of(head)].T for head in range(heads)]

    def body(tile, _):
        for head in range(heads):
            hc = cols_of(head)
            q = routed_tile(routed, tile, head_cols(head, heads, 0))
            g = routed_tile(routed, tile, head_cols(head, heads, 1))
            log_total = slot_row(slots, tile, head, 0, group)
            center = slot_row(slots, tile, head, 1, group)
            mixed_into(
                mixed.at[head], None, key[:, hc], value[:, hc], q, g, log_total, center, None
            )
            query_new = (dot(turned[head], mixed[head], 1, 0) * SCALING).T
            for a in range(count):
                out[:, tile * count + a, :, hc] = (
                    query_new[a * group : (a + 1) * group]
                    .reshape(helpers, capacity, HEAD_DIM)
                    .astype(BF16)
                )
        return 0

    lax.fori_loop(0, blocks // count, body, 0)


def routed_block_kernel(
    heads, helpers, pos, routed, key, value, slots, key_own, value_own, query_own, *rest
):
    pieces = rest[:helpers]
    key_acc, value_acc, mixed, probs = rest[helpers:]
    _, blocks, capacity, _ = routed.shape
    group = helpers * capacity
    key_acc[...] = key_own[...]
    value_acc[...] = value_own[...]

    def body(tile, _):
        for head in range(heads):
            hc = cols_of(head)
            q = routed_tile(routed, tile, head_cols(head, heads, 0))
            g = routed_tile(routed, tile, head_cols(head, heads, 1))
            log_total = slot_row(slots, tile, head, 0, group)
            center = slot_row(slots, tile, head, 1, group)
            mixed_into(
                mixed.at[head],
                probs.at[head],
                key[:, hc],
                value[:, hc],
                q,
                g,
                log_total,
                center,
                None,
            )
            value_acc[:, hc] += dot(probs[head], g, 1, 0)
            key_acc[:, hc] += dot(mixed[head], q, 1, 0)
        return 0

    lax.fori_loop(0, blocks * group // TILE, body, 0)
    width = key_acc.shape[1]
    share = key_acc.shape[0] // helpers
    for k in range(helpers):
        at = pl.ds(pl.multiple_of((pos[1] ^ k) * share, share), share)
        pieces[k][:, 0:width] = query_own[k]
        pieces[k][:, width : 2 * width] = (key_acc[at, :] * SCALING).astype(BF16)
        pieces[k][:, 2 * width : 3 * width] = value_acc[at, :].astype(BF16)


def place_kernel(helpers, pos, *refs):
    pieces = refs[:helpers]
    key_out, value_out = refs[helpers:]
    width = key_out.shape[1] // helpers
    for k in range(helpers):
        cols = pl.ds(pl.multiple_of((pos[1] ^ k) * width, width), width)
        key_out[:, cols] = pieces[k][:, width : 2 * width]
        value_out[:, cols] = pieces[k][:, 2 * width : 3 * width]


def finish_kernel(helpers, pos, picker, returned, *refs):
    pieces = refs[:helpers]
    out = refs[helpers]
    width = out.shape[1] // helpers
    slots = picker.shape[1]
    for k in range(helpers):
        d = pos[1] ^ k
        cols = pl.ds(pl.multiple_of(d * width, width), width)
        terms = returned[d].astype(F32).reshape(slots, width).astype(BF16)
        out[:, cols] = (dot(picker[...], terms, 1, 0) + pieces[k][:, 0:width].astype(F32)).astype(
            BF16
        )


def exchange(pieces, helpers):
    received = [pieces[0]]
    for k in range(1, helpers):
        received.append(lax.ppermute(pieces[k], "help", [(i, i ^ k) for i in range(helpers)]))
    return received


def call(kernel, out_shape, name, scratch=()):
    return pl.pallas_call(kernel, out_shape=out_shape, scratch_shapes=scratch, name=name)


def with_position(kernel, out_shape, name, operands, scratch=()):
    vmem = pl.BlockSpec(memory_space=pltpu.VMEM)
    return pl.pallas_call(
        kernel,
        out_shape=out_shape,
        in_specs=[pl.BlockSpec(memory_space=pltpu.SMEM)] + [vmem] * operands,
        scratch_shapes=scratch,
        name=name,
    )


def swap(array, axes):
    return lax.all_to_all(array, axes, split_axis=0, concat_axis=0, tiled=True)


def per_device(query_rows, key_rows, value_rows, output_grad, block_choice):
    blocks = lax.axis_size("ctx")
    helpers = lax.axis_size("help")
    helper = lax.axis_index("help")
    position = jnp.stack([lax.axis_index("ctx"), helper]).astype(jnp.int32)
    _, rows, features = query_rows.shape
    length = key_rows.shape[1]
    width = features // helpers
    heads = width // HEAD_DIM
    group = helpers * CAPACITY
    slots = blocks * CAPACITY
    shape = jax.ShapeDtypeStruct
    everyone = ("help", "ctx")

    piece = shape((rows + INFO, 2 * width), BF16)
    packed = with_position(
        functools.partial(pack_kernel, blocks, helpers),
        [
            shape((helpers, blocks, CAPACITY, 2 * width), BF16),
            shape((rows, slots), BF16),
        ]
        + [piece] * helpers,
        "pack",
        3,
    )(position, jnp.transpose(block_choice[0]), query_rows[0], output_grad[0])
    sent, picker, pieces = packed[0], packed[1], packed[2:]

    own = jnp.stack(exchange(pieces, helpers))
    with jax.named_scope("dispatch"):
        routed = swap(sent.reshape(blocks * helpers, CAPACITY, 2 * width), everyone)
    routed = routed.reshape(helpers, blocks, CAPACITY, 2 * width)

    key = lax.dynamic_slice_in_dim(key_rows[0], helper * width, width, 1)
    value = lax.dynamic_slice_in_dim(value_rows[0], helper * width, width, 1)
    stats = with_position(
        functools.partial(own_statistics_kernel, heads, helpers),
        shape((2 * heads + 4, length), F32),
        "own_statistics",
        3,
    )(position, own, key, value)

    slot_shape = shape((blocks, heads, 2 * group), F32)
    parts = call(
        functools.partial(routed_statistics_kernel, heads), slot_shape, "routed_statistics"
    )(routed, key, value)
    with jax.named_scope("parts"):
        parts = swap(parts, "ctx")

    totals, spread = call(
        functools.partial(combine_kernel, heads, helpers),
        [shape((2 * heads, length), F32), slot_shape],
        "combine",
    )(stats, parts)
    with jax.named_scope("totals"):
        spread = swap(spread, "ctx")

    tile = (heads, length, TILE)
    query_own, key_own, value_own = with_position(
        functools.partial(own_gradients_kernel, heads),
        [
            shape((helpers, rows, width), BF16),
            shape((length, width), F32),
            shape((length, width), F32),
        ],
        "own_gradients",
        4,
        [pltpu.VMEM(tile[1:], BF16), pltpu.VMEM(tile[1:], BF16)],
    )(position, own, key, value, totals)
    spread, query_own, key_own, value_own = lax.optimization_barrier(
        (spread, query_own, key_own, value_own)
    )

    terms = call(
        functools.partial(routed_query_kernel, heads),
        shape((helpers, blocks, CAPACITY, width), BF16),
        "routed_query",
        [pltpu.VMEM(tile, BF16)],
    )(routed, key, value, spread)
    with jax.named_scope("back"):
        returned = swap(terms.reshape(blocks * helpers, CAPACITY, width), everyone)
    returned = returned.reshape(helpers, blocks, CAPACITY, width)

    share = length // helpers
    pieces = with_position(
        functools.partial(routed_block_kernel, heads, helpers),
        [shape((share, 3 * width), BF16)] * helpers,
        "routed_block",
        7,
        [pltpu.VMEM((length, width), F32)] * 2 + [pltpu.VMEM(tile, BF16)] * 2,
    )(position, routed, key, value, spread, key_own, value_own, query_own)
    pieces = exchange(pieces, helpers)

    key_grad, value_grad = with_position(
        functools.partial(place_kernel, helpers),
        [shape((share, features), BF16)] * 2,
        "place",
        helpers,
    )(position, *pieces)
    query_grad = with_position(
        functools.partial(finish_kernel, helpers),
        shape((rows, features), BF16),
        "finish",
        helpers + 2,
    )(position, picker, returned, *pieces)
    return query_grad[None], key_grad[None], value_grad[None]


def solution(mesh):
    split = P(None, ("ctx", "help"), None)
    shared = P(None, "ctx", None)
    return jax.shard_map(
        per_device,
        mesh=mesh,
        in_specs=(split, shared, shared, split, split),
        out_specs=(split, split, split),
        check_vma=False,
    )
```

time: 197 us -> 190 us (0.964)
  blocking collectives: 15.4 us -> 0 us
  Pallas kernels: 68.1 us -> 57.7 us
  local copies, waits for them, and re-layouts: 4.9 us -> 13.1 us
  starting transfers between devices: 49.7 us -> 57.1 us
  waiting for transfers between devices: 56.6 us -> 59.6 us
    all_to_all x1 -> x0, blocking collectives: 15.4 us -> none  [per_device(): lax.all_to_all(spread, 'ctx', split_axis=0, concat_axis=0, tiled=True)]
    pallas_call x9, Pallas kernels: 68.1 us -> 57.7 us  [the longest x1 14.1 us: per_device(): with_position(functools.partial(routed_block_kernel, heads, helpers), [sh...]
    all_to_all x3 -> x4, starting transfers between devices: 28.9 us -> 36.5 us  [swap(): return lax.all_to_all(array, axes, split_axis=0, concat_axis=0, tiled=True)]
    unnamed x31 -> x33, local copies, waits for them, and re-layouts: 4.88 us -> 9.89 us
    ppermute x14, waiting for transfers between devices: 29.5 us -> 31.9 us  [exchange(): lax.ppermute(pieces[k], 'help', [(i, i ^ k) for i in range(helpers)])]
    dynamic_slice x0 -> x1, local copies, waits for them, and re-layouts: none -> 2.28 us  [per_device(): value = lax.dynamic_slice_in_dim(value_rows[0], helper * width, width, 1)]
    all_to_all x3 -> x4, waiting for transfers between devices: 27.1 us -> 27.6 us  [swap(): return lax.all_to_all(array, axes, split_axis=0, concat_axis=0, tiled=True)]
  transfers between devices with their start and end apart: 17 -> 18, of which waited for: 10 -> 12; matrix products, arithmetic and copies ran while one was open for 0% -> 4% of each run, Pallas kernels for 21% -> 19%
where the time goes in v1:
time: 190 us; the launch traced here: 189 us
  waiting for transfers between devices  59.6 us (31%)
  Pallas kernels  57.7 us (30%)
  starting transfers between devices  57.1 us (30%)
  local copies, waits for them, and re-layouts  13.1 us (7%)
    all_to_all x4, starting transfers between devices, swap(): return lax.all_to_all(array, axes, split_axis=0, concat_axis=0, tiled=True)  36.5 us
    ppermute x14, waiting for transfers between devices, exchange(): lax.ppermute(pieces[k], 'help', [(i, i ^ k) for i in range(helpers)])  31.9 us
    all_to_all x4, waiting for transfers between devices, swap(): return lax.all_to_all(array, axes, split_axis=0, concat_axis=0, tiled=True)  27.6 us
    ppermute x14, starting transfers between devices, exchange(): lax.ppermute(pieces[k], 'help', [(i, i ^ k) for i in range(helpers)])  20.5 us
    pallas_call x1, Pallas kernels, per_device(): with_position(functools.partial(routed_block_kernel, heads, helpers), [sh...  14.1 us
    pallas_call x1, Pallas kernels, per_device(): call(functools.partial(routed_query_kernel, heads), shape((helpers, block...  11.8 us
    unnamed x33, local copies, waits for them, and re-layouts  9.89 us
    pallas_call x1, Pallas kernels, per_device(): call(functools.partial(routed_statistics_kernel, heads), slot_shape, 'rou...  9.35 us
  transfers between devices with their start and end apart: 18, of which 12 were waited for; matrix products, arithmetic and copies ran while one was open for 4% of the time, Pallas kernels for 19%

profile of v1, /device:TPU:1, one launch (start us, length us, event | category | flops | bytes accessed | tf_op | source)
XLA Modules:
  0.0 188.9 jit_solution(17887656592322772279)
XLA Ops:
  1.2 3.7 %pack.1 = (bf16[8,32,8,512]{3,2,1,0:T(8,128)(2,1)}, bf16[128,256]{1,0:T(8,128)(2,1)}, bf16[144,512]{1,0:T(8,128)(2,1)}, bf16[144,512]{1,0:T(8,128)(2,1)}, bf16[1...) custom-call(s32[2]{0:T(128)} %pad_add_fusion.pos, ...), custom_call_target="tpu_custom_call" | custom-call | tf_op jit(solution)/shard_map/pack/pallas_call | solution.py:426
  5.0 15.7 %all-to-all-start = ((bf16[256,8,512]{2,1,0:T(8,128)(2,1)}), bf16[256,8,512]{2,1,0:T(8,128)(2,1)S(1)}, u32[]{:S(2)}, u32[]{:S(2)}) async-start(bf16[256,8,512]{2,1,0:T(8,128)(2,1)} %bitcast.39), calls=%async_computation | async-start | bytes 4194304 | tf_op jit(solution)/shard_map/dispatch/all_to_all | solution.py:408
  38.5 4.1 %collective-permute-done.3 = bf16[144,512]{1,0:T(8,128)(2,1)} collective-permute-done((bf16[144,512]{1,0:T(8,128)(2,1)}, bf16[144,512]{1,0:T(8,128)(2,1)}, u32[]{:S(2)}, u32[]{:S(2)}) %collective-permute-start.3) | collective-permute-done | bytes 147488 | tf_op jit(solution)/shard_map/ppermute | solution.py:388
  43.5 5.2 %collective-permute-done.4 = bf16[144,512]{1,0:T(8,128)(2,1)S(1)} collective-permute-done((bf16[144,512]{1,0:T(8,128)(2,1)}, bf16[144,512]{1,0:T(8,128)(2,1)S(1)}, u32[]{:S(2)}, u32[]{:S(2)}) %collective-permute-start.4) | collective-permute-done | bytes 147488 | tf_op jit(solution)/shard_map/ppermute | solution.py:388
  48.7 2.6 %collective-permute-done.5 = bf16[144,512]{1,0:T(8,128)(2,1)S(1)} collective-permute-done((bf16[144,512]{1,0:T(8,128)(2,1)S(1)}, bf16[144,512]{1,0:T(8,128)(2,1)S(1)}, u32[]{:S(2)}, u32[]{:S(2)}) %collective-permute-start.5) | collective-permute-done | bytes 147488 | tf_op jit(solution)/shard_map/ppermute | solution.py:388
  51.3 23.0 %all-to-all-done = bf16[256,8,512]{2,1,0:T(8,128)(2,1)S(1)} async-done(((bf16[256,8,512]{2,1,0:T(8,128)(2,1)}), bf16[256,8,512]{2,1,0:T(8,128)(2,1)S(1)}, u32[]{:S(2)}, u32[]{:S(2)}) %all-to-all-start) | async-done | bytes 2097184 | tf_op jit(solution)/shard_map/dispatch/all_to_all | solution.py:408
  75.7 9.4 %routed_statistics.1 = f32[32,2,128]{2,1,0:T(2,128)} custom-call(bf16[8,32,8,512]{3,2,1,0:T(8,128)(2,1)} %bitcast.34, bf16[1024,256]{1,0:T(8,128)(2,1)} %get-tuple-element.62.key, bf16[1024,256]{1,0:T(8,128)(2,1)} %get-tuple-element.61.value), custom_call_target="tpu_custom_call" | custom-call | tf_op jit(solution)/shard_map/routed_statistics/pallas_call | solution.py:453
  85.0 3.8 %all-to-all-start.1 = ((f32[32,2,128]{2,1,0:T(2,128)}), f32[32,2,128]{2,1,0:T(2,128)S(1)}, u32[]{:S(2)}, u32[]{:S(2)}) async-start(f32[32,2,128]{2,1,0:T(2,128)} %routed_statistics.1), calls=%async_computation.1 | async-start | bytes 65536 | tf_op jit(solution)/shard_map/parts/all_to_all | solution.py:408
  90.8 3.9 %own_statistics.1.stats = f32[8,1024]{1,0:T(8,128)} custom-call(s32[2]{0:T(128)} %pad_add_fusion.pos, bf16[8,144,512]{2,1,0:T(8,128)(2,1)} %copy-done.1, bf16[1024,256]{1,0:T(8,128)(2,1)} %get-tuple-element.62.key, bf16[1024,256]{1,0:T(8,128)(2,1)} %get-tuple-element.61.value), custom_call_target="tpu_custom_call" | custom-call | tf_op jit(solution)/shard_map/own_statistics/pallas_call | solution.py:445
  94.7 2.8 %all-to-all-done.1.got = f32[32,2,128]{2,1,0:T(2,128)S(1)} async-done(((f32[32,2,128]{2,1,0:T(2,128)}), f32[32,2,128]{2,1,0:T(2,128)S(1)}, u32[]{:S(2)}, u32[]{:S(2)}) %all-to-all-start.1) | async-done | bytes 32800 | tf_op jit(solution)/shard_map/parts/all_to_all | solution.py:408
  98.1 2.9 %combine.1 = (f32[4,1024]{1,0:T(4,128)}, f32[32,2,128]{2,1,0:T(2,128)}) custom-call(f32[8,1024]{1,0:T(8,128)} %own_statistics.1.stats, f32[32,2,128]{2,1,0:T(2,128)} %copy-done.11), custom_call_target="tpu_custom_call" | custom-call | tf_op jit(solution)/shard_map/combine/pallas_call | solution.py:459
  100.9 6.6 %all-to-all-start.2 = ((f32[32,2,128]{2,1,0:T(2,128)}), f32[32,2,128]{2,1,0:T(2,128)S(1)}, u32[]{:S(2)}, u32[]{:S(2)}) async-start(f32[32,2,128]{2,1,0:T(2,128)} %get-tuple-element.42), calls=%async_computation.2 | async-start | bytes 65536 | tf_op jit(solution)/shard_map/totals/all_to_all | solution.py:408
  107.6 6.6 %own_gradients.1 = (bf16[8,128,256]{2,1,0:T(8,128)(2,1)}, f32[1024,256]{1,0:T(8,128)}, f32[1024,256]{1,0:T(8,128)}) custom-call(s32[2]{0:T(128)} %pad_add_fusion.pos, bf16[8,144,512]{2,1,0:T(8,128)(2,1)} %copy-done.1, bf16[1024,256]{1,0:T(8,128)(2,1)} %get-tuple-element.62.key, bf16[1024,256]{1,0:T(8,128)(2,1)} %get-tuple-element.61.value, ...), custom_call_target="tpu_custom_call" | custom-call | tf_op jit(solution)/shard_map/own_gradients/pallas_call | solution.py:468
  116.7 11.8 %routed_query.1 = bf16[8,32,8,256]{3,2,1,0:T(8,128)(2,1)} custom-call(bf16[8,32,8,512]{3,2,1,0:T(8,128)(2,1)} %bitcast.35, bf16[1024,256]{1,0:T(8,128)(2,1)} %get-tuple-element.62.key, bf16[1024,256]{1,0:T(8,128)(2,1)} %get-tuple-element.61.value, f32[32,2,128]{2,1,0:T(2,128)} %copy-done.10), custom_call_target="tpu_custom_call" | custom-call | tf_op jit(solution)/shard_map/routed_query/pallas_call | solution.py:483
  128.5 10.4 %all-to-all-start.3 = ((bf16[256,8,256]{2,1,0:T(8,128)(2,1)}), bf16[256,8,256]{2,1,0:T(8,128)(2,1)S(1)}, u32[]{:S(2)}, u32[]{:S(2)}) async-start(bf16[256,8,256]{2,1,0:T(8,128)(2,1)} %bitcast.38), calls=%async_computation.3 | async-start | bytes 2097152 | tf_op jit(solution)/shard_map/back/all_to_all | solution.py:408
  138.9 14.1 %routed_block.1 = (bf16[128,768]{1,0:T(8,128)(2,1)}, bf16[128,768]{1,0:T(8,128)(2,1)}, bf16[128,768]{1,0:T(8,128)(2,1)}, bf16[128,768]{1,0:T(8,128)(2,1)}, bf16[...) custom-call(s32[2]{0:T(128)} %pad_add_fusion.pos, ...), custom_call_target="tpu_custom_call" | custom-call | tf_op jit(solution)/shard_map/routed_block/pallas_call | solution.py:494
  161.0 3.6 %collective-permute-done.8.refs_2_ = bf16[128,768]{1,0:T(8,128)(2,1)S(1)} collective-permute-done((bf16[128,768]{1,0:T(8,128)(2,1)}, bf16[128,768]{1,0:T(8,128)(2,1)S(1)}, u32[]{:S(2)}, u32[]{:S(2)}) %collective-permute-start.8) | collective-permute-done | bytes 196640 | tf_op jit(solution)/shard_map/ppermute | solution.py:388
  164.6 2.3 %collective-permute-start.13 = (bf16[128,768]{1,0:T(8,128)(2,1)}, bf16[128,768]{1,0:T(8,128)(2,1)S(1)}, u32[]{:S(2)}, u32[]{:S(2)}) collective-permute-start(bf16[128,768]{1,0:T(8,128)(2,1)} %get-tuple-element.58), channel_id=1, source_target_pairs={{0,7},{1,6},{2,5},{3,4},{4,3},{5,2},{6,1},{7,0},{8,15},{9,14},{10,... | collective-permute-start | bytes 589832 | tf_op jit(solution)/shard_map/ppermute | solution.py:388
  166.9 3.0 %collective-permute-done.9.refs_3_ = bf16[128,768]{1,0:T(8,128)(2,1)S(1)} collective-permute-done((bf16[128,768]{1,0:T(8,128)(2,1)}, bf16[128,768]{1,0:T(8,128)(2,1)S(1)}, u32[]{:S(2)}, u32[]{:S(2)}) %collective-permute-start.9) | collective-permute-done | bytes 196640 | tf_op jit(solution)/shard_map/ppermute | solution.py:388
  169.9 4.6 %collective-permute-done.10.refs_4_ = bf16[128,768]{1,0:T(8,128)(2,1)S(1)} collective-permute-done((bf16[128,768]{1,0:T(8,128)(2,1)}, bf16[128,768]{1,0:T(8,128)(2,1)S(1)}, u32[]{:S(2)}, u32[]{:S(2)}) %collective-permute-start.10) | collective-permute-done | bytes 196640 | tf_op jit(solution)/shard_map/ppermute | solution.py:388
  174.5 4.3 %collective-permute-done.11.refs_5_ = bf16[128,768]{1,0:T(8,128)(2,1)S(1)} collective-permute-done((bf16[128,768]{1,0:T(8,128)(2,1)}, bf16[128,768]{1,0:T(8,128)(2,1)S(1)}, u32[]{:S(2)}, u32[]{:S(2)}) %collective-permute-start.11) | collective-permute-done | bytes 196640 | tf_op jit(solution)/shard_map/ppermute | solution.py:388
  178.8 3.0 %collective-permute-done.13.refs_7_ = bf16[128,768]{1,0:T(8,128)(2,1)S(1)} collective-permute-done((bf16[128,768]{1,0:T(8,128)(2,1)}, bf16[128,768]{1,0:T(8,128)(2,1)S(1)}, u32[]{:S(2)}, u32[]{:S(2)}) %collective-permute-start.13) | collective-permute-done | bytes 196640 | tf_op jit(solution)/shard_map/ppermute | solution.py:388
  182.5 2.6 %place.1 = (bf16[128,2048]{1,0:T(8,128)(2,1)}, bf16[128,2048]{1,0:T(8,128)(2,1)}) custom-call(s32[2]{0:T(128)} %pad_add_fusion.pos, bf16[128,768]{1,0:T(8,128)(2,1)} %get-tuple-element.51.refs_0_, bf16[128,768]{1,0:T(8,128)(2,1)} %copy-done.3, bf16[128,768]{1,0:T(8,128)(2,1)} %copy-done.4, bf16[128,768]{1,0:T(8,128)(2,1)} %copy-done.5, ...), custom_call_target="tpu_custom_call" | custom-call | tf_op jit(solution)/shard_map/place/pallas_call | solution.py:503
  186.1 2.8 %finish.1 = bf16[128,2048]{1,0:T(8,128)(2,1)} custom-call(s32[2]{0:T(128)} %pad_add_fusion.pos, bf16[128,256]{1,0:T(8,128)(2,1)} %get-tuple-element.32.picker, bf16[8,32,8,256]{3,2,1,0:T(8,128)(2,1)} %bitcast.37, bf16[128,768]{1,0:T(8,128)(2,1)} %get-tuple-element.51.refs_0_, bf16[128,768]{1,0:T(8,128)(2,1)} %copy-done.3, bf16[128,768]{1,0:T(8,128)(2,1)} %copy-done.4, ...), custom_call_target="tpu_custom_call" | custom-call | tf_op jit(solution)/shard_map/finish/pallas_call | solution.py:509
  (57 shorter events, 35.4 us)
Async XLA Ops:
  5.0 69.3 %all-to-all-start = ((bf16[256,8,512]{2,1,0:T(8,128)(2,1)}), bf16[256,8,512]{2,1,0:T(8,128)(2,1)S(1)}, u32[]{:S(2)}, u32[]{:S(2)}) async-start(bf16[256,8,512]{2,1,0:T(8,128)(2,1)} %bitcast.39), calls=%async_computation | async-start | bytes 4194304 | tf_op jit(solution)/shard_map/dispatch/all_to_all | solution.py:408
  20.6 10.5 %collective-permute-start = (bf16[144,512]{1,0:T(8,128)(2,1)}, bf16[144,512]{1,0:T(8,128)(2,1)}, u32[]{:S(2)}, u32[]{:S(2)}) collective-permute-start(bf16[144,512]{1,0:T(8,128)(2,1)} %get-tuple-element.35), channel_id=1, source_target_pairs={{0,1},{1,0},{2,3},{3,2},{4,5},{5,4},{6,7},{7,6},{8,9},{9,8},{10,11... | collective-permute-start | bytes 442376 | tf_op jit(solution)/shard_map/ppermute | solution.py:388
  22.9 10.0 %collective-permute-start.1 = (bf16[144,512]{1,0:T(8,128)(2,1)}, bf16[144,512]{1,0:T(8,128)(2,1)}, u32[]{:S(2)}, u32[]{:S(2)}) collective-permute-start(bf16[144,512]{1,0:T(8,128)(2,1)} %get-tuple-element.36), channel_id=1, source_target_pairs={{0,2},{1,3},{2,0},{3,1},{4,6},{5,7},{6,4},{7,5},{8,10},{9,11},{10,... | collective-permute-start | bytes 442376 | tf_op jit(solution)/shard_map/ppermute | solution.py:388
  22.9 14.7 %collective-permute-start.2 = (bf16[144,512]{1,0:T(8,128)(2,1)}, bf16[144,512]{1,0:T(8,128)(2,1)}, u32[]{:S(2)}, u32[]{:S(2)}) collective-permute-start(bf16[144,512]{1,0:T(8,128)(2,1)} %get-tuple-element.37), channel_id=1, source_target_pairs={{0,3},{1,2},{2,1},{3,0},{4,7},{5,6},{6,5},{7,4},{8,11},{9,10},{10,... | collective-permute-start | bytes 442376 | tf_op jit(solution)/shard_map/ppermute | solution.py:388
  24.6 18.0 %collective-permute-start.3 = (bf16[144,512]{1,0:T(8,128)(2,1)}, bf16[144,512]{1,0:T(8,128)(2,1)}, u32[]{:S(2)}, u32[]{:S(2)}) collective-permute-start(bf16[144,512]{1,0:T(8,128)(2,1)} %get-tuple-element.38), channel_id=1, source_target_pairs={{0,4},{1,5},{2,6},{3,7},{4,0},{5,1},{6,2},{7,3},{8,12},{9,13},{10,... | collective-permute-start | bytes 442376 | tf_op jit(solution)/shard_map/ppermute | solution.py:388
  25.7 23.0 %collective-permute-start.4 = (bf16[144,512]{1,0:T(8,128)(2,1)}, bf16[144,512]{1,0:T(8,128)(2,1)S(1)}, u32[]{:S(2)}, u32[]{:S(2)}) collective-permute-start(bf16[144,512]{1,0:T(8,128)(2,1)} %get-tuple-element.39), channel_id=1, source_target_pairs={{0,5},{1,4},{2,7},{3,6},{4,1},{5,0},{6,3},{7,2},{8,13},{9,12},{10,... | collective-permute-start | bytes 442376 | tf_op jit(solution)/shard_map/ppermute | solution.py:388
  31.1 20.2 %collective-permute-start.5 = (bf16[144,512]{1,0:T(8,128)(2,1)S(1)}, bf16[144,512]{1,0:T(8,128)(2,1)S(1)}, u32[]{:S(2)}, u32[]{:S(2)}) collective-permute-start(bf16[144,512]{1,0:T(8,128)(2,1)S(1)} %copy-done.12), channel_id=1, source_target_pairs={{0,6},{1,7},{2,4},{3,5},{4,2},{5,3},{6,0},{7,1},{8,14},{9,15},{10,... | collective-permute-start | bytes 442376 | tf_op jit(solution)/shard_map/ppermute | solution.py:388
  32.9 55.9 %collective-permute-start.6 = (bf16[144,512]{1,0:T(8,128)(2,1)}, bf16[144,512]{1,0:T(8,128)(2,1)}, u32[]{:S(2)}, u32[]{:S(2)}) collective-permute-start(bf16[144,512]{1,0:T(8,128)(2,1)} %get-tuple-element.41), channel_id=1, source_target_pairs={{0,7},{1,6},{2,5},{3,4},{4,3},{5,2},{6,1},{7,0},{8,15},{9,14},{10,... | collective-permute-start | bytes 442376 | tf_op jit(solution)/shard_map/ppermute | solution.py:388
  85.0 12.4 %all-to-all-start.1 = ((f32[32,2,128]{2,1,0:T(2,128)}), f32[32,2,128]{2,1,0:T(2,128)S(1)}, u32[]{:S(2)}, u32[]{:S(2)}) async-start(f32[32,2,128]{2,1,0:T(2,128)} %routed_statistics.1), calls=%async_computation.1 | async-start | bytes 65536 | tf_op jit(solution)/shard_map/parts/all_to_all | solution.py:408
  100.9 15.1 %all-to-all-start.2 = ((f32[32,2,128]{2,1,0:T(2,128)}), f32[32,2,128]{2,1,0:T(2,128)S(1)}, u32[]{:S(2)}, u32[]{:S(2)}) async-start(f32[32,2,128]{2,1,0:T(2,128)} %get-tuple-element.42), calls=%async_computation.2 | async-start | bytes 65536 | tf_op jit(solution)/shard_map/totals/all_to_all | solution.py:408
  128.5 56.6 %all-to-all-start.3 = ((bf16[256,8,256]{2,1,0:T(8,128)(2,1)}), bf16[256,8,256]{2,1,0:T(8,128)(2,1)S(1)}, u32[]{:S(2)}, u32[]{:S(2)}) async-start(bf16[256,8,256]{2,1,0:T(8,128)(2,1)} %bitcast.38), calls=%async_computation.3 | async-start | bytes 2097152 | tf_op jit(solution)/shard_map/back/all_to_all | solution.py:408
  153.1 7.1 %collective-permute-start.7 = (bf16[128,768]{1,0:T(8,128)(2,1)}, bf16[128,768]{1,0:T(8,128)(2,1)S(1)}, u32[]{:S(2)}, u32[]{:S(2)}) collective-permute-start(bf16[128,768]{1,0:T(8,128)(2,1)} %get-tuple-element.52), channel_id=1, source_target_pairs={{0,1},{1,0},{2,3},{3,2},{4,5},{5,4},{6,7},{7,6},{8,9},{9,8},{10,11... | collective-permute-start | bytes 589832 | tf_op jit(solution)/shard_map/ppermute | solution.py:388
  155.2 9.4 %collective-permute-start.8 = (bf16[128,768]{1,0:T(8,128)(2,1)}, bf16[128,768]{1,0:T(8,128)(2,1)S(1)}, u32[]{:S(2)}, u32[]{:S(2)}) collective-permute-start(bf16[128,768]{1,0:T(8,128)(2,1)} %get-tuple-element.53), channel_id=1, source_target_pairs={{0,2},{1,3},{2,0},{3,1},{4,6},{5,7},{6,4},{7,5},{8,10},{9,11},{10,... | collective-permute-start | bytes 589832 | tf_op jit(solution)/shard_map/ppermute | solution.py:388
  155.2 14.6 %collective-permute-start.9 = (bf16[128,768]{1,0:T(8,128)(2,1)}, bf16[128,768]{1,0:T(8,128)(2,1)S(1)}, u32[]{:S(2)}, u32[]{:S(2)}) collective-permute-start(bf16[128,768]{1,0:T(8,128)(2,1)} %get-tuple-element.54), channel_id=1, source_target_pairs={{0,3},{1,2},{2,1},{3,0},{4,7},{5,6},{6,5},{7,4},{8,11},{9,10},{10,... | collective-permute-start | bytes 589832 | tf_op jit(solution)/shard_map/ppermute | solution.py:388
  156.9 17.6 %collective-permute-start.10 = (bf16[128,768]{1,0:T(8,128)(2,1)}, bf16[128,768]{1,0:T(8,128)(2,1)S(1)}, u32[]{:S(2)}, u32[]{:S(2)}) collective-permute-start(bf16[128,768]{1,0:T(8,128)(2,1)} %get-tuple-element.55), channel_id=1, source_target_pairs={{0,4},{1,5},{2,6},{3,7},{4,0},{5,1},{6,2},{7,3},{8,12},{9,13},{10,... | collective-permute-start | bytes 589832 | tf_op jit(solution)/shard_map/ppermute | solution.py:388
  158.1 20.8 %collective-permute-start.11 = (bf16[128,768]{1,0:T(8,128)(2,1)}, bf16[128,768]{1,0:T(8,128)(2,1)S(1)}, u32[]{:S(2)}, u32[]{:S(2)}) collective-permute-start(bf16[128,768]{1,0:T(8,128)(2,1)} %get-tuple-element.56), channel_id=1, source_target_pairs={{0,5},{1,4},{2,7},{3,6},{4,1},{5,0},{6,3},{7,2},{8,13},{9,12},{10,... | collective-permute-start | bytes 589832 | tf_op jit(solution)/shard_map/ppermute | solution.py:388
  160.2 21.6 %copy-start.3 = (bf16[128,768]{1,0:T(8,128)(2,1)}, bf16[128,768]{1,0:T(8,128)(2,1)S(1)}, u32[]{:S(2)}) copy-start(bf16[128,768]{1,0:T(8,128)(2,1)S(1)} %collective-permute-done.7.refs_1_) | copy-start | bytes 589828
  160.2 18.6 %collective-permute-start.12 = (bf16[128,768]{1,0:T(8,128)(2,1)}, bf16[128,768]{1,0:T(8,128)(2,1)S(1)}, u32[]{:S(2)}, u32[]{:S(2)}) collective-permute-start(bf16[128,768]{1,0:T(8,128)(2,1)} %get-tuple-element.57), channel_id=1, source_target_pairs={{0,6},{1,7},{2,4},{3,5},{4,2},{5,3},{6,0},{7,1},{8,14},{9,15},{10,... | collective-permute-start | bytes 589832 | tf_op jit(solution)/shard_map/ppermute | solution.py:388
  164.6 17.2 %copy-start.4 = (bf16[128,768]{1,0:T(8,128)(2,1)}, bf16[128,768]{1,0:T(8,128)(2,1)S(1)}, u32[]{:S(2)}) copy-start(bf16[128,768]{1,0:T(8,128)(2,1)S(1)} %collective-permute-done.8.refs_2_) | copy-start | bytes 589828
  164.6 17.2 %collective-permute-start.13 = (bf16[128,768]{1,0:T(8,128)(2,1)}, bf16[128,768]{1,0:T(8,128)(2,1)S(1)}, u32[]{:S(2)}, u32[]{:S(2)}) collective-permute-start(bf16[128,768]{1,0:T(8,128)(2,1)} %get-tuple-element.58), channel_id=1, source_target_pairs={{0,7},{1,6},{2,5},{3,4},{4,3},{5,2},{6,1},{7,0},{8,15},{9,14},{10,... | collective-permute-start | bytes 589832 | tf_op jit(solution)/shard_map/ppermute | solution.py:388
  169.9 12.0 %copy-start.5 = (bf16[128,768]{1,0:T(8,128)(2,1)}, bf16[128,768]{1,0:T(8,128)(2,1)S(1)}, u32[]{:S(2)}) copy-start(bf16[128,768]{1,0:T(8,128)(2,1)S(1)} %collective-permute-done.9.refs_3_) | copy-start | bytes 589828
  174.5 7.4 %copy-start.6 = (bf16[128,768]{1,0:T(8,128)(2,1)}, bf16[128,768]{1,0:T(8,128)(2,1)S(1)}, u32[]{:S(2)}) copy-start(bf16[128,768]{1,0:T(8,128)(2,1)S(1)} %collective-permute-done.10.refs_4_) | copy-start | bytes 589828
  178.8 3.0 %copy-start.7 = (bf16[128,768]{1,0:T(8,128)(2,1)}, bf16[128,768]{1,0:T(8,128)(2,1)S(1)}, u32[]{:S(2)}) copy-start(bf16[128,768]{1,0:T(8,128)(2,1)S(1)} %collective-permute-done.11.refs_5_) | copy-start | bytes 589828
  178.8 3.1 %copy-start.8 = (bf16[128,768]{1,0:T(8,128)(2,1)}, bf16[128,768]{1,0:T(8,128)(2,1)S(1)}, u32[]{:S(2)}) copy-start(bf16[128,768]{1,0:T(8,128)(2,1)S(1)} %collective-permute-done.12.refs_6_) | copy-start | bytes 589828
  (7 other events, 7.6 us)

commit v2 on v1

--- a/solution.py
+++ b/solution.py
@@ -7,15 +7,17 @@
 from jax.experimental.pallas import tpu as pltpu
 from jax.sharding import PartitionSpec as P
 
+
 HEAD_DIM = 128
 CAPACITY = 8
 NEGATIVE = -1e30
 LOG2E = 1.4426950408889634
-LN2 = 0.6931471805599453
 SCALING = HEAD_DIM ** (-0.5)
 INFO = 16
 TILE = 256
 CHUNK = 64
+STRIP = 256
+VMEM_BYTES = 24 * 2**20
 F32 = jnp.float32
 BF16 = jnp.bfloat16
 
@@ -28,10 +30,6 @@
     return lax.dot_general(
         a, b, (((ca,), (cb,)), ((), ())), precision=precision, preferred_element_type=F32
     )
-
-
-def params(**kw):
-    return pltpu.CompilerParams(**kw)
 
 
 def pack_kernel(blocks, helpers, pos, choice, query, grad, sent, picker_out, *own):
@@ -70,9 +68,10 @@
     info = jnp.broadcast_to(info, (INFO, info.shape[1])).astype(BF16)
     for k in range(helpers):
         cols = pl.ds(pl.multiple_of((helper ^ k) * width, width), width)
-        own[k][0:rows, 0:width] = query[:, cols]
-        own[k][0:rows, width : 2 * width] = grad[:, cols]
-        own[k][rows : rows + INFO, :] = info
+        piece = piece_ref(own, k)
+        piece[0:rows, 0:width] = query[:, cols]
+        piece[0:rows, width : 2 * width] = grad[:, cols]
+        piece[rows : rows + INFO, :] = info
 
 
 def head_cols(head, heads, which):
@@ -248,11 +247,13 @@
 
 
 def own_gradients_kernel(
-    heads, pos, own, key, value, totals, query_out, key_out, value_out, mixed, probs
+    heads, pos, own, key, value, totals, key_out, value_out, *rest
 ):
+    *pieces, terms, mixed, probs = rest
     helper = pos[1]
     rows = own.shape[1] - INFO
     length = key.shape[0]
+    helpers = length // rows
     for head in range(heads):
         hc = cols_of(head)
         turned = key[:, hc].T
@@ -274,10 +275,10 @@
                 value_out[0:end, hc] += value_new
                 key_out[0:end, hc] += key_new
             query_new = (dot(turned[:, 0:end], mixed[0:end, :], 1, 0) * SCALING).T
-            for n in range(TILE // rows):
-                query_out[helper ^ (start // rows + n), :, hc] = query_new[
-                    n * rows : (n + 1) * rows
-                ].astype(BF16)
+            terms[start:end, hc] = query_new
+    for k in range(helpers):
+        at = pl.ds(pl.multiple_of((helper ^ k) * rows, rows), rows)
+        piece_ref(pieces, k)[...] = terms[at, :].astype(BF16)
 
 
 def slot_row(slots, tile, head, which, group):
@@ -292,19 +293,27 @@
     helpers, blocks, capacity, _ = routed.shape
     group = helpers * capacity
     count = TILE // group
-    turned = [key[:, cols_of(head)].T for head in range(heads)]
+    length = key.shape[0]
 
     def body(tile, _):
+        rows = [
+            slot_row(slots, tile, head, which, group) for head in range(heads) for which in range(2)
+        ]
+        pad = jnp.zeros((8 - len(rows), TILE), F32)
+        columns = jnp.concatenate(rows + [pad], axis=0).T
         for head in range(heads):
             hc = cols_of(head)
             q = routed_tile(routed, tile, head_cols(head, heads, 0))
             g = routed_tile(routed, tile, head_cols(head, heads, 1))
-            log_total = slot_row(slots, tile, head, 0, group)
-            center = slot_row(slots, tile, head, 1, group)
-            mixed_into(
-                mixed.at[head], None, key[:, hc], value[:, hc], q, g, log_total, center, None
-            )
-            query_new = (dot(turned[head], mixed[head], 1, 0) * SCALING).T
+            log_total = columns[:, 2 * head : 2 * head + 1]
+            center = columns[:, 2 * head + 1 : 2 * head + 2]
+            for at in range(0, length, STRIP):
+                keys = slice(at, at + STRIP)
+                scores = dot(q, key[keys, hc], 1, 1) * (SCALING * LOG2E)
+                products = dot(g, value[keys, hc], 1, 1)
+                weights = jnp.exp2(scores - log_total)
+                mixed[head, :, keys] = (weights * (products - center)).astype(BF16)
+            query_new = dot(mixed[head], key[:, hc], 1, 0) * SCALING
             for a in range(count):
                 out[:, tile * count + a, :, hc] = (
                     query_new[a * group : (a + 1) * group]
@@ -317,10 +326,9 @@
 
 
 def routed_block_kernel(
-    heads, helpers, pos, routed, key, value, slots, key_own, value_own, query_own, *rest
+    heads, helpers, pos, routed, key, value, slots, key_own, value_own, *rest
 ):
-    pieces = rest[:helpers]
-    key_acc, value_acc, mixed, probs = rest[helpers:]
+    *pieces, key_acc, value_acc, mixed, probs = rest
     _, blocks, capacity, _ = routed.shape
     group = helpers * capacity
     key_acc[...] = key_own[...]
@@ -353,9 +361,9 @@
     share = key_acc.shape[0] // helpers
     for k in range(helpers):
         at = pl.ds(pl.multiple_of((pos[1] ^ k) * share, share), share)
-        pieces[k][:, 0:width] = query_own[k]
-        pieces[k][:, width : 2 * width] = (key_acc[at, :] * SCALING).astype(BF16)
-        pieces[k][:, 2 * width : 3 * width] = value_acc[at, :].astype(BF16)
+        piece = piece_ref(pieces, k)
+        piece[:, 0:width] = (key_acc[at, :] * SCALING).astype(BF16)
+        piece[:, width : 2 * width] = value_acc[at, :].astype(BF16)
 
 
 def place_kernel(helpers, pos, *refs):
@@ -364,8 +372,8 @@
     width = key_out.shape[1] // helpers
     for k in range(helpers):
         cols = pl.ds(pl.multiple_of((pos[1] ^ k) * width, width), width)
-        key_out[:, cols] = pieces[k][:, width : 2 * width]
-        value_out[:, cols] = pieces[k][:, 2 * width : 3 * width]
+        key_out[:, cols] = pieces[k][:, 0:width]
+        value_out[:, cols] = pieces[k][:, width : 2 * width]
 
 
 def finish_kernel(helpers, pos, picker, returned, *refs):
@@ -377,31 +385,67 @@
         d = pos[1] ^ k
         cols = pl.ds(pl.multiple_of(d * width, width), width)
         terms = returned[d].astype(F32).reshape(slots, width).astype(BF16)
-        out[:, cols] = (dot(picker[...], terms, 1, 0) + pieces[k][:, 0:width].astype(F32)).astype(
+        out[:, cols] = (dot(picker[...], terms, 1, 0) + pieces[k][...].astype(F32)).astype(
             BF16
         )
 
 
+DIRECT = (1, 3, 6)
+RELAYED = ((2, 4, 6), (7, 5, 2))
+
+
+def piece_shapes(shape, dtype, kind=pltpu.VMEM):
+    one = kind(shape, dtype)
+    pair = kind((2,) + shape, dtype)
+    return [one] * (1 + len(DIRECT)) + [pair] * len(RELAYED)
+
+
+def piece_ref(refs, k):
+    if k == 0:
+        return refs[0]
+    if k in DIRECT:
+        return refs[1 + DIRECT.index(k)]
+    for n, (near, far, _) in enumerate(RELAYED):
+        if k in (near, far):
+            return refs[1 + len(DIRECT) + n].at[(near, far).index(k)]
+    raise ValueError(k)
+
+
 def exchange(pieces, helpers):
-    received = [pieces[0]]
-    for k in range(1, helpers):
-        received.append(lax.ppermute(pieces[k], "help", [(i, i ^ k) for i in range(helpers)]))
-    return received
-
-
-def call(kernel, out_shape, name, scratch=()):
-    return pl.pallas_call(kernel, out_shape=out_shape, scratch_shapes=scratch, name=name)
-
-
-def with_position(kernel, out_shape, name, operands, scratch=()):
+    def send(array, k):
+        return lax.ppermute(array, "help", [(i, i ^ k) for i in range(helpers)])
+
+    received = {0: pieces[0]}
+    pairs = []
+    for n, (near, _, _) in enumerate(RELAYED):
+        pairs.append(send(pieces[1 + len(DIRECT) + n], near))
+    for n, k in enumerate(DIRECT):
+        received[k] = send(pieces[1 + n], k)
+    for pair, (near, far, last) in zip(pairs, RELAYED):
+        received[near] = pair[0]
+        received[far] = send(pair[1], last)
+    return [received[k] for k in range(helpers)]
+
+
+def resident(x):
+    return pltpu.with_memory_space_constraint(x, pltpu.VMEM)
+
+
+def call(kernel, outputs, operands, position=None, scratch=(), flops=0, fast=99):
     vmem = pl.BlockSpec(memory_space=pltpu.VMEM)
+    operands = [resident(x) if n < fast else x for n, x in enumerate(operands)]
+    specs = [vmem] * len(operands)
+    if position is not None:
+        operands = [position] + list(operands)
+        specs = [pl.BlockSpec(memory_space=pltpu.SMEM)] + specs
     return pl.pallas_call(
         kernel,
-        out_shape=out_shape,
-        in_specs=[pl.BlockSpec(memory_space=pltpu.SMEM)] + [vmem] * operands,
+        out_shape=outputs,
+        in_specs=specs,
         scratch_shapes=scratch,
-        name=name,
-    )
+        compiler_params=pltpu.CompilerParams(vmem_limit_bytes=VMEM_BYTES),
+        cost_estimate=pl.CostEstimate(flops=flops, bytes_accessed=0, transcendentals=0),
+    )(*operands)
 
 
 def swap(array, axes):
@@ -419,105 +463,104 @@
     heads = width // HEAD_DIM
     group = helpers * CAPACITY
     slots = blocks * CAPACITY
+    share = length // helpers
+    pairs = 2 * blocks * group * length * width
     shape = jax.ShapeDtypeStruct
+    fast = pltpu.VMEM
     everyone = ("help", "ctx")
 
-    piece = shape((rows + INFO, 2 * width), BF16)
-    packed = with_position(
+    sent, picker, *pieces = call(
         functools.partial(pack_kernel, blocks, helpers),
-        [
-            shape((helpers, blocks, CAPACITY, 2 * width), BF16),
-            shape((rows, slots), BF16),
-        ]
-        + [piece] * helpers,
-        "pack",
-        3,
-    )(position, jnp.transpose(block_choice[0]), query_rows[0], output_grad[0])
-    sent, picker, pieces = packed[0], packed[1], packed[2:]
-
+        [fast((helpers, blocks, CAPACITY, 2 * width), BF16), shape((rows, slots), BF16)]
+        + piece_shapes((rows + INFO, 2 * width), BF16),
+        [jnp.transpose(block_choice[0]), query_rows[0], output_grad[0]],
+        position,
+        flops=2 * rows * slots * features * 2,
+        fast=0,
+    )
     own = jnp.stack(exchange(pieces, helpers))
-    with jax.named_scope("dispatch"):
-        routed = swap(sent.reshape(blocks * helpers, CAPACITY, 2 * width), everyone)
+    routed = swap(sent.reshape(blocks * helpers, CAPACITY, 2 * width), everyone)
     routed = routed.reshape(helpers, blocks, CAPACITY, 2 * width)
 
     key = lax.dynamic_slice_in_dim(key_rows[0], helper * width, width, 1)
     value = lax.dynamic_slice_in_dim(value_rows[0], helper * width, width, 1)
-    stats = with_position(
+    stats = call(
         functools.partial(own_statistics_kernel, heads, helpers),
-        shape((2 * heads + 4, length), F32),
-        "own_statistics",
-        3,
-    )(position, own, key, value)
-
-    slot_shape = shape((blocks, heads, 2 * group), F32)
+        fast((2 * heads + 4, length), F32),
+        [own, key, value],
+        position,
+        flops=pairs // 2,
+    )
+    slot_shape = fast((blocks, heads, 2 * group), F32)
     parts = call(
-        functools.partial(routed_statistics_kernel, heads), slot_shape, "routed_statistics"
-    )(routed, key, value)
-    with jax.named_scope("parts"):
-        parts = swap(parts, "ctx")
+        functools.partial(routed_statistics_kernel, heads),
+        slot_shape,
+        [routed, key, value],
+        flops=2 * pairs,
+    )
+    parts = swap(parts, "ctx")
 
     totals, spread = call(
         functools.partial(combine_kernel, heads, helpers),
-        [shape((2 * heads, length), F32), slot_shape],
-        "combine",
-    )(stats, parts)
-    with jax.named_scope("totals"):
-        spread = swap(spread, "ctx")
+        [fast((2 * heads, length), F32), slot_shape],
+        [stats, parts],
+        flops=pairs // 8,
+    )
+    spread = swap(spread, "ctx")
 
     tile = (heads, length, TILE)
-    query_own, key_own, value_own = with_position(
+    own_out = call(
         functools.partial(own_gradients_kernel, heads),
-        [
-            shape((helpers, rows, width), BF16),
-            shape((length, width), F32),
-            shape((length, width), F32),
-        ],
-        "own_gradients",
-        4,
-        [pltpu.VMEM(tile[1:], BF16), pltpu.VMEM(tile[1:], BF16)],
-    )(position, own, key, value, totals)
-    spread, query_own, key_own, value_own = lax.optimization_barrier(
-        (spread, query_own, key_own, value_own)
-    )
+        [shape((length, width), F32)] * 2 + piece_shapes((rows, width), BF16, shape),
+        [own, key, value, totals],
+        position,
+        [pltpu.VMEM((length, width), F32)] + [pltpu.VMEM(tile[1:], BF16)] * 2,
+        flops=2 * pairs,
+    )
+    key_own, value_own, *query_own = own_out
+    spread, key_own, value_own = lax.optimization_barrier((spread, key_own, value_own))
+    query_own = exchange(query_own, helpers)
 
     terms = call(
         functools.partial(routed_query_kernel, heads),
-        shape((helpers, blocks, CAPACITY, width), BF16),
-        "routed_query",
-        [pltpu.VMEM(tile, BF16)],
-    )(routed, key, value, spread)
-    with jax.named_scope("back"):
-        returned = swap(terms.reshape(blocks * helpers, CAPACITY, width), everyone)
+        fast((helpers, blocks, CAPACITY, width), BF16),
+        [routed, key, value, spread],
+        scratch=[pltpu.VMEM((heads, TILE, length), BF16)],
+        flops=3 * pairs,
+    )
+    returned = swap(terms.reshape(blocks * helpers, CAPACITY, width), everyone)
     returned = returned.reshape(helpers, blocks, CAPACITY, width)
 
-    share = length // helpers
-    pieces = with_position(
+    pieces = call(
         functools.partial(routed_block_kernel, heads, helpers),
-        [shape((share, 3 * width), BF16)] * helpers,
-        "routed_block",
-        7,
+        piece_shapes((share, 2 * width), BF16),
+        [routed, key, value, spread, key_own, value_own],
+        position,
         [pltpu.VMEM((length, width), F32)] * 2 + [pltpu.VMEM(tile, BF16)] * 2,
-    )(position, routed, key, value, spread, key_own, value_own, query_own)
+        flops=4 * pairs,
+        fast=4,
+    )
     pieces = exchange(pieces, helpers)
 
-    key_grad, value_grad = with_position(
+    key_grad, value_grad = call(
         functools.partial(place_kernel, helpers),
         [shape((share, features), BF16)] * 2,
-        "place",
-        helpers,
-    )(position, *pieces)
-    query_grad = with_position(
+        pieces,
+        position,
+    )
+    query_grad = call(
         functools.partial(finish_kernel, helpers),
         shape((rows, features), BF16),
-        "finish",
-        helpers + 2,
-    )(position, picker, returned, *pieces)
+        [picker, returned, *query_own],
+        position,
+    )
     return query_grad[None], key_grad[None], value_grad[None]
 
 
 def solution(mesh):
     split = P(None, ("ctx", "help"), None)
     shared = P(None, "ctx", None)
+
     return jax.shard_map(
         per_device,
         mesh=mesh,

time: 190 us -> 183 us (0.963)
  Pallas kernels: 57.7 us -> 47.3 us
  waiting for transfers between devices: 59.6 us -> 53.2 us
  starting transfers between devices: 57.1 us -> 62.5 us
  local copies, waits for them, and re-layouts: 13.1 us -> 16.7 us
    pallas_call x9, Pallas kernels: 57.7 us -> 47.3 us  [call(): pl.pallas_call(kernel, out_shape=outputs, in_specs=specs, scratch_shapes=...]
    all_to_all x4, waiting for transfers between devices: 27.6 us -> 22.1 us  [swap(): return lax.all_to_all(array, axes, split_axis=0, concat_axis=0, tiled=True)]
    ppermute x14 -> x21, starting transfers between devices: 20.5 us -> 25.1 us  [send(): return lax.ppermute(array, 'help', [(i, i ^ k) for i in range(helpers)])]
    unnamed x33 -> x36, local copies, waits for them, and re-layouts: 9.89 us -> 12.5 us
    squeeze x0 -> x6, local copies, waits for them, and re-layouts: none -> 1.98 us  [the longest x4 1.95 us: exchange(): received[far] = send(pair[1], last)]
    ppermute x14 -> x21, waiting for transfers between devices: 31.9 us -> 31.1 us  [send(): return lax.ppermute(array, 'help', [(i, i ^ k) for i in range(helpers)])]
  transfers between devices with their start and end apart: 18 -> 25, of which waited for: 12 -> 7; matrix products, arithmetic and copies ran while one was open for 4% -> 4% of each run, Pallas kernels for 19% -> 11%
where the time goes in v2:
time: 183 us; the launch traced here: 181 us
  starting transfers between devices  62.5 us (34%)
  waiting for transfers between devices  53.2 us (29%)
  Pallas kernels  47.3 us (26%)
  local copies, waits for them, and re-layouts  16.7 us (9%)
    pallas_call x9, Pallas kernels, call(): pl.pallas_call(kernel, out_shape=outputs, in_specs=specs, scratch_shapes=...  47.3 us
    all_to_all x4, starting transfers between devices, swap(): return lax.all_to_all(array, axes, split_axis=0, concat_axis=0, tiled=True)  37.4 us
    ppermute x21, waiting for transfers between devices, send(): return lax.ppermute(array, 'help', [(i, i ^ k) for i in range(helpers)])  31.1 us
    ppermute x21, starting transfers between devices, send(): return lax.ppermute(array, 'help', [(i, i ^ k) for i in range(helpers)])  25.1 us
    all_to_all x4, waiting for transfers between devices, swap(): return lax.all_to_all(array, axes, split_axis=0, concat_axis=0, tiled=True)  22.1 us
    unnamed x36, local copies, waits for them, and re-layouts  12.5 us
  transfers between devices with their start and end apart: 25, of which 7 were waited for; matrix products, arithmetic and copies ran while one was open for 4% of the time, Pallas kernels for 11%

profile of v2, /device:TPU:1, one launch (start us, length us, event | category | flops | bytes accessed | tf_op | source)
XLA Modules:
  0.0 180.7 jit_solution(11216291592558335399)
XLA Ops:
  3.5 2.9 %shard_map.76 = (bf16[8,32,8,512]{3,2,1,0:T(8,128)(2,1)}, bf16[128,256]{1,0:T(8,128)(2,1)S(1)}, bf16[144,512]{1,0:T(8,128)(2,1)S(1)}, bf16[144,512]{1,0:T(8,128)...) custom-call(s32[2]{0:T(128)S(1)} %pad_add_fusion.pos, ...), custom_call_target="tpu_custom_call" | custom-call | flops 268435456 | tf_op jit(solution)/shard_map/pallas_call | solution.py:441
  6.3 16.6 %all-to-all-start = ((bf16[256,8,512]{2,1,0:T(8,128)(2,1)}), bf16[256,8,512]{2,1,0:T(8,128)(2,1)}, u32[]{:S(2)}, u32[]{:S(2)}) async-start(bf16[256,8,512]{2,1,0:T(8,128)(2,1)} %bitcast.6), calls=%async_computation | async-start | bytes 4194304 | tf_op jit(solution)/shard_map/all_to_all | solution.py:452
  23.0 2.3 %collective-permute-start = (bf16[144,512]{1,0:T(8,128)(2,1)}, bf16[144,512]{1,0:T(8,128)(2,1)}, u32[]{:S(2)}, u32[]{:S(2)}) collective-permute-start(bf16[144,512]{1,0:T(8,128)(2,1)} %get-tuple-element.35), channel_id=1, source_target_pairs={{0,1},{1,0},{2,3},{3,2},{4,5},{5,4},{6,7},{7,6},{8,9},{9,8},{10,11... | collective-permute-start | bytes 442376 | tf_op jit(solution)/shard_map/ppermute | solution.py:416
  26.9 2.8 %collective-permute-start.4 = (bf16[2,144,512]{2,1,0:T(8,128)(2,1)S(1)}, bf16[2,144,512]{2,1,0:T(8,128)(2,1)}, u32[]{:S(2)}, u32[]{:S(2)}) collective-permute-start(bf16[2,144,512]{2,1,0:T(8,128)(2,1)S(1)} %get-tuple-element.38), channel_id=1, source_target_pairs={{0,7},{1,6},{2,5},{3,4},{4,3},{5,2},{6,1},{7,0},{8,15},{9,14},{10,... | collective-permute-start | bytes 884744 | tf_op jit(solution)/shard_map/ppermute | solution.py:416
  31.9 14.6 %collective-permute-done.4 = bf16[2,144,512]{2,1,0:T(8,128)(2,1)} collective-permute-done((bf16[2,144,512]{2,1,0:T(8,128)(2,1)S(1)}, bf16[2,144,512]{2,1,0:T(8,128)(2,1)}, u32[]{:S(2)}, u32[]{:S(2)}) %collective-permute-start.4) | collective-permute-done | bytes 294944 | tf_op jit(solution)/shard_map/ppermute | solution.py:416
  50.8 7.3 %collective-permute-done.3 = bf16[144,512]{1,0:T(8,128)(2,1)S(1)} collective-permute-done((bf16[144,512]{1,0:T(8,128)(2,1)S(1)}, bf16[144,512]{1,0:T(8,128)(2,1)S(1)}, u32[]{:S(2)}, u32[]{:S(2)}) %collective-permute-start.3) | collective-permute-done | bytes 147488 | tf_op jit(solution)/shard_map/ppermute | solution.py:416
  59.1 16.7 %all-to-all-done = bf16[256,8,512]{2,1,0:T(8,128)(2,1)} async-done(((bf16[256,8,512]{2,1,0:T(8,128)(2,1)}), bf16[256,8,512]{2,1,0:T(8,128)(2,1)}, u32[]{:S(2)}, u32[]{:S(2)}) %all-to-all-start) | async-done | bytes 2097184 | tf_op jit(solution)/shard_map/all_to_all | solution.py:452
  75.7 9.2 %shard_map.78 = f32[32,2,128]{2,1,0:T(2,128)} custom-call(bf16[8,32,8,512]{3,2,1,0:T(8,128)(2,1)} %bitcast.7.routed, bf16[1024,256]{1,0:T(8,128)(2,1)S(1)} %get-tuple-element.72.key, bf16[1024,256]{1,0:T(8,128)(2,1)S(1)} %get-tuple-element.71.value), custom_call_target="tpu_custom_call" | custom-call | flops 2147483648 | tf_op jit(solution)/shard_map/pallas_call | solution.py:441
  85.0 3.9 %all-to-all-start.1 = ((f32[32,2,128]{2,1,0:T(2,128)}), f32[32,2,128]{2,1,0:T(2,128)S(1)}, u32[]{:S(2)}, u32[]{:S(2)}) async-start(f32[32,2,128]{2,1,0:T(2,128)} %shard_map.78), calls=%async_computation.1 | async-start | bytes 65536 | tf_op jit(solution)/shard_map/all_to_all | solution.py:452
  89.7 2.3 %shard_map.77.stats = f32[8,1024]{1,0:T(8,128)S(1)} custom-call(s32[2]{0:T(128)S(1)} %pad_add_fusion.pos, bf16[8,144,512]{2,1,0:T(8,128)(2,1)S(1)} %slice_dynamic-update-slice_fusion.own, bf16[1024,256]{1,0:T(8,128)(2,1)S(1)} %get-tuple-element.72.key, bf16[1024,256]{1,0:T(8,128)(2,1)S(1)} %get-tuple-element.71.value), custom_call_target="tpu_custom_call" | custom-call | flops 536870912 | tf_op jit(solution)/shard_map/pallas_call | solution.py:441
  92.1 5.4 %all-to-all-done.1.got = f32[32,2,128]{2,1,0:T(2,128)S(1)} async-done(((f32[32,2,128]{2,1,0:T(2,128)}), f32[32,2,128]{2,1,0:T(2,128)S(1)}, u32[]{:S(2)}, u32[]{:S(2)}) %all-to-all-start.1) | async-done | bytes 32800 | tf_op jit(solution)/shard_map/all_to_all | solution.py:452
  97.5 2.1 %shard_map.79 = (f32[4,1024]{1,0:T(4,128)S(1)}, f32[32,2,128]{2,1,0:T(2,128)}) custom-call(f32[8,1024]{1,0:T(8,128)S(1)} %shard_map.77.stats, f32[32,2,128]{2,1,0:T(2,128)S(1)} %all-to-all-done.1.got), custom_call_target="tpu_custom_call" | custom-call | flops 134217728 | tf_op jit(solution)/shard_map/pallas_call | solution.py:441
  99.5 4.0 %all-to-all-start.2 = ((f32[32,2,128]{2,1,0:T(2,128)}), f32[32,2,128]{2,1,0:T(2,128)S(1)}, u32[]{:S(2)}, u32[]{:S(2)}) async-start(f32[32,2,128]{2,1,0:T(2,128)} %get-tuple-element.40), calls=%async_computation.2 | async-start | bytes 65536 | tf_op jit(solution)/shard_map/all_to_all | solution.py:452
  103.6 4.2 %shard_map.80 = (f32[1024,256]{1,0:T(8,128)S(1)}, f32[1024,256]{1,0:T(8,128)S(1)}, bf16[128,256]{1,0:T(8,128)(2,1)S(1)}, bf16[128,256]{1,0:T(8,128)(2,1)S(1)}, b...) custom-call(s32[2]{0:T(128)S(1)} %pad_add_fusion.pos, ...), custom_call_target="tpu_custom_call" | custom-call | flops 2147483648 | tf_op jit(solution)/shard_map/pallas_call | solution.py:441
  112.3 11.3 %shard_map.81 = bf16[8,32,8,256]{3,2,1,0:T(8,128)(2,1)} custom-call(bf16[8,32,8,512]{3,2,1,0:T(8,128)(2,1)} %bitcast.7.routed, bf16[1024,256]{1,0:T(8,128)(2,1)S(1)} %get-tuple-element.72.key, bf16[1024,256]{1,0:T(8,128)(2,1)S(1)} %get-tuple-element.71.value, f32[32,2,128]{2,1,0:T(2,128)S(1)} %all-to-all-done.2.slots), custom_call_target="tpu_custom_call" | custom-call | flops 3221225472 | tf_op jit(solution)/shard_map/pallas_call | solution.py:441
  123.7 12.9 %all-to-all-start.3 = ((bf16[256,8,256]{2,1,0:T(8,128)(2,1)}), bf16[256,8,256]{2,1,0:T(8,128)(2,1)S(1)}, u32[]{:S(2)}, u32[]{:S(2)}) async-start(bf16[256,8,256]{2,1,0:T(8,128)(2,1)} %bitcast.18), calls=%async_computation.3 | async-start | bytes 2097152 | tf_op jit(solution)/shard_map/all_to_all | solution.py:452
  140.4 12.0 %shard_map.83 = (bf16[128,512]{1,0:T(8,128)(2,1)S(1)}, bf16[128,512]{1,0:T(8,128)(2,1)S(1)}, bf16[128,512]{1,0:T(8,128)(2,1)S(1)}, bf16[128,512]{1,0:T(8,128)(2,...) custom-call(s32[2]{0:T(128)S(1)} %pad_add_fusion.pos, bf16[8,32,8,512]{3,2,1,0:T(8,128)(2,1)} %bitcast.7.routed, ...), custom_call_target="tpu_custom_call" | custom-call | flops 4294967296 | tf_op jit(solution)/shard_map/pallas_call | solution.py:441
  152.7 3.4 %collective-permute-start.11 = (bf16[2,128,256]{2,1,0:T(8,128)(2,1)S(1)}, bf16[2,128,256]{2,1,0:T(8,128)(2,1)S(1)}, u32[]{:S(2)}, u32[]{:S(2)}) collective-permute-start(bf16[2,128,256]{2,1,0:T(8,128)(2,1)S(1)} %copy-done.4), channel_id=1, source_target_pairs={{0,7},{1,6},{2,5},{3,4},{4,3},{5,2},{6,1},{7,0},{8,15},{9,14},{10,... | collective-permute-start | bytes 393224 | tf_op jit(solution)/shard_map/ppermute | solution.py:416
  156.4 1.9 %collective-permute-start.18 = (bf16[2,128,512]{2,1,0:T(8,128)(2,1)S(1)}, bf16[2,128,512]{2,1,0:T(8,128)(2,1)S(1)}, u32[]{:S(2)}, u32[]{:S(2)}) collective-permute-start(bf16[2,128,512]{2,1,0:T(8,128)(2,1)S(1)} %get-tuple-element.57), channel_id=1, source_target_pairs={{0,7},{1,6},{2,5},{3,4},{4,3},{5,2},{6,1},{7,0},{8,15},{9,14},{10,... | collective-permute-start | bytes 786440 | tf_op jit(solution)/shard_map/ppermute | solution.py:416
  158.4 5.0 %collective-permute-done.15 = bf16[2,128,512]{2,1,0:T(8,128)(2,1)S(1)} collective-permute-done((bf16[2,128,512]{2,1,0:T(8,128)(2,1)S(1)}, bf16[2,128,512]{2,1,0:T(8,128)(2,1)S(1)}, u32[]{:S(2)}, u32[]{:S(2)}) %collective-permute-start.15) | collective-permute-done | bytes 262176 | tf_op jit(solution)/shard_map/ppermute | solution.py:416
  163.3 1.9 %collective-permute-start.20 = (bf16[128,512]{1,0:T(8,128)(2,1)S(1)}, bf16[128,512]{1,0:T(8,128)(2,1)S(1)}, u32[]{:S(2)}, u32[]{:S(2)}) collective-permute-start(bf16[128,512]{1,0:T(8,128)(2,1)S(1)} %get-tuple-element.58), channel_id=1, source_target_pairs={{0,6},{1,7},{2,4},{3,5},{4,2},{5,3},{6,0},{7,1},{8,14},{9,15},{10,... | collective-permute-start | bytes 393224 | tf_op jit(solution)/shard_map/ppermute | solution.py:416
  165.2 2.8 %collective-permute-done.18 = bf16[2,128,512]{2,1,0:T(8,128)(2,1)S(1)} collective-permute-done((bf16[2,128,512]{2,1,0:T(8,128)(2,1)S(1)}, bf16[2,128,512]{2,1,0:T(8,128)(2,1)S(1)}, u32[]{:S(2)}, u32[]{:S(2)}) %collective-permute-start.18) | collective-permute-done | bytes 262176 | tf_op jit(solution)/shard_map/ppermute | solution.py:416
  168.0 2.1 %collective-permute-start.17 = (bf16[128,512]{1,0:T(8,128)(2,1)S(1)}, bf16[128,512]{1,0:T(8,128)(2,1)S(1)}, u32[]{:S(2)}, u32[]{:S(2)}) collective-permute-start(bf16[128,512]{1,0:T(8,128)(2,1)S(1)} %get-tuple-element.65), channel_id=1, source_target_pairs={{0,6},{1,7},{2,4},{3,5},{4,2},{5,3},{6,0},{7,1},{8,14},{9,15},{10,... | collective-permute-start | bytes 393224 | tf_op jit(solution)/shard_map/ppermute | solution.py:416
  171.4 1.7 collective-permute-start.9
  (80 shorter events, 30.7 us)
Async XLA Ops:
  6.3 69.4 %all-to-all-start = ((bf16[256,8,512]{2,1,0:T(8,128)(2,1)}), bf16[256,8,512]{2,1,0:T(8,128)(2,1)}, u32[]{:S(2)}, u32[]{:S(2)}) async-start(bf16[256,8,512]{2,1,0:T(8,128)(2,1)} %bitcast.6), calls=%async_computation | async-start | bytes 4194304 | tf_op jit(solution)/shard_map/all_to_all | solution.py:452
  23.0 8.0 %collective-permute-start = (bf16[144,512]{1,0:T(8,128)(2,1)}, bf16[144,512]{1,0:T(8,128)(2,1)}, u32[]{:S(2)}, u32[]{:S(2)}) collective-permute-start(bf16[144,512]{1,0:T(8,128)(2,1)} %get-tuple-element.35), channel_id=1, source_target_pairs={{0,1},{1,0},{2,3},{3,2},{4,5},{5,4},{6,7},{7,6},{8,9},{9,8},{10,11... | collective-permute-start | bytes 442376 | tf_op jit(solution)/shard_map/ppermute | solution.py:416
  25.3 24.6 %collective-permute-start.2 = (bf16[144,512]{1,0:T(8,128)(2,1)S(1)}, bf16[144,512]{1,0:T(8,128)(2,1)}, u32[]{:S(2)}, u32[]{:S(2)}) collective-permute-start(bf16[144,512]{1,0:T(8,128)(2,1)S(1)} %get-tuple-element.37), channel_id=1, source_target_pairs={{0,3},{1,2},{2,1},{3,0},{4,7},{5,6},{6,5},{7,4},{8,11},{9,10},{10,... | collective-permute-start | bytes 442376 | tf_op jit(solution)/shard_map/ppermute | solution.py:416
  25.3 32.8 %collective-permute-start.6 = (bf16[144,512]{1,0:T(8,128)(2,1)S(1)}, bf16[144,512]{1,0:T(8,128)(2,1)}, u32[]{:S(2)}, u32[]{:S(2)}) collective-permute-start(bf16[144,512]{1,0:T(8,128)(2,1)S(1)} %get-tuple-element.39), channel_id=1, source_target_pairs={{0,6},{1,7},{2,4},{3,5},{4,2},{5,3},{6,0},{7,1},{8,14},{9,15},{10,... | collective-permute-start | bytes 442376 | tf_op jit(solution)/shard_map/ppermute | solution.py:416
  26.6 21.1 %collective-permute-start.1 = (bf16[2,144,512]{2,1,0:T(8,128)(2,1)S(1)}, bf16[2,144,512]{2,1,0:T(8,128)(2,1)}, u32[]{:S(2)}, u32[]{:S(2)}) collective-permute-start(bf16[2,144,512]{2,1,0:T(8,128)(2,1)S(1)} %get-tuple-element.36), channel_id=1, source_target_pairs={{0,2},{1,3},{2,0},{3,1},{4,6},{5,7},{6,4},{7,5},{8,10},{9,11},{10,... | collective-permute-start | bytes 884744 | tf_op jit(solution)/shard_map/ppermute | solution.py:416
  26.9 19.6 %collective-permute-start.4 = (bf16[2,144,512]{2,1,0:T(8,128)(2,1)S(1)}, bf16[2,144,512]{2,1,0:T(8,128)(2,1)}, u32[]{:S(2)}, u32[]{:S(2)}) collective-permute-start(bf16[2,144,512]{2,1,0:T(8,128)(2,1)S(1)} %get-tuple-element.38), channel_id=1, source_target_pairs={{0,7},{1,6},{2,5},{3,4},{4,3},{5,2},{6,1},{7,0},{8,15},{9,14},{10,... | collective-permute-start | bytes 884744 | tf_op jit(solution)/shard_map/ppermute | solution.py:416
  47.4 10.7 %collective-permute-start.5 = (bf16[144,512]{1,0:T(8,128)(2,1)S(1)}, bf16[144,512]{1,0:T(8,128)(2,1)S(1)}, u32[]{:S(2)}, u32[]{:S(2)}) collective-permute-start(bf16[144,512]{1,0:T(8,128)(2,1)S(1)} %slice_bitcast_fusion), channel_id=1, source_target_pairs={{0,2},{1,3},{2,0},{3,1},{4,6},{5,7},{6,4},{7,5},{8,10},{9,11},{10,... | collective-permute-start | bytes 442376 | tf_op jit(solution)/shard_map/ppermute | solution.py:416
  48.7 9.4 %collective-permute-start.3 = (bf16[144,512]{1,0:T(8,128)(2,1)S(1)}, bf16[144,512]{1,0:T(8,128)(2,1)S(1)}, u32[]{:S(2)}, u32[]{:S(2)}) collective-permute-start(bf16[144,512]{1,0:T(8,128)(2,1)S(1)} %get-tuple-element.61), channel_id=1, source_target_pairs={{0,6},{1,7},{2,4},{3,5},{4,2},{5,3},{6,0},{7,1},{8,14},{9,15},{10,... | collective-permute-start | bytes 442376 | tf_op jit(solution)/shard_map/ppermute | solution.py:416
  85.0 12.5 %all-to-all-start.1 = ((f32[32,2,128]{2,1,0:T(2,128)}), f32[32,2,128]{2,1,0:T(2,128)S(1)}, u32[]{:S(2)}, u32[]{:S(2)}) async-start(f32[32,2,128]{2,1,0:T(2,128)} %shard_map.78), calls=%async_computation.1 | async-start | bytes 65536 | tf_op jit(solution)/shard_map/all_to_all | solution.py:452
  99.5 12.8 %all-to-all-start.2 = ((f32[32,2,128]{2,1,0:T(2,128)}), f32[32,2,128]{2,1,0:T(2,128)S(1)}, u32[]{:S(2)}, u32[]{:S(2)}) async-start(f32[32,2,128]{2,1,0:T(2,128)} %get-tuple-element.40), calls=%async_computation.2 | async-start | bytes 65536 | tf_op jit(solution)/shard_map/all_to_all | solution.py:452
  123.7 55.3 %all-to-all-start.3 = ((bf16[256,8,256]{2,1,0:T(8,128)(2,1)}), bf16[256,8,256]{2,1,0:T(8,128)(2,1)S(1)}, u32[]{:S(2)}, u32[]{:S(2)}) async-start(bf16[256,8,256]{2,1,0:T(8,128)(2,1)} %bitcast.18), calls=%async_computation.3 | async-start | bytes 2097152 | tf_op jit(solution)/shard_map/all_to_all | solution.py:452
  136.6 19.9 %collective-permute-start.8 = (bf16[2,128,256]{2,1,0:T(8,128)(2,1)S(1)}, bf16[2,128,256]{2,1,0:T(8,128)(2,1)S(1)}, u32[]{:S(2)}, u32[]{:S(2)}) collective-permute-start(bf16[2,128,256]{2,1,0:T(8,128)(2,1)S(1)} %copy-done.6), channel_id=1, source_target_pairs={{0,2},{1,3},{2,0},{3,1},{4,6},{5,7},{6,4},{7,5},{8,10},{9,11},{10,... | collective-permute-start | bytes 393224 | tf_op jit(solution)/shard_map/ppermute | solution.py:416
  152.5 10.9 %collective-permute-start.15 = (bf16[2,128,512]{2,1,0:T(8,128)(2,1)S(1)}, bf16[2,128,512]{2,1,0:T(8,128)(2,1)S(1)}, u32[]{:S(2)}, u32[]{:S(2)}) collective-permute-start(bf16[2,128,512]{2,1,0:T(8,128)(2,1)S(1)} %get-tuple-element.55), channel_id=1, source_target_pairs={{0,2},{1,3},{2,0},{3,1},{4,6},{5,7},{6,4},{7,5},{8,10},{9,11},{10,... | collective-permute-start | bytes 786440 | tf_op jit(solution)/shard_map/ppermute | solution.py:416
  152.7 17.4 %collective-permute-start.11 = (bf16[2,128,256]{2,1,0:T(8,128)(2,1)S(1)}, bf16[2,128,256]{2,1,0:T(8,128)(2,1)S(1)}, u32[]{:S(2)}, u32[]{:S(2)}) collective-permute-start(bf16[2,128,256]{2,1,0:T(8,128)(2,1)S(1)} %copy-done.4), channel_id=1, source_target_pairs={{0,7},{1,6},{2,5},{3,4},{4,3},{5,2},{6,1},{7,0},{8,15},{9,14},{10,... | collective-permute-start | bytes 393224 | tf_op jit(solution)/shard_map/ppermute | solution.py:416
  156.1 14.4 %collective-permute-start.14 = (bf16[128,512]{1,0:T(8,128)(2,1)S(1)}, bf16[128,512]{1,0:T(8,128)(2,1)S(1)}, u32[]{:S(2)}, u32[]{:S(2)}) collective-permute-start(bf16[128,512]{1,0:T(8,128)(2,1)S(1)} %get-tuple-element.54), channel_id=1, source_target_pairs={{0,1},{1,0},{2,3},{3,2},{4,5},{5,4},{6,7},{7,6},{8,9},{9,8},{10,11... | collective-permute-start | bytes 393224 | tf_op jit(solution)/shard_map/ppermute | solution.py:416
  156.1 15.3 %collective-permute-start.16 = (bf16[128,512]{1,0:T(8,128)(2,1)S(1)}, bf16[128,512]{1,0:T(8,128)(2,1)S(1)}, u32[]{:S(2)}, u32[]{:S(2)}) collective-permute-start(bf16[128,512]{1,0:T(8,128)(2,1)S(1)} %get-tuple-element.56), channel_id=1, source_target_pairs={{0,3},{1,2},{2,1},{3,0},{4,7},{5,6},{6,5},{7,4},{8,11},{9,10},{10,... | collective-permute-start | bytes 393224 | tf_op jit(solution)/shard_map/ppermute | solution.py:416
  156.4 11.5 %collective-permute-start.18 = (bf16[2,128,512]{2,1,0:T(8,128)(2,1)S(1)}, bf16[2,128,512]{2,1,0:T(8,128)(2,1)S(1)}, u32[]{:S(2)}, u32[]{:S(2)}) collective-permute-start(bf16[2,128,512]{2,1,0:T(8,128)(2,1)S(1)} %get-tuple-element.57), channel_id=1, source_target_pairs={{0,7},{1,6},{2,5},{3,4},{4,3},{5,2},{6,1},{7,0},{8,15},{9,14},{10,... | collective-permute-start | bytes 786440 | tf_op jit(solution)/shard_map/ppermute | solution.py:416
  163.3 9.8 %collective-permute-start.20 = (bf16[128,512]{1,0:T(8,128)(2,1)S(1)}, bf16[128,512]{1,0:T(8,128)(2,1)S(1)}, u32[]{:S(2)}, u32[]{:S(2)}) collective-permute-start(bf16[128,512]{1,0:T(8,128)(2,1)S(1)} %get-tuple-element.58), channel_id=1, source_target_pairs={{0,6},{1,7},{2,4},{3,5},{4,2},{5,3},{6,0},{7,1},{8,14},{9,15},{10,... | collective-permute-start | bytes 393224 | tf_op jit(solution)/shard_map/ppermute | solution.py:416
  168.0 6.5 %collective-permute-start.17 = (bf16[128,512]{1,0:T(8,128)(2,1)S(1)}, bf16[128,512]{1,0:T(8,128)(2,1)S(1)}, u32[]{:S(2)}, u32[]{:S(2)}) collective-permute-start(bf16[128,512]{1,0:T(8,128)(2,1)S(1)} %get-tuple-element.65), channel_id=1, source_target_pairs={{0,6},{1,7},{2,4},{3,5},{4,2},{5,3},{6,0},{7,1},{8,14},{9,15},{10,... | collective-permute-start | bytes 393224 | tf_op jit(solution)/shard_map/ppermute | solution.py:416
  170.1 5.7 %collective-permute-start.19 = (bf16[128,512]{1,0:T(8,128)(2,1)S(1)}, bf16[128,512]{1,0:T(8,128)(2,1)S(1)}, u32[]{:S(2)}, u32[]{:S(2)}) collective-permute-start(bf16[128,512]{1,0:T(8,128)(2,1)S(1)} %get-tuple-element.64), channel_id=1, source_target_pairs={{0,2},{1,3},{2,0},{3,1},{4,6},{5,7},{6,4},{7,5},{8,10},{9,11},{10,... | collective-permute-start | bytes 393224 | tf_op jit(solution)/shard_map/ppermute | solution.py:416
  170.5 7.0 %collective-permute-start.7 = (bf16[128,256]{1,0:T(8,128)(2,1)S(1)}, bf16[128,256]{1,0:T(8,128)(2,1)S(1)}, u32[]{:S(2)}, u32[]{:S(2)}) collective-permute-start(bf16[128,256]{1,0:T(8,128)(2,1)S(1)} %copy-done.10), channel_id=1, source_target_pairs={{0,1},{1,0},{2,3},{3,2},{4,5},{5,4},{6,7},{7,6},{8,9},{9,8},{10,11... | collective-permute-start | bytes 196616 | tf_op jit(solution)/shard_map/ppermute | solution.py:416
  171.4 6.1 %collective-permute-start.9 = (bf16[128,256]{1,0:T(8,128)(2,1)S(1)}, bf16[128,256]{1,0:T(8,128)(2,1)S(1)}, u32[]{:S(2)}, u32[]{:S(2)}) collective-permute-start(bf16[128,256]{1,0:T(8,128)(2,1)S(1)} %copy-done.8), channel_id=1, source_target_pairs={{0,3},{1,2},{2,1},{3,0},{4,7},{5,6},{6,5},{7,4},{8,11},{9,10},{10,... | collective-permute-start | bytes 196616 | tf_op jit(solution)/shard_map/ppermute | solution.py:416
  173.1 4.3 %collective-permute-start.13 = (bf16[128,256]{1,0:T(8,128)(2,1)S(1)}, bf16[128,256]{1,0:T(8,128)(2,1)S(1)}, u32[]{:S(2)}, u32[]{:S(2)}) collective-permute-start(bf16[128,256]{1,0:T(8,128)(2,1)S(1)} %get-tuple-element.50), channel_id=1, source_target_pairs={{0,6},{1,7},{2,4},{3,5},{4,2},{5,3},{6,0},{7,1},{8,14},{9,15},{10,... | collective-permute-start | bytes 196616 | tf_op jit(solution)/shard_map/ppermute | solution.py:416
  174.5 4.5 %collective-permute-start.10 = (bf16[128,256]{1,0:T(8,128)(2,1)S(1)}, bf16[128,256]{1,0:T(8,128)(2,1)S(1)}, u32[]{:S(2)}, u32[]{:S(2)}) collective-permute-start(bf16[128,256]{1,0:T(8,128)(2,1)S(1)} %get-tuple-element.69), channel_id=1, source_target_pairs={{0,6},{1,7},{2,4},{3,5},{4,2},{5,3},{6,0},{7,1},{8,14},{9,15},{10,... | collective-permute-start | bytes 196616 | tf_op jit(solution)/shard_map/ppermute | solution.py:416
  (16 other events, 78.9 us)

commit v3 on v2

--- a/solution.py
+++ b/solution.py
@@ -16,7 +16,6 @@
 INFO = 16
 TILE = 256
 CHUNK = 64
-STRIP = 256
 VMEM_BYTES = 24 * 2**20
 F32 = jnp.float32
 BF16 = jnp.bfloat16
@@ -246,14 +245,11 @@
         mixed[rows, :] = (weights * (products[rows] - center)).astype(BF16)
 
 
-def own_gradients_kernel(
-    heads, pos, own, key, value, totals, key_out, value_out, *rest
-):
+def own_gradients_kernel(heads, pos, own, key, value, totals, key_out, value_out, *rest):
     *pieces, terms, mixed, probs = rest
     helper = pos[1]
     rows = own.shape[1] - INFO
     length = key.shape[0]
-    helpers = length // rows
     for head in range(heads):
         hc = cols_of(head)
         turned = key[:, hc].T
@@ -266,17 +262,16 @@
             mixed_into(
                 mixed, probs, key[0:end, hc], value[0:end, hc], q, g, log_total, center, start
             )
-            value_new = dot(probs[0:end, :], g, 1, 0)
-            key_new = dot(mixed[0:end, :], q, 1, 0)
+            value_new = dot(g.T, probs[0:end, :], 1, 1)
+            key_new = dot(q.T, mixed[0:end, :], 1, 1)
             if end == length:
-                value_out[:, hc] = value_new
-                key_out[:, hc] = key_new
+                value_out[hc, :] = value_new
+                key_out[hc, :] = key_new
             else:
-                value_out[0:end, hc] += value_new
-                key_out[0:end, hc] += key_new
-            query_new = (dot(turned[:, 0:end], mixed[0:end, :], 1, 0) * SCALING).T
-            terms[start:end, hc] = query_new
-    for k in range(helpers):
+                value_out[hc, 0:end] += value_new
+                key_out[hc, 0:end] += key_new
+            terms[start:end, hc] = (dot(turned[:, 0:end], mixed[0:end, :], 1, 0) * SCALING).T
+    for k in range(length // rows):
         at = pl.ds(pl.multiple_of((helper ^ k) * rows, rows), rows)
         piece_ref(pieces, k)[...] = terms[at, :].astype(BF16)
 
@@ -289,31 +284,30 @@
     )
 
 
-def routed_query_kernel(heads, routed, key, value, slots, out, mixed):
-    helpers, blocks, capacity, _ = routed.shape
+def routed_gradients_kernel(
+    heads, helpers, pos, routed, key, value, slots, key_own, value_own, out, *rest
+):
+    *pieces, key_acc, value_acc, mixed, probs = rest
+    _, blocks, capacity, _ = routed.shape
     group = helpers * capacity
     count = TILE // group
-    length = key.shape[0]
+    key_acc[...] = key_own[...]
+    value_acc[...] = value_own[...]
+    turned = [key[:, cols_of(head)].T for head in range(heads)]
 
     def body(tile, _):
-        rows = [
-            slot_row(slots, tile, head, which, group) for head in range(heads) for which in range(2)
-        ]
-        pad = jnp.zeros((8 - len(rows), TILE), F32)
-        columns = jnp.concatenate(rows + [pad], axis=0).T
         for head in range(heads):
             hc = cols_of(head)
             q = routed_tile(routed, tile, head_cols(head, heads, 0))
             g = routed_tile(routed, tile, head_cols(head, heads, 1))
-            log_total = columns[:, 2 * head : 2 * head + 1]
-            center = columns[:, 2 * head + 1 : 2 * head + 2]
-            for at in range(0, length, STRIP):
-                keys = slice(at, at + STRIP)
-                scores = dot(q, key[keys, hc], 1, 1) * (SCALING * LOG2E)
-                products = dot(g, value[keys, hc], 1, 1)
-                weights = jnp.exp2(scores - log_total)
-                mixed[head, :, keys] = (weights * (products - center)).astype(BF16)
-            query_new = dot(mixed[head], key[:, hc], 1, 0) * SCALING
+            log_total = slot_row(slots, tile, head, 0, group)
+            center = slot_row(slots, tile, head, 1, group)
+            low = mixed.at[head]
+            high = probs.at[head]
+            mixed_into(low, high, key[:, hc], value[:, hc], q, g, log_total, center, None)
+            value_acc[hc, :] += dot(g.T, high[...], 1, 1)
+            key_acc[hc, :] += dot(q.T, low[...], 1, 1)
+            query_new = (dot(turned[head], low[...], 1, 0) * SCALING).T
             for a in range(count):
                 out[:, tile * count + a, :, hc] = (
                     query_new[a * group : (a + 1) * group]
@@ -323,47 +317,13 @@
         return 0
 
     lax.fori_loop(0, blocks // count, body, 0)
-
-
-def routed_block_kernel(
-    heads, helpers, pos, routed, key, value, slots, key_own, value_own, *rest
-):
-    *pieces, key_acc, value_acc, mixed, probs = rest
-    _, blocks, capacity, _ = routed.shape
-    group = helpers * capacity
-    key_acc[...] = key_own[...]
-    value_acc[...] = value_own[...]
-
-    def body(tile, _):
-        for head in range(heads):
-            hc = cols_of(head)
-            q = routed_tile(routed, tile, head_cols(head, heads, 0))
-            g = routed_tile(routed, tile, head_cols(head, heads, 1))
-            log_total = slot_row(slots, tile, head, 0, group)
-            center = slot_row(slots, tile, head, 1, group)
-            mixed_into(
-                mixed.at[head],
-                probs.at[head],
-                key[:, hc],
-                value[:, hc],
-                q,
-                g,
-                log_total,
-                center,
-                None,
-            )
-            value_acc[:, hc] += dot(probs[head], g, 1, 0)
-            key_acc[:, hc] += dot(mixed[head], q, 1, 0)
-        return 0
-
-    lax.fori_loop(0, blocks * group // TILE, body, 0)
-    width = key_acc.shape[1]
-    share = key_acc.shape[0] // helpers
+    width = key_acc.shape[0]
+    share = key_acc.shape[1] // helpers
     for k in range(helpers):
         at = pl.ds(pl.multiple_of((pos[1] ^ k) * share, share), share)
         piece = piece_ref(pieces, k)
-        piece[:, 0:width] = (key_acc[at, :] * SCALING).astype(BF16)
-        piece[:, width : 2 * width] = value_acc[at, :].astype(BF16)
+        piece[:, 0:width] = (key_acc[:, at] * SCALING).T.astype(BF16)
+        piece[:, width : 2 * width] = value_acc[:, at].T.astype(BF16)
 
 
 def place_kernel(helpers, pos, *refs):
@@ -427,13 +387,12 @@
     return [received[k] for k in range(helpers)]
 
 
-def resident(x):
-    return pltpu.with_memory_space_constraint(x, pltpu.VMEM)
-
-
 def call(kernel, outputs, operands, position=None, scratch=(), flops=0, fast=99):
     vmem = pl.BlockSpec(memory_space=pltpu.VMEM)
-    operands = [resident(x) if n < fast else x for n, x in enumerate(operands)]
+    operands = [
+        pltpu.with_memory_space_constraint(x, pltpu.VMEM if n < fast else pltpu.HBM)
+        for n, x in enumerate(operands)
+    ]
     specs = [vmem] * len(operands)
     if position is not None:
         operands = [position] + list(operands)
@@ -471,7 +430,7 @@
 
     sent, picker, *pieces = call(
         functools.partial(pack_kernel, blocks, helpers),
-        [fast((helpers, blocks, CAPACITY, 2 * width), BF16), shape((rows, slots), BF16)]
+        [pltpu.HBM((helpers, blocks, CAPACITY, 2 * width), BF16), shape((rows, slots), BF16)]
         + piece_shapes((rows + INFO, 2 * width), BF16),
         [jnp.transpose(block_choice[0]), query_rows[0], output_grad[0]],
         position,
@@ -511,7 +470,7 @@
     tile = (heads, length, TILE)
     own_out = call(
         functools.partial(own_gradients_kernel, heads),
-        [shape((length, width), F32)] * 2 + piece_shapes((rows, width), BF16, shape),
+        [pltpu.HBM((width, length), F32)] * 2 + piece_shapes((rows, width), BF16, pltpu.HBM),
         [own, key, value, totals],
         position,
         [pltpu.VMEM((length, width), F32)] + [pltpu.VMEM(tile[1:], BF16)] * 2,
@@ -521,25 +480,18 @@
     spread, key_own, value_own = lax.optimization_barrier((spread, key_own, value_own))
     query_own = exchange(query_own, helpers)
 
-    terms = call(
-        functools.partial(routed_query_kernel, heads),
-        fast((helpers, blocks, CAPACITY, width), BF16),
-        [routed, key, value, spread],
-        scratch=[pltpu.VMEM((heads, TILE, length), BF16)],
-        flops=3 * pairs,
+    terms, *pieces = call(
+        functools.partial(routed_gradients_kernel, heads, helpers),
+        [pltpu.HBM((helpers, blocks, CAPACITY, width), BF16)] + piece_shapes((share, 2 * width), BF16, pltpu.HBM),
+        [routed, key, value, spread, key_own, value_own],
+        position,
+        [pltpu.VMEM((width, length), F32)] * 2 + [pltpu.VMEM(tile, BF16)] * 2,
+        flops=5 * pairs,
+        fast=4,
     )
     returned = swap(terms.reshape(blocks * helpers, CAPACITY, width), everyone)
     returned = returned.reshape(helpers, blocks, CAPACITY, width)
 
-    pieces = call(
-        functools.partial(routed_block_kernel, heads, helpers),
-        piece_shapes((share, 2 * width), BF16),
-        [routed, key, value, spread, key_own, value_own],
-        position,
-        [pltpu.VMEM((length, width), F32)] * 2 + [pltpu.VMEM(tile, BF16)] * 2,
-        flops=4 * pairs,
-        fast=4,
-    )
     pieces = exchange(pieces, helpers)
 
     key_grad, value_grad = call(

time: 183 us -> 173 us (0.945)
  local copies, waits for them, and re-layouts: 16.7 us -> 11.4 us
  Pallas kernels: 47.3 us -> 42.1 us
  starting transfers between devices: 62.5 us -> 65.1 us
    unnamed x36 -> x30, local copies, waits for them, and re-layouts: 12.5 us -> 5.87 us
    pallas_call x9 -> x8, Pallas kernels: 47.3 us -> 42.1 us  [call(): pl.pallas_call(kernel, out_shape=outputs, in_specs=specs, scratch_shapes=...]
    ppermute x21, starting transfers between devices: 25.1 us -> 29.9 us  [send(): return lax.ppermute(array, 'help', [(i, i ^ k) for i in range(helpers)])]
    all_to_all x4, starting transfers between devices: 37.4 us -> 35.2 us  [swap(): return lax.all_to_all(array, axes, split_axis=0, concat_axis=0, tiled=True)]
  transfers between devices with their start and end apart: 25 -> 25, of which waited for: 7 -> 10; matrix products, arithmetic and copies ran while one was open for 4% -> 7% of each run, Pallas kernels for 11% -> 7%
where the time goes in v3:
time: 173 us; the launch traced here: 172 us
  starting transfers between devices  65.1 us (38%)
  waiting for transfers between devices  52.6 us (30%)
  Pallas kernels  42.1 us (24%)
  local copies, waits for them, and re-layouts  11.4 us (7%)
    pallas_call x8, Pallas kernels, call(): pl.pallas_call(kernel, out_shape=outputs, in_specs=specs, scratch_shapes=...  42.1 us
    all_to_all x4, starting transfers between devices, swap(): return lax.all_to_all(array, axes, split_axis=0, concat_axis=0, tiled=True)  35.2 us
    ppermute x21, starting transfers between devices, send(): return lax.ppermute(array, 'help', [(i, i ^ k) for i in range(helpers)])  29.9 us
    ppermute x21, waiting for transfers between devices, send(): return lax.ppermute(array, 'help', [(i, i ^ k) for i in range(helpers)])  29.9 us
    all_to_all x4, waiting for transfers between devices, swap(): return lax.all_to_all(array, axes, split_axis=0, concat_axis=0, tiled=True)  22.8 us
    unnamed x30, local copies, waits for them, and re-layouts  5.87 us
  transfers between devices with their start and end apart: 25, of which 10 were waited for; matrix products, arithmetic and copies ran while one was open for 7% of the time, Pallas kernels for 7%

profile of v3, /device:TPU:1, one launch (start us, length us, event | category | flops | bytes accessed | tf_op | source)
XLA Modules:
  0.0 172.1 jit_solution(5588881401623350)
XLA Ops:
  0.7 3.7 %shard_map.76 = (bf16[8,32,8,512]{3,2,1,0:T(8,128)(2,1)}, bf16[128,256]{1,0:T(8,128)(2,1)S(1)}, bf16[144,512]{1,0:T(8,128)(2,1)S(1)}, bf16[144,512]{1,0:T(8,128)...) custom-call(s32[2]{0:T(128)S(1)} %pad_add_fusion.pos, ...), custom_call_target="tpu_custom_call" | custom-call | flops 268435456 | tf_op jit(solution)/shard_map/pallas_call | solution.py:400
  4.5 15.6 %all-to-all-start = ((bf16[256,8,512]{2,1,0:T(8,128)(2,1)}), bf16[256,8,512]{2,1,0:T(8,128)(2,1)S(1)}, u32[]{:S(2)}, u32[]{:S(2)}) async-start(bf16[256,8,512]{2,1,0:T(8,128)(2,1)} %bitcast.53), calls=%async_computation | async-start | bytes 4194304 | tf_op jit(solution)/shard_map/all_to_all | solution.py:411
  20.1 2.2 %collective-permute-start = (bf16[144,512]{1,0:T(8,128)(2,1)}, bf16[144,512]{1,0:T(8,128)(2,1)}, u32[]{:S(2)}, u32[]{:S(2)}) collective-permute-start(bf16[144,512]{1,0:T(8,128)(2,1)} %get-tuple-element.36), channel_id=1, source_target_pairs={{0,1},{1,0},{2,3},{3,2},{4,5},{5,4},{6,7},{7,6},{8,9},{9,8},{10,11... | collective-permute-start | bytes 442376 | tf_op jit(solution)/shard_map/ppermute | solution.py:376
  24.0 2.7 %collective-permute-start.4 = (bf16[2,144,512]{2,1,0:T(8,128)(2,1)}, bf16[2,144,512]{2,1,0:T(8,128)(2,1)}, u32[]{:S(2)}, u32[]{:S(2)}) collective-permute-start(bf16[2,144,512]{2,1,0:T(8,128)(2,1)} %get-tuple-element.39), channel_id=1, source_target_pairs={{0,7},{1,6},{2,5},{3,4},{4,3},{5,2},{6,1},{7,0},{8,15},{9,14},{10,... | collective-permute-start | bytes 884744 | tf_op jit(solution)/shard_map/ppermute | solution.py:376
  30.3 12.8 %collective-permute-done.4 = bf16[2,144,512]{2,1,0:T(8,128)(2,1)} collective-permute-done((bf16[2,144,512]{2,1,0:T(8,128)(2,1)}, bf16[2,144,512]{2,1,0:T(8,128)(2,1)}, u32[]{:S(2)}, u32[]{:S(2)}) %collective-permute-start.4) | collective-permute-done | bytes 294944 | tf_op jit(solution)/shard_map/ppermute | solution.py:376
  48.6 6.3 %collective-permute-done.3 = bf16[144,512]{1,0:T(8,128)(2,1)S(1)} collective-permute-done((bf16[144,512]{1,0:T(8,128)(2,1)S(1)}, bf16[144,512]{1,0:T(8,128)(2,1)S(1)}, u32[]{:S(2)}, u32[]{:S(2)}) %collective-permute-start.3) | collective-permute-done | bytes 147488 | tf_op jit(solution)/shard_map/ppermute | solution.py:376
  56.9 16.8 %all-to-all-done = bf16[256,8,512]{2,1,0:T(8,128)(2,1)S(1)} async-done(((bf16[256,8,512]{2,1,0:T(8,128)(2,1)}), bf16[256,8,512]{2,1,0:T(8,128)(2,1)S(1)}, u32[]{:S(2)}, u32[]{:S(2)}) %all-to-all-start) | async-done | bytes 2097184 | tf_op jit(solution)/shard_map/all_to_all | solution.py:411
  73.8 7.6 %shard_map.78 = f32[32,2,128]{2,1,0:T(2,128)} custom-call(bf16[8,32,8,512]{3,2,1,0:T(8,128)(2,1)S(1)} %bitcast.51, bf16[1024,256]{1,0:T(8,128)(2,1)S(1)} %get-tuple-element.74.key, bf16[1024,256]{1,0:T(8,128)(2,1)S(1)} %get-tuple-element.73.value), custom_call_target="tpu_custom_call" | custom-call | flops 2147483648 | tf_op jit(solution)/shard_map/pallas_call | solution.py:400
  81.4 3.9 %all-to-all-start.1 = ((f32[32,2,128]{2,1,0:T(2,128)}), f32[32,2,128]{2,1,0:T(2,128)S(1)}, u32[]{:S(2)}, u32[]{:S(2)}) async-start(f32[32,2,128]{2,1,0:T(2,128)} %shard_map.78), calls=%async_computation.1 | async-start | bytes 65536 | tf_op jit(solution)/shard_map/all_to_all | solution.py:411
  86.8 3.1 %shard_map.77.stats = f32[8,1024]{1,0:T(8,128)S(1)} custom-call(s32[2]{0:T(128)S(1)} %pad_add_fusion.pos, bf16[8,144,512]{2,1,0:T(8,128)(2,1)} %slice_dynamic-update-slice_fusion.own, bf16[1024,256]{1,0:T(8,128)(2,1)S(1)} %get-tuple-element.74.key, bf16[1024,256]{1,0:T(8,128)(2,1)S(1)} %get-tuple-element.73.value), custom_call_target="tpu_custom_call" | custom-call | flops 536870912 | tf_op jit(solution)/shard_map/pallas_call | solution.py:400
  89.9 4.0 %all-to-all-done.1.got = f32[32,2,128]{2,1,0:T(2,128)S(1)} async-done(((f32[32,2,128]{2,1,0:T(2,128)}), f32[32,2,128]{2,1,0:T(2,128)S(1)}, u32[]{:S(2)}, u32[]{:S(2)}) %all-to-all-start.1) | async-done | bytes 32800 | tf_op jit(solution)/shard_map/all_to_all | solution.py:411
  93.9 2.1 %shard_map.79 = (f32[4,1024]{1,0:T(4,128)S(1)}, f32[32,2,128]{2,1,0:T(2,128)}) custom-call(f32[8,1024]{1,0:T(8,128)S(1)} %shard_map.77.stats, f32[32,2,128]{2,1,0:T(2,128)S(1)} %all-to-all-done.1.got), custom_call_target="tpu_custom_call" | custom-call | flops 134217728 | tf_op jit(solution)/shard_map/pallas_call | solution.py:400
  96.0 5.4 %all-to-all-start.2 = ((f32[32,2,128]{2,1,0:T(2,128)}), f32[32,2,128]{2,1,0:T(2,128)S(1)}, u32[]{:S(2)}, u32[]{:S(2)}) async-start(f32[32,2,128]{2,1,0:T(2,128)} %get-tuple-element.41), calls=%async_computation.2 | async-start | bytes 65536 | tf_op jit(solution)/shard_map/all_to_all | solution.py:411
  101.4 6.5 %shard_map.80 = (f32[256,1024]{1,0:T(8,128)}, f32[256,1024]{1,0:T(8,128)}, bf16[128,256]{1,0:T(8,128)(2,1)}, bf16[128,256]{1,0:T(8,128)(2,1)}, bf16[128,256]{1,0...) custom-call(s32[2]{0:T(128)S(1)} %pad_add_fusion.pos, ...), custom_call_target="tpu_custom_call" | custom-call | flops 2147483648 | tf_op jit(solution)/shard_map/pallas_call | solution.py:400
  108.0 2.0 %all-to-all-done.2.slots = f32[32,2,128]{2,1,0:T(2,128)S(1)} async-done(((f32[32,2,128]{2,1,0:T(2,128)}), f32[32,2,128]{2,1,0:T(2,128)S(1)}, u32[]{:S(2)}, u32[]{:S(2)}) %all-to-all-start.2) | async-done | bytes 32800 | tf_op jit(solution)/shard_map/all_to_all | solution.py:411
  109.9 15.7 %shard_map.81 = (bf16[8,32,8,256]{3,2,1,0:T(8,128)(2,1)}, bf16[128,512]{1,0:T(8,128)(2,1)}, bf16[128,512]{1,0:T(8,128)(2,1)}, bf16[128,512]{1,0:T(8,128)(2,1)}, ...) custom-call(s32[2]{0:T(128)S(1)} %pad_add_fusion.pos, ...), custom_call_target="tpu_custom_call" | custom-call | flops 5368709120 | tf_op jit(solution)/shard_map/pallas_call | solution.py:400
  125.7 10.3 %all-to-all-start.3 = ((bf16[256,8,256]{2,1,0:T(8,128)(2,1)}), bf16[256,8,256]{2,1,0:T(8,128)(2,1)S(1)}, u32[]{:S(2)}, u32[]{:S(2)}) async-start(bf16[256,8,256]{2,1,0:T(8,128)(2,1)} %bitcast.54), calls=%async_computation.3 | async-start | bytes 2097152 | tf_op jit(solution)/shard_map/all_to_all | solution.py:411
  137.6 3.4 %collective-permute-start.11 = (bf16[2,128,256]{2,1,0:T(8,128)(2,1)S(1)}, bf16[2,128,256]{2,1,0:T(8,128)(2,1)S(1)}, u32[]{:S(2)}, u32[]{:S(2)}) collective-permute-start(bf16[2,128,256]{2,1,0:T(8,128)(2,1)S(1)} %copy-done.6), channel_id=1, source_target_pairs={{0,7},{1,6},{2,5},{3,4},{4,3},{5,2},{6,1},{7,0},{8,15},{9,14},{10,... | collective-permute-start | bytes 393224 | tf_op jit(solution)/shard_map/ppermute | solution.py:376
  141.7 5.5 %collective-permute-start.18 = (bf16[2,128,512]{2,1,0:T(8,128)(2,1)S(1)}, bf16[2,128,512]{2,1,0:T(8,128)(2,1)S(1)}, u32[]{:S(2)}, u32[]{:S(2)}) collective-permute-start(bf16[2,128,512]{2,1,0:T(8,128)(2,1)S(1)} %copy-done.2), channel_id=1, source_target_pairs={{0,7},{1,6},{2,5},{3,4},{4,3},{5,2},{6,1},{7,0},{8,15},{9,14},{10,... | collective-permute-start | bytes 786440 | tf_op jit(solution)/shard_map/ppermute | solution.py:376
  147.2 4.7 %collective-permute-done.15 = bf16[2,128,512]{2,1,0:T(8,128)(2,1)S(1)} collective-permute-done((bf16[2,128,512]{2,1,0:T(8,128)(2,1)S(1)}, bf16[2,128,512]{2,1,0:T(8,128)(2,1)S(1)}, u32[]{:S(2)}, u32[]{:S(2)}) %collective-permute-start.15) | collective-permute-done | bytes 262176 | tf_op jit(solution)/shard_map/ppermute | solution.py:376
  151.9 2.6 %collective-permute-start.20 = (bf16[128,512]{1,0:T(8,128)(2,1)S(1)}, bf16[128,512]{1,0:T(8,128)(2,1)S(1)}, u32[]{:S(2)}, u32[]{:S(2)}) collective-permute-start(bf16[128,512]{1,0:T(8,128)(2,1)S(1)} %copy-done.4), channel_id=1, source_target_pairs={{0,6},{1,7},{2,4},{3,5},{4,2},{5,3},{6,0},{7,1},{8,14},{9,15},{10,... | collective-permute-start | bytes 393224 | tf_op jit(solution)/shard_map/ppermute | solution.py:376
  154.5 2.9 %collective-permute-done.18 = bf16[2,128,512]{2,1,0:T(8,128)(2,1)S(1)} collective-permute-done((bf16[2,128,512]{2,1,0:T(8,128)(2,1)S(1)}, bf16[2,128,512]{2,1,0:T(8,128)(2,1)S(1)}, u32[]{:S(2)}, u32[]{:S(2)}) %collective-permute-start.18) | collective-permute-done | bytes 262176 | tf_op jit(solution)/shard_map/ppermute | solution.py:376
  157.4 3.5 %collective-permute-start.17 = (bf16[128,512]{1,0:T(8,128)(2,1)S(1)}, bf16[128,512]{1,0:T(8,128)(2,1)S(1)}, u32[]{:S(2)}, u32[]{:S(2)}) collective-permute-start(bf16[128,512]{1,0:T(8,128)(2,1)S(1)} %get-tuple-element.67), channel_id=1, source_target_pairs={{0,6},{1,7},{2,4},{3,5},{4,2},{5,3},{6,0},{7,1},{8,14},{9,15},{10,... | collective-permute-start | bytes 393224 | tf_op jit(solution)/shard_map/ppermute | solution.py:376
  162.2 1.7 %collective-permute-start.9 = (bf16[128,256]{1,0:T(8,128)(2,1)S(1)}, bf16[128,256]{1,0:T(8,128)(2,1)S(1)}, u32[]{:S(2)}, u32[]{:S(2)}) collective-permute-start(bf16[128,256]{1,0:T(8,128)(2,1)S(1)} %copy-done.10), channel_id=1, source_target_pairs={{0,3},{1,2},{2,1},{3,0},{4,7},{5,6},{6,5},{7,4},{8,11},{9,10},{10,... | collective-permute-start | bytes 196616 | tf_op jit(solution)/shard_map/ppermute | solution.py:376
  (73 shorter events, 26.2 us)
Async XLA Ops:
  4.5 69.3 %all-to-all-start = ((bf16[256,8,512]{2,1,0:T(8,128)(2,1)}), bf16[256,8,512]{2,1,0:T(8,128)(2,1)S(1)}, u32[]{:S(2)}, u32[]{:S(2)}) async-start(bf16[256,8,512]{2,1,0:T(8,128)(2,1)} %bitcast.53), calls=%async_computation | async-start | bytes 4194304 | tf_op jit(solution)/shard_map/all_to_all | solution.py:411
  20.1 8.6 %collective-permute-start = (bf16[144,512]{1,0:T(8,128)(2,1)}, bf16[144,512]{1,0:T(8,128)(2,1)}, u32[]{:S(2)}, u32[]{:S(2)}) collective-permute-start(bf16[144,512]{1,0:T(8,128)(2,1)} %get-tuple-element.36), channel_id=1, source_target_pairs={{0,1},{1,0},{2,3},{3,2},{4,5},{5,4},{6,7},{7,6},{8,9},{9,8},{10,11... | collective-permute-start | bytes 442376 | tf_op jit(solution)/shard_map/ppermute | solution.py:376
  22.3 24.7 %collective-permute-start.2 = (bf16[144,512]{1,0:T(8,128)(2,1)}, bf16[144,512]{1,0:T(8,128)(2,1)}, u32[]{:S(2)}, u32[]{:S(2)}) collective-permute-start(bf16[144,512]{1,0:T(8,128)(2,1)} %get-tuple-element.38), channel_id=1, source_target_pairs={{0,3},{1,2},{2,1},{3,0},{4,7},{5,6},{6,5},{7,4},{8,11},{9,10},{10,... | collective-permute-start | bytes 442376 | tf_op jit(solution)/shard_map/ppermute | solution.py:376
  22.3 33.9 %collective-permute-start.6 = (bf16[144,512]{1,0:T(8,128)(2,1)S(1)}, bf16[144,512]{1,0:T(8,128)(2,1)S(1)}, u32[]{:S(2)}, u32[]{:S(2)}) collective-permute-start(bf16[144,512]{1,0:T(8,128)(2,1)S(1)} %get-tuple-element.40), channel_id=1, source_target_pairs={{0,6},{1,7},{2,4},{3,5},{4,2},{5,3},{6,0},{7,1},{8,14},{9,15},{10,... | collective-permute-start | bytes 442376 | tf_op jit(solution)/shard_map/ppermute | solution.py:376
  23.7 20.9 %collective-permute-start.1 = (bf16[2,144,512]{2,1,0:T(8,128)(2,1)}, bf16[2,144,512]{2,1,0:T(8,128)(2,1)}, u32[]{:S(2)}, u32[]{:S(2)}) collective-permute-start(bf16[2,144,512]{2,1,0:T(8,128)(2,1)} %get-tuple-element.37), channel_id=1, source_target_pairs={{0,2},{1,3},{2,0},{3,1},{4,6},{5,7},{6,4},{7,5},{8,10},{9,11},{10,... | collective-permute-start | bytes 884744 | tf_op jit(solution)/shard_map/ppermute | solution.py:376
  24.0 19.0 %collective-permute-start.4 = (bf16[2,144,512]{2,1,0:T(8,128)(2,1)}, bf16[2,144,512]{2,1,0:T(8,128)(2,1)}, u32[]{:S(2)}, u32[]{:S(2)}) collective-permute-start(bf16[2,144,512]{2,1,0:T(8,128)(2,1)} %get-tuple-element.39), channel_id=1, source_target_pairs={{0,7},{1,6},{2,5},{3,4},{4,3},{5,2},{6,1},{7,0},{8,15},{9,14},{10,... | collective-permute-start | bytes 884744 | tf_op jit(solution)/shard_map/ppermute | solution.py:376
  44.0 11.6 %collective-permute-start.5 = (bf16[144,512]{1,0:T(8,128)(2,1)S(1)}, bf16[144,512]{1,0:T(8,128)(2,1)S(1)}, u32[]{:S(2)}, u32[]{:S(2)}) collective-permute-start(bf16[144,512]{1,0:T(8,128)(2,1)S(1)} %slice_bitcast_fusion), channel_id=1, source_target_pairs={{0,2},{1,3},{2,0},{3,1},{4,6},{5,7},{6,4},{7,5},{8,10},{9,11},{10,... | collective-permute-start | bytes 442376 | tf_op jit(solution)/shard_map/ppermute | solution.py:376
  46.3 8.7 %collective-permute-start.3 = (bf16[144,512]{1,0:T(8,128)(2,1)S(1)}, bf16[144,512]{1,0:T(8,128)(2,1)S(1)}, u32[]{:S(2)}, u32[]{:S(2)}) collective-permute-start(bf16[144,512]{1,0:T(8,128)(2,1)S(1)} %get-tuple-element.63), channel_id=1, source_target_pairs={{0,6},{1,7},{2,4},{3,5},{4,2},{5,3},{6,0},{7,1},{8,14},{9,15},{10,... | collective-permute-start | bytes 442376 | tf_op jit(solution)/shard_map/ppermute | solution.py:376
  81.4 12.5 %all-to-all-start.1 = ((f32[32,2,128]{2,1,0:T(2,128)}), f32[32,2,128]{2,1,0:T(2,128)S(1)}, u32[]{:S(2)}, u32[]{:S(2)}) async-start(f32[32,2,128]{2,1,0:T(2,128)} %shard_map.78), calls=%async_computation.1 | async-start | bytes 65536 | tf_op jit(solution)/shard_map/all_to_all | solution.py:411
  96.0 13.9 %all-to-all-start.2 = ((f32[32,2,128]{2,1,0:T(2,128)}), f32[32,2,128]{2,1,0:T(2,128)S(1)}, u32[]{:S(2)}, u32[]{:S(2)}) async-start(f32[32,2,128]{2,1,0:T(2,128)} %get-tuple-element.41), calls=%async_computation.2 | async-start | bytes 65536 | tf_op jit(solution)/shard_map/all_to_all | solution.py:411
  125.7 44.8 %all-to-all-start.3 = ((bf16[256,8,256]{2,1,0:T(8,128)(2,1)}), bf16[256,8,256]{2,1,0:T(8,128)(2,1)S(1)}, u32[]{:S(2)}, u32[]{:S(2)}) async-start(bf16[256,8,256]{2,1,0:T(8,128)(2,1)} %bitcast.54), calls=%async_computation.3 | async-start | bytes 2097152 | tf_op jit(solution)/shard_map/all_to_all | solution.py:411
  136.1 5.7 %collective-permute-start.8 = (bf16[2,128,256]{2,1,0:T(8,128)(2,1)S(1)}, bf16[2,128,256]{2,1,0:T(8,128)(2,1)S(1)}, u32[]{:S(2)}, u32[]{:S(2)}) collective-permute-start(bf16[2,128,256]{2,1,0:T(8,128)(2,1)S(1)} %copy-done.8), channel_id=1, source_target_pairs={{0,2},{1,3},{2,0},{3,1},{4,6},{5,7},{6,4},{7,5},{8,10},{9,11},{10,... | collective-permute-start | bytes 393224 | tf_op jit(solution)/shard_map/ppermute | solution.py:376
  137.5 14.4 %collective-permute-start.15 = (bf16[2,128,512]{2,1,0:T(8,128)(2,1)S(1)}, bf16[2,128,512]{2,1,0:T(8,128)(2,1)S(1)}, u32[]{:S(2)}, u32[]{:S(2)}) collective-permute-start(bf16[2,128,512]{2,1,0:T(8,128)(2,1)S(1)} %copy-done.3), channel_id=1, source_target_pairs={{0,2},{1,3},{2,0},{3,1},{4,6},{5,7},{6,4},{7,5},{8,10},{9,11},{10,... | collective-permute-start | bytes 786440 | tf_op jit(solution)/shard_map/ppermute | solution.py:376
  137.6 23.3 %collective-permute-start.11 = (bf16[2,128,256]{2,1,0:T(8,128)(2,1)S(1)}, bf16[2,128,256]{2,1,0:T(8,128)(2,1)S(1)}, u32[]{:S(2)}, u32[]{:S(2)}) collective-permute-start(bf16[2,128,256]{2,1,0:T(8,128)(2,1)S(1)} %copy-done.6), channel_id=1, source_target_pairs={{0,7},{1,6},{2,5},{3,4},{4,3},{5,2},{6,1},{7,0},{8,15},{9,14},{10,... | collective-permute-start | bytes 393224 | tf_op jit(solution)/shard_map/ppermute | solution.py:376
  141.0 20.1 %collective-permute-start.14 = (bf16[128,512]{1,0:T(8,128)(2,1)S(1)}, bf16[128,512]{1,0:T(8,128)(2,1)S(1)}, u32[]{:S(2)}, u32[]{:S(2)}) collective-permute-start(bf16[128,512]{1,0:T(8,128)(2,1)S(1)} %copy-done.7), channel_id=1, source_target_pairs={{0,1},{1,0},{2,3},{3,2},{4,5},{5,4},{6,7},{7,6},{8,9},{9,8},{10,11... | collective-permute-start | bytes 393224 | tf_op jit(solution)/shard_map/ppermute | solution.py:376
  141.0 21.2 %collective-permute-start.16 = (bf16[128,512]{1,0:T(8,128)(2,1)S(1)}, bf16[128,512]{1,0:T(8,128)(2,1)S(1)}, u32[]{:S(2)}, u32[]{:S(2)}) collective-permute-start(bf16[128,512]{1,0:T(8,128)(2,1)S(1)} %copy-done.5), channel_id=1, source_target_pairs={{0,3},{1,2},{2,1},{3,0},{4,7},{5,6},{6,5},{7,4},{8,11},{9,10},{10,... | collective-permute-start | bytes 393224 | tf_op jit(solution)/shard_map/ppermute | solution.py:376
  141.7 15.7 %collective-permute-start.18 = (bf16[2,128,512]{2,1,0:T(8,128)(2,1)S(1)}, bf16[2,128,512]{2,1,0:T(8,128)(2,1)S(1)}, u32[]{:S(2)}, u32[]{:S(2)}) collective-permute-start(bf16[2,128,512]{2,1,0:T(8,128)(2,1)S(1)} %copy-done.2), channel_id=1, source_target_pairs={{0,7},{1,6},{2,5},{3,4},{4,3},{5,2},{6,1},{7,0},{8,15},{9,14},{10,... | collective-permute-start | bytes 786440 | tf_op jit(solution)/shard_map/ppermute | solution.py:376
  151.9 12.0 %collective-permute-start.20 = (bf16[128,512]{1,0:T(8,128)(2,1)S(1)}, bf16[128,512]{1,0:T(8,128)(2,1)S(1)}, u32[]{:S(2)}, u32[]{:S(2)}) collective-permute-start(bf16[128,512]{1,0:T(8,128)(2,1)S(1)} %copy-done.4), channel_id=1, source_target_pairs={{0,6},{1,7},{2,4},{3,5},{4,2},{5,3},{6,0},{7,1},{8,14},{9,15},{10,... | collective-permute-start | bytes 393224 | tf_op jit(solution)/shard_map/ppermute | solution.py:376
  157.4 8.3 %collective-permute-start.17 = (bf16[128,512]{1,0:T(8,128)(2,1)S(1)}, bf16[128,512]{1,0:T(8,128)(2,1)S(1)}, u32[]{:S(2)}, u32[]{:S(2)}) collective-permute-start(bf16[128,512]{1,0:T(8,128)(2,1)S(1)} %get-tuple-element.67), channel_id=1, source_target_pairs={{0,6},{1,7},{2,4},{3,5},{4,2},{5,3},{6,0},{7,1},{8,14},{9,15},{10,... | collective-permute-start | bytes 393224 | tf_op jit(solution)/shard_map/ppermute | solution.py:376
  161.0 6.2 %collective-permute-start.19 = (bf16[128,512]{1,0:T(8,128)(2,1)S(1)}, bf16[128,512]{1,0:T(8,128)(2,1)S(1)}, u32[]{:S(2)}, u32[]{:S(2)}) collective-permute-start(bf16[128,512]{1,0:T(8,128)(2,1)S(1)} %get-tuple-element.66), channel_id=1, source_target_pairs={{0,2},{1,3},{2,0},{3,1},{4,6},{5,7},{6,4},{7,5},{8,10},{9,11},{10,... | collective-permute-start | bytes 393224 | tf_op jit(solution)/shard_map/ppermute | solution.py:376
  161.1 7.8 %collective-permute-start.7 = (bf16[128,256]{1,0:T(8,128)(2,1)S(1)}, bf16[128,256]{1,0:T(8,128)(2,1)S(1)}, u32[]{:S(2)}, u32[]{:S(2)}) collective-permute-start(bf16[128,256]{1,0:T(8,128)(2,1)S(1)} %copy-done.11), channel_id=1, source_target_pairs={{0,1},{1,0},{2,3},{3,2},{4,5},{5,4},{6,7},{7,6},{8,9},{9,8},{10,11... | collective-permute-start | bytes 196616 | tf_op jit(solution)/shard_map/ppermute | solution.py:376
  162.2 6.7 %collective-permute-start.9 = (bf16[128,256]{1,0:T(8,128)(2,1)S(1)}, bf16[128,256]{1,0:T(8,128)(2,1)S(1)}, u32[]{:S(2)}, u32[]{:S(2)}) collective-permute-start(bf16[128,256]{1,0:T(8,128)(2,1)S(1)} %copy-done.10), channel_id=1, source_target_pairs={{0,3},{1,2},{2,1},{3,0},{4,7},{5,6},{6,5},{7,4},{8,11},{9,10},{10,... | collective-permute-start | bytes 196616 | tf_op jit(solution)/shard_map/ppermute | solution.py:376
  163.9 4.9 %collective-permute-start.13 = (bf16[128,256]{1,0:T(8,128)(2,1)S(1)}, bf16[128,256]{1,0:T(8,128)(2,1)S(1)}, u32[]{:S(2)}, u32[]{:S(2)}) collective-permute-start(bf16[128,256]{1,0:T(8,128)(2,1)S(1)} %copy-done.9), channel_id=1, source_target_pairs={{0,6},{1,7},{2,4},{3,5},{4,2},{5,3},{6,0},{7,1},{8,14},{9,15},{10,... | collective-permute-start | bytes 196616 | tf_op jit(solution)/shard_map/ppermute | solution.py:376
  165.6 4.8 %collective-permute-start.10 = (bf16[128,256]{1,0:T(8,128)(2,1)S(1)}, bf16[128,256]{1,0:T(8,128)(2,1)S(1)}, u32[]{:S(2)}, u32[]{:S(2)}) collective-permute-start(bf16[128,256]{1,0:T(8,128)(2,1)S(1)} %get-tuple-element.71), channel_id=1, source_target_pairs={{0,6},{1,7},{2,4},{3,5},{4,2},{5,3},{6,0},{7,1},{8,14},{9,15},{10,... | collective-permute-start | bytes 196616 | tf_op jit(solution)/shard_map/ppermute | solution.py:376
  (13 other events, 239.4 us)

commit v4 on v3

--- a/solution.py
+++ b/solution.py
@@ -15,6 +15,7 @@
 SCALING = HEAD_DIM ** (-0.5)
 INFO = 16
 TILE = 256
+WIDE_TILE = 512
 CHUNK = 64
 VMEM_BYTES = 24 * 2**20
 F32 = jnp.float32
@@ -87,10 +88,9 @@
     return jnp.concatenate(parts, axis=0)
 
 
-def routed_tile(routed, tile, cols):
+def routed_tile(routed, tile, count, cols):
     helpers, _, capacity, _ = routed.shape
     group = helpers * capacity
-    count = TILE // group
     parts = [
         routed[:, tile * count + a, :, cols].astype(F32).reshape(group, HEAD_DIM)
         for a in range(count)
@@ -157,8 +157,8 @@
     def body(tile, _):
         for head in range(heads):
             hc = cols_of(head)
-            q = routed_tile(routed, tile, head_cols(head, heads, 0))
-            g = routed_tile(routed, tile, head_cols(head, heads, 1))
+            q = routed_tile(routed, tile, count, head_cols(head, heads, 0))
+            g = routed_tile(routed, tile, count, head_cols(head, heads, 1))
             log_sum, mean = statistics_of(key[:, hc], value[:, hc], q, g, None)
             for a in range(count):
                 cut = slice(a * group, (a + 1) * group)
@@ -276,9 +276,8 @@
         piece_ref(pieces, k)[...] = terms[at, :].astype(BF16)
 
 
-def slot_row(slots, tile, head, which, group):
+def slot_row(slots, tile, count, head, which, group):
     cut = slice(which * group, (which + 1) * group)
-    count = TILE // group
     return jnp.concatenate(
         [slots[tile * count + a, head : head + 1, cut] for a in range(count)], axis=1
     )
@@ -290,7 +289,7 @@
     *pieces, key_acc, value_acc, mixed, probs = rest
     _, blocks, capacity, _ = routed.shape
     group = helpers * capacity
-    count = TILE // group
+    count = WIDE_TILE // group
     key_acc[...] = key_own[...]
     value_acc[...] = value_own[...]
     turned = [key[:, cols_of(head)].T for head in range(heads)]
@@ -298,10 +297,10 @@
     def body(tile, _):
         for head in range(heads):
             hc = cols_of(head)
-            q = routed_tile(routed, tile, head_cols(head, heads, 0))
-            g = routed_tile(routed, tile, head_cols(head, heads, 1))
-            log_total = slot_row(slots, tile, head, 0, group)
-            center = slot_row(slots, tile, head, 1, group)
+            q = routed_tile(routed, tile, count, head_cols(head, heads, 0))
+            g = routed_tile(routed, tile, count, head_cols(head, heads, 1))
+            log_total = slot_row(slots, tile, count, head, 0, group)
+            center = slot_row(slots, tile, count, head, 1, group)
             low = mixed.at[head]
             high = probs.at[head]
             mixed_into(low, high, key[:, hc], value[:, hc], q, g, log_total, center, None)
@@ -467,13 +466,12 @@
     )
     spread = swap(spread, "ctx")
 
-    tile = (heads, length, TILE)
     own_out = call(
         functools.partial(own_gradients_kernel, heads),
         [pltpu.HBM((width, length), F32)] * 2 + piece_shapes((rows, width), BF16, pltpu.HBM),
         [own, key, value, totals],
         position,
-        [pltpu.VMEM((length, width), F32)] + [pltpu.VMEM(tile[1:], BF16)] * 2,
+        [pltpu.VMEM((length, width), F32)] + [pltpu.VMEM((length, TILE), BF16)] * 2,
         flops=2 * pairs,
     )
     key_own, value_own, *query_own = own_out
@@ -485,7 +483,7 @@
         [pltpu.HBM((helpers, blocks, CAPACITY, width), BF16)] + piece_shapes((share, 2 * width), BF16, pltpu.HBM),
         [routed, key, value, spread, key_own, value_own],
         position,
-        [pltpu.VMEM((width, length), F32)] * 2 + [pltpu.VMEM(tile, BF16)] * 2,
+        [pltpu.VMEM((width, length), F32)] * 2 + [pltpu.VMEM((heads, length, WIDE_TILE), BF16)] * 2,
         flops=5 * pairs,
         fast=4,
     )
@@ -494,16 +492,17 @@
 
     pieces = exchange(pieces, helpers)
 
+    query_grad = call(
+        functools.partial(finish_kernel, helpers),
+        shape((rows, features), BF16),
+        [picker, returned, *query_own],
+        position,
+    )
+    *pieces, query_grad = lax.optimization_barrier((*pieces, query_grad))
     key_grad, value_grad = call(
         functools.partial(place_kernel, helpers),
         [shape((share, features), BF16)] * 2,
         pieces,
-        position,
-    )
-    query_grad = call(
-        functools.partial(finish_kernel, helpers),
-        shape((rows, features), BF16),
-        [picker, returned, *query_own],
         position,
     )
     return query_grad[None], key_grad[None], value_grad[None]

time: 173 us -> 178 us (1.029)
  waiting for transfers between devices: 52.6 us -> 63.6 us
  starting transfers between devices: 65.1 us -> 59.5 us
    ppermute x21, waiting for transfers between devices: 29.9 us -> 40.8 us  [send(): return lax.ppermute(array, 'help', [(i, i ^ k) for i in range(helpers)])]
    ppermute x21, starting transfers between devices: 29.9 us -> 24.2 us  [send(): return lax.ppermute(array, 'help', [(i, i ^ k) for i in range(helpers)])]
  transfers between devices with their start and end apart: 25 -> 25, of which waited for: 10 -> 10; matrix products, arithmetic and copies ran while one was open for 7% -> 6% of each run, Pallas kernels for 7% -> 6%
where the time goes in v4:
time: 178 us; the launch traced here: 177 us
  waiting for transfers between devices  63.6 us (36%)
  starting transfers between devices  59.5 us (33%)
  Pallas kernels  41.6 us (23%)
  local copies, waits for them, and re-layouts  11.4 us (6%)
    pallas_call x8, Pallas kernels, call(): pl.pallas_call(kernel, out_shape=outputs, in_specs=specs, scratch_shapes=...  41.6 us
    ppermute x21, waiting for transfers between devices, send(): return lax.ppermute(array, 'help', [(i, i ^ k) for i in range(helpers)])  40.8 us
    all_to_all x4, starting transfers between devices, swap(): return lax.all_to_all(array, axes, split_axis=0, concat_axis=0, tiled=True)  35.2 us
    ppermute x21, starting transfers between devices, send(): return lax.ppermute(array, 'help', [(i, i ^ k) for i in range(helpers)])  24.2 us
    all_to_all x4, waiting for transfers between devices, swap(): return lax.all_to_all(array, axes, split_axis=0, concat_axis=0, tiled=True)  22.8 us
    unnamed x30, local copies, waits for them, and re-layouts  5.88 us
  transfers between devices with their start and end apart: 25, of which 10 were waited for; matrix products, arithmetic and copies ran while one was open for 6% of the time, Pallas kernels for 6%

profile of v4, /device:TPU:1, one launch (start us, length us, event | category | flops | bytes accessed | tf_op | source)
XLA Modules:
  0.0 177.0 jit_solution(7405305696831396584)
XLA Ops:
  0.7 3.7 %shard_map.76 = (bf16[8,32,8,512]{3,2,1,0:T(8,128)(2,1)}, bf16[128,256]{1,0:T(8,128)(2,1)S(1)}, bf16[144,512]{1,0:T(8,128)(2,1)S(1)}, bf16[144,512]{1,0:T(8,128)...) custom-call(s32[2]{0:T(128)S(1)} %pad_add_fusion.pos, ...), custom_call_target="tpu_custom_call" | custom-call | flops 268435456 | tf_op jit(solution)/shard_map/pallas_call | solution.py:399
  4.5 15.6 %all-to-all-start = ((bf16[256,8,512]{2,1,0:T(8,128)(2,1)}), bf16[256,8,512]{2,1,0:T(8,128)(2,1)S(1)}, u32[]{:S(2)}, u32[]{:S(2)}) async-start(bf16[256,8,512]{2,1,0:T(8,128)(2,1)} %bitcast.53), calls=%async_computation | async-start | bytes 4194304 | tf_op jit(solution)/shard_map/all_to_all | solution.py:410
  20.1 2.2 %collective-permute-start = (bf16[144,512]{1,0:T(8,128)(2,1)}, bf16[144,512]{1,0:T(8,128)(2,1)}, u32[]{:S(2)}, u32[]{:S(2)}) collective-permute-start(bf16[144,512]{1,0:T(8,128)(2,1)} %get-tuple-element.44), channel_id=1, source_target_pairs={{0,1},{1,0},{2,3},{3,2},{4,5},{5,4},{6,7},{7,6},{8,9},{9,8},{10,11... | collective-permute-start | bytes 442376 | tf_op jit(solution)/shard_map/ppermute | solution.py:375
  24.0 2.7 %collective-permute-start.4 = (bf16[2,144,512]{2,1,0:T(8,128)(2,1)}, bf16[2,144,512]{2,1,0:T(8,128)(2,1)}, u32[]{:S(2)}, u32[]{:S(2)}) collective-permute-start(bf16[2,144,512]{2,1,0:T(8,128)(2,1)} %get-tuple-element.47), channel_id=1, source_target_pairs={{0,7},{1,6},{2,5},{3,4},{4,3},{5,2},{6,1},{7,0},{8,15},{9,14},{10,... | collective-permute-start | bytes 884744 | tf_op jit(solution)/shard_map/ppermute | solution.py:375
  30.3 12.8 %collective-permute-done.4 = bf16[2,144,512]{2,1,0:T(8,128)(2,1)} collective-permute-done((bf16[2,144,512]{2,1,0:T(8,128)(2,1)}, bf16[2,144,512]{2,1,0:T(8,128)(2,1)}, u32[]{:S(2)}, u32[]{:S(2)}) %collective-permute-start.4) | collective-permute-done | bytes 294944 | tf_op jit(solution)/shard_map/ppermute | solution.py:375
  48.6 6.3 %collective-permute-done.3 = bf16[144,512]{1,0:T(8,128)(2,1)S(1)} collective-permute-done((bf16[144,512]{1,0:T(8,128)(2,1)S(1)}, bf16[144,512]{1,0:T(8,128)(2,1)S(1)}, u32[]{:S(2)}, u32[]{:S(2)}) %collective-permute-start.3) | collective-permute-done | bytes 147488 | tf_op jit(solution)/shard_map/ppermute | solution.py:375
  56.9 16.8 %all-to-all-done = bf16[256,8,512]{2,1,0:T(8,128)(2,1)S(1)} async-done(((bf16[256,8,512]{2,1,0:T(8,128)(2,1)}), bf16[256,8,512]{2,1,0:T(8,128)(2,1)S(1)}, u32[]{:S(2)}, u32[]{:S(2)}) %all-to-all-start) | async-done | bytes 2097184 | tf_op jit(solution)/shard_map/all_to_all | solution.py:410
  73.8 7.6 %shard_map.78 = f32[32,2,128]{2,1,0:T(2,128)} custom-call(bf16[8,32,8,512]{3,2,1,0:T(8,128)(2,1)S(1)} %bitcast.51, bf16[1024,256]{1,0:T(8,128)(2,1)S(1)} %get-tuple-element.92.key, bf16[1024,256]{1,0:T(8,128)(2,1)S(1)} %get-tuple-element.91.value), custom_call_target="tpu_custom_call" | custom-call | flops 2147483648 | tf_op jit(solution)/shard_map/pallas_call | solution.py:399
  81.4 3.9 %all-to-all-start.1 = ((f32[32,2,128]{2,1,0:T(2,128)}), f32[32,2,128]{2,1,0:T(2,128)S(1)}, u32[]{:S(2)}, u32[]{:S(2)}) async-start(f32[32,2,128]{2,1,0:T(2,128)} %shard_map.78), calls=%async_computation.1 | async-start | bytes 65536 | tf_op jit(solution)/shard_map/all_to_all | solution.py:410
  86.8 3.1 %shard_map.77.stats = f32[8,1024]{1,0:T(8,128)S(1)} custom-call(s32[2]{0:T(128)S(1)} %pad_add_fusion.pos, bf16[8,144,512]{2,1,0:T(8,128)(2,1)} %slice_dynamic-update-slice_fusion.own, bf16[1024,256]{1,0:T(8,128)(2,1)S(1)} %get-tuple-element.92.key, bf16[1024,256]{1,0:T(8,128)(2,1)S(1)} %get-tuple-element.91.value), custom_call_target="tpu_custom_call" | custom-call | flops 536870912 | tf_op jit(solution)/shard_map/pallas_call | solution.py:399
  89.9 4.0 %all-to-all-done.1.got = f32[32,2,128]{2,1,0:T(2,128)S(1)} async-done(((f32[32,2,128]{2,1,0:T(2,128)}), f32[32,2,128]{2,1,0:T(2,128)S(1)}, u32[]{:S(2)}, u32[]{:S(2)}) %all-to-all-start.1) | async-done | bytes 32800 | tf_op jit(solution)/shard_map/all_to_all | solution.py:410
  93.9 2.1 %shard_map.79 = (f32[4,1024]{1,0:T(4,128)S(1)}, f32[32,2,128]{2,1,0:T(2,128)}) custom-call(f32[8,1024]{1,0:T(8,128)S(1)} %shard_map.77.stats, f32[32,2,128]{2,1,0:T(2,128)S(1)} %all-to-all-done.1.got), custom_call_target="tpu_custom_call" | custom-call | flops 134217728 | tf_op jit(solution)/shard_map/pallas_call | solution.py:399
  96.0 5.4 %all-to-all-start.2 = ((f32[32,2,128]{2,1,0:T(2,128)}), f32[32,2,128]{2,1,0:T(2,128)S(1)}, u32[]{:S(2)}, u32[]{:S(2)}) async-start(f32[32,2,128]{2,1,0:T(2,128)} %get-tuple-element.49), calls=%async_computation.2 | async-start | bytes 65536 | tf_op jit(solution)/shard_map/all_to_all | solution.py:410
  101.4 6.5 %shard_map.80 = (f32[256,1024]{1,0:T(8,128)}, f32[256,1024]{1,0:T(8,128)}, bf16[128,256]{1,0:T(8,128)(2,1)}, bf16[128,256]{1,0:T(8,128)(2,1)}, bf16[128,256]{1,0...) custom-call(s32[2]{0:T(128)S(1)} %pad_add_fusion.pos, ...), custom_call_target="tpu_custom_call" | custom-call | flops 2147483648 | tf_op jit(solution)/shard_map/pallas_call | solution.py:399
  108.0 2.0 %all-to-all-done.2.slots = f32[32,2,128]{2,1,0:T(2,128)S(1)} async-done(((f32[32,2,128]{2,1,0:T(2,128)}), f32[32,2,128]{2,1,0:T(2,128)S(1)}, u32[]{:S(2)}, u32[]{:S(2)}) %all-to-all-start.2) | async-done | bytes 32800 | tf_op jit(solution)/shard_map/all_to_all | solution.py:410
  109.9 15.3 %shard_map.81 = (bf16[8,32,8,256]{3,2,1,0:T(8,128)(2,1)}, bf16[128,512]{1,0:T(8,128)(2,1)}, bf16[128,512]{1,0:T(8,128)(2,1)}, bf16[128,512]{1,0:T(8,128)(2,1)}, ...) custom-call(s32[2]{0:T(128)S(1)} %pad_add_fusion.pos, ...), custom_call_target="tpu_custom_call" | custom-call | flops 5368709120 | tf_op jit(solution)/shard_map/pallas_call | solution.py:399
  125.3 10.3 %all-to-all-start.3 = ((bf16[256,8,256]{2,1,0:T(8,128)(2,1)}), bf16[256,8,256]{2,1,0:T(8,128)(2,1)S(1)}, u32[]{:S(2)}, u32[]{:S(2)}) async-start(bf16[256,8,256]{2,1,0:T(8,128)(2,1)} %bitcast.54), calls=%async_computation.3 | async-start | bytes 2097152 | tf_op jit(solution)/shard_map/all_to_all | solution.py:410
  140.4 2.4 %collective-permute-start.18 = (bf16[2,128,256]{2,1,0:T(8,128)(2,1)S(1)}, bf16[2,128,256]{2,1,0:T(8,128)(2,1)S(1)}, u32[]{:S(2)}, u32[]{:S(2)}) collective-permute-start(bf16[2,128,256]{2,1,0:T(8,128)(2,1)S(1)} %copy-done.7), channel_id=1, source_target_pairs={{0,7},{1,6},{2,5},{3,4},{4,3},{5,2},{6,1},{7,0},{8,15},{9,14},{10,... | collective-permute-start | bytes 393224 | tf_op jit(solution)/shard_map/ppermute | solution.py:375
  144.0 7.0 %collective-permute-done.18 = bf16[2,128,256]{2,1,0:T(8,128)(2,1)S(1)} collective-permute-done((bf16[2,128,256]{2,1,0:T(8,128)(2,1)S(1)}, bf16[2,128,256]{2,1,0:T(8,128)(2,1)S(1)}, u32[]{:S(2)}, u32[]{:S(2)}) %collective-permute-start.18) | collective-permute-done | bytes 131104 | tf_op jit(solution)/shard_map/ppermute | solution.py:375
  153.5 2.1 %collective-permute-start.17 = (bf16[128,256]{1,0:T(8,128)(2,1)S(1)}, bf16[128,256]{1,0:T(8,128)(2,1)S(1)}, u32[]{:S(2)}, u32[]{:S(2)}) collective-permute-start(bf16[128,256]{1,0:T(8,128)(2,1)S(1)} %get-tuple-element.89), channel_id=1, source_target_pairs={{0,6},{1,7},{2,4},{3,5},{4,2},{5,3},{6,0},{7,1},{8,14},{9,15},{10,... | collective-permute-start | bytes 196616 | tf_op jit(solution)/shard_map/ppermute | solution.py:375
  155.6 8.8 %collective-permute-done.11 = bf16[2,128,512]{2,1,0:T(8,128)(2,1)S(1)} collective-permute-done((bf16[2,128,512]{2,1,0:T(8,128)(2,1)S(1)}, bf16[2,128,512]{2,1,0:T(8,128)(2,1)S(1)}, u32[]{:S(2)}, u32[]{:S(2)}) %collective-permute-start.11) | collective-permute-done | bytes 262176 | tf_op jit(solution)/shard_map/ppermute | solution.py:375
  164.6 1.8 %collective-permute-start.9 = (bf16[128,512]{1,0:T(8,128)(2,1)S(1)}, bf16[128,512]{1,0:T(8,128)(2,1)S(1)}, u32[]{:S(2)}, u32[]{:S(2)}) collective-permute-start(bf16[128,512]{1,0:T(8,128)(2,1)S(1)} %copy-done.5), channel_id=1, source_target_pairs={{0,3},{1,2},{2,1},{3,0},{4,7},{5,6},{6,5},{7,4},{8,11},{9,10},{10,... | collective-permute-start | bytes 393224 | tf_op jit(solution)/shard_map/ppermute | solution.py:375
  167.1 1.9 %collective-permute-start.10 = (bf16[128,512]{1,0:T(8,128)(2,1)S(1)}, bf16[128,512]{1,0:T(8,128)(2,1)S(1)}, u32[]{:S(2)}, u32[]{:S(2)}) collective-permute-start(bf16[128,512]{1,0:T(8,128)(2,1)S(1)} %get-tuple-element.85), channel_id=1, source_target_pairs={{0,6},{1,7},{2,4},{3,5},{4,2},{5,3},{6,0},{7,1},{8,14},{9,15},{10,... | collective-permute-start | bytes 393224 | tf_op jit(solution)/shard_map/ppermute | solution.py:375
  172.5 2.8 %collective-permute-done.10.refs_4_ = bf16[128,512]{1,0:T(8,128)(2,1)S(1)} collective-permute-done((bf16[128,512]{1,0:T(8,128)(2,1)S(1)}, bf16[128,512]{1,0:T(8,128)(2,1)S(1)}, u32[]{:S(2)}, u32[]{:S(2)}) %collective-permute-start.10) | collective-permute-done | bytes 131104 | tf_op jit(solution)/shard_map/ppermute | solution.py:375
  (73 shorter events, 29.0 us)
Async XLA Ops:
  4.5 69.3 %all-to-all-start = ((bf16[256,8,512]{2,1,0:T(8,128)(2,1)}), bf16[256,8,512]{2,1,0:T(8,128)(2,1)S(1)}, u32[]{:S(2)}, u32[]{:S(2)}) async-start(bf16[256,8,512]{2,1,0:T(8,128)(2,1)} %bitcast.53), calls=%async_computation | async-start | bytes 4194304 | tf_op jit(solution)/shard_map/all_to_all | solution.py:410
  20.1 8.6 %collective-permute-start = (bf16[144,512]{1,0:T(8,128)(2,1)}, bf16[144,512]{1,0:T(8,128)(2,1)}, u32[]{:S(2)}, u32[]{:S(2)}) collective-permute-start(bf16[144,512]{1,0:T(8,128)(2,1)} %get-tuple-element.44), channel_id=1, source_target_pairs={{0,1},{1,0},{2,3},{3,2},{4,5},{5,4},{6,7},{7,6},{8,9},{9,8},{10,11... | collective-permute-start | bytes 442376 | tf_op jit(solution)/shard_map/ppermute | solution.py:375
  22.3 24.7 %collective-permute-start.2 = (bf16[144,512]{1,0:T(8,128)(2,1)}, bf16[144,512]{1,0:T(8,128)(2,1)}, u32[]{:S(2)}, u32[]{:S(2)}) collective-permute-start(bf16[144,512]{1,0:T(8,128)(2,1)} %get-tuple-element.46), channel_id=1, source_target_pairs={{0,3},{1,2},{2,1},{3,0},{4,7},{5,6},{6,5},{7,4},{8,11},{9,10},{10,... | collective-permute-start | bytes 442376 | tf_op jit(solution)/shard_map/ppermute | solution.py:375
  22.3 33.9 %collective-permute-start.6 = (bf16[144,512]{1,0:T(8,128)(2,1)S(1)}, bf16[144,512]{1,0:T(8,128)(2,1)S(1)}, u32[]{:S(2)}, u32[]{:S(2)}) collective-permute-start(bf16[144,512]{1,0:T(8,128)(2,1)S(1)} %get-tuple-element.48), channel_id=1, source_target_pairs={{0,6},{1,7},{2,4},{3,5},{4,2},{5,3},{6,0},{7,1},{8,14},{9,15},{10,... | collective-permute-start | bytes 442376 | tf_op jit(solution)/shard_map/ppermute | solution.py:375
  23.7 20.9 %collective-permute-start.1 = (bf16[2,144,512]{2,1,0:T(8,128)(2,1)}, bf16[2,144,512]{2,1,0:T(8,128)(2,1)}, u32[]{:S(2)}, u32[]{:S(2)}) collective-permute-start(bf16[2,144,512]{2,1,0:T(8,128)(2,1)} %get-tuple-element.45), channel_id=1, source_target_pairs={{0,2},{1,3},{2,0},{3,1},{4,6},{5,7},{6,4},{7,5},{8,10},{9,11},{10,... | collective-permute-start | bytes 884744 | tf_op jit(solution)/shard_map/ppermute | solution.py:375
  24.0 19.0 %collective-permute-start.4 = (bf16[2,144,512]{2,1,0:T(8,128)(2,1)}, bf16[2,144,512]{2,1,0:T(8,128)(2,1)}, u32[]{:S(2)}, u32[]{:S(2)}) collective-permute-start(bf16[2,144,512]{2,1,0:T(8,128)(2,1)} %get-tuple-element.47), channel_id=1, source_target_pairs={{0,7},{1,6},{2,5},{3,4},{4,3},{5,2},{6,1},{7,0},{8,15},{9,14},{10,... | collective-permute-start | bytes 884744 | tf_op jit(solution)/shard_map/ppermute | solution.py:375
  44.0 11.6 %collective-permute-start.5 = (bf16[144,512]{1,0:T(8,128)(2,1)S(1)}, bf16[144,512]{1,0:T(8,128)(2,1)S(1)}, u32[]{:S(2)}, u32[]{:S(2)}) collective-permute-start(bf16[144,512]{1,0:T(8,128)(2,1)S(1)} %slice_bitcast_fusion), channel_id=1, source_target_pairs={{0,2},{1,3},{2,0},{3,1},{4,6},{5,7},{6,4},{7,5},{8,10},{9,11},{10,... | collective-permute-start | bytes 442376 | tf_op jit(solution)/shard_map/ppermute | solution.py:375
  46.3 8.7 %collective-permute-start.3 = (bf16[144,512]{1,0:T(8,128)(2,1)S(1)}, bf16[144,512]{1,0:T(8,128)(2,1)S(1)}, u32[]{:S(2)}, u32[]{:S(2)}) collective-permute-start(bf16[144,512]{1,0:T(8,128)(2,1)S(1)} %get-tuple-element.81), channel_id=1, source_target_pairs={{0,6},{1,7},{2,4},{3,5},{4,2},{5,3},{6,0},{7,1},{8,14},{9,15},{10,... | collective-permute-start | bytes 442376 | tf_op jit(solution)/shard_map/ppermute | solution.py:375
  81.4 12.5 %all-to-all-start.1 = ((f32[32,2,128]{2,1,0:T(2,128)}), f32[32,2,128]{2,1,0:T(2,128)S(1)}, u32[]{:S(2)}, u32[]{:S(2)}) async-start(f32[32,2,128]{2,1,0:T(2,128)} %shard_map.78), calls=%async_computation.1 | async-start | bytes 65536 | tf_op jit(solution)/shard_map/all_to_all | solution.py:410
  96.0 13.9 %all-to-all-start.2 = ((f32[32,2,128]{2,1,0:T(2,128)}), f32[32,2,128]{2,1,0:T(2,128)S(1)}, u32[]{:S(2)}, u32[]{:S(2)}) async-start(f32[32,2,128]{2,1,0:T(2,128)} %get-tuple-element.49), calls=%async_computation.2 | async-start | bytes 65536 | tf_op jit(solution)/shard_map/all_to_all | solution.py:410
  125.3 43.8 %all-to-all-start.3 = ((bf16[256,8,256]{2,1,0:T(8,128)(2,1)}), bf16[256,8,256]{2,1,0:T(8,128)(2,1)S(1)}, u32[]{:S(2)}, u32[]{:S(2)}) async-start(bf16[256,8,256]{2,1,0:T(8,128)(2,1)} %bitcast.54), calls=%async_computation.3 | async-start | bytes 2097152 | tf_op jit(solution)/shard_map/all_to_all | solution.py:410
  135.6 7.2 %collective-permute-start.15 = (bf16[2,128,256]{2,1,0:T(8,128)(2,1)S(1)}, bf16[2,128,256]{2,1,0:T(8,128)(2,1)S(1)}, u32[]{:S(2)}, u32[]{:S(2)}) collective-permute-start(bf16[2,128,256]{2,1,0:T(8,128)(2,1)S(1)} %copy-done.8), channel_id=1, source_target_pairs={{0,2},{1,3},{2,0},{3,1},{4,6},{5,7},{6,4},{7,5},{8,10},{9,11},{10,... | collective-permute-start | bytes 393224 | tf_op jit(solution)/shard_map/ppermute | solution.py:375
  137.1 27.4 %collective-permute-start.14 = (bf16[128,256]{1,0:T(8,128)(2,1)S(1)}, bf16[128,256]{1,0:T(8,128)(2,1)S(1)}, u32[]{:S(2)}, u32[]{:S(2)}) collective-permute-start(bf16[128,256]{1,0:T(8,128)(2,1)S(1)} %copy-done.11), channel_id=1, source_target_pairs={{0,1},{1,0},{2,3},{3,2},{4,5},{5,4},{6,7},{7,6},{8,9},{9,8},{10,11... | collective-permute-start | bytes 196616 | tf_op jit(solution)/shard_map/ppermute | solution.py:375
  138.0 26.6 %collective-permute-start.16 = (bf16[128,256]{1,0:T(8,128)(2,1)S(1)}, bf16[128,256]{1,0:T(8,128)(2,1)S(1)}, u32[]{:S(2)}, u32[]{:S(2)}) collective-permute-start(bf16[128,256]{1,0:T(8,128)(2,1)S(1)} %copy-done.10), channel_id=1, source_target_pairs={{0,3},{1,2},{2,1},{3,0},{4,7},{5,6},{6,5},{7,4},{8,11},{9,10},{10,... | collective-permute-start | bytes 196616 | tf_op jit(solution)/shard_map/ppermute | solution.py:375
  139.6 26.8 %collective-permute-start.20 = (bf16[128,256]{1,0:T(8,128)(2,1)S(1)}, bf16[128,256]{1,0:T(8,128)(2,1)S(1)}, u32[]{:S(2)}, u32[]{:S(2)}) collective-permute-start(bf16[128,256]{1,0:T(8,128)(2,1)S(1)} %copy-done.9), channel_id=1, source_target_pairs={{0,6},{1,7},{2,4},{3,5},{4,2},{5,3},{6,0},{7,1},{8,14},{9,15},{10,... | collective-permute-start | bytes 196616 | tf_op jit(solution)/shard_map/ppermute | solution.py:375
  140.4 10.6 %collective-permute-start.18 = (bf16[2,128,256]{2,1,0:T(8,128)(2,1)S(1)}, bf16[2,128,256]{2,1,0:T(8,128)(2,1)S(1)}, u32[]{:S(2)}, u32[]{:S(2)}) collective-permute-start(bf16[2,128,256]{2,1,0:T(8,128)(2,1)S(1)} %copy-done.7), channel_id=1, source_target_pairs={{0,7},{1,6},{2,5},{3,4},{4,3},{5,2},{6,1},{7,0},{8,15},{9,14},{10,... | collective-permute-start | bytes 393224 | tf_op jit(solution)/shard_map/ppermute | solution.py:375
  142.8 10.7 %collective-permute-start.8 = (bf16[2,128,512]{2,1,0:T(8,128)(2,1)S(1)}, bf16[2,128,512]{2,1,0:T(8,128)(2,1)S(1)}, u32[]{:S(2)}, u32[]{:S(2)}) collective-permute-start(bf16[2,128,512]{2,1,0:T(8,128)(2,1)S(1)} %copy-done.3), channel_id=1, source_target_pairs={{0,2},{1,3},{2,0},{3,1},{4,6},{5,7},{6,4},{7,5},{8,10},{9,11},{10,... | collective-permute-start | bytes 786440 | tf_op jit(solution)/shard_map/ppermute | solution.py:375
  151.0 13.4 %collective-permute-start.11 = (bf16[2,128,512]{2,1,0:T(8,128)(2,1)S(1)}, bf16[2,128,512]{2,1,0:T(8,128)(2,1)S(1)}, u32[]{:S(2)}, u32[]{:S(2)}) collective-permute-start(bf16[2,128,512]{2,1,0:T(8,128)(2,1)S(1)} %copy-done.2), channel_id=1, source_target_pairs={{0,7},{1,6},{2,5},{3,4},{4,3},{5,2},{6,1},{7,0},{8,15},{9,14},{10,... | collective-permute-start | bytes 786440 | tf_op jit(solution)/shard_map/ppermute | solution.py:375
  153.5 13.6 %collective-permute-start.17 = (bf16[128,256]{1,0:T(8,128)(2,1)S(1)}, bf16[128,256]{1,0:T(8,128)(2,1)S(1)}, u32[]{:S(2)}, u32[]{:S(2)}) collective-permute-start(bf16[128,256]{1,0:T(8,128)(2,1)S(1)} %get-tuple-element.89), channel_id=1, source_target_pairs={{0,6},{1,7},{2,4},{3,5},{4,2},{5,3},{6,0},{7,1},{8,14},{9,15},{10,... | collective-permute-start | bytes 196616 | tf_op jit(solution)/shard_map/ppermute | solution.py:375
  164.4 6.3 %collective-permute-start.7 = (bf16[128,512]{1,0:T(8,128)(2,1)S(1)}, bf16[128,512]{1,0:T(8,128)(2,1)S(1)}, u32[]{:S(2)}, u32[]{:S(2)}) collective-permute-start(bf16[128,512]{1,0:T(8,128)(2,1)S(1)} %copy-done.6), channel_id=1, source_target_pairs={{0,1},{1,0},{2,3},{3,2},{4,5},{5,4},{6,7},{7,6},{8,9},{9,8},{10,11... | collective-permute-start | bytes 393224 | tf_op jit(solution)/shard_map/ppermute | solution.py:375
  164.6 6.2 %collective-permute-start.9 = (bf16[128,512]{1,0:T(8,128)(2,1)S(1)}, bf16[128,512]{1,0:T(8,128)(2,1)S(1)}, u32[]{:S(2)}, u32[]{:S(2)}) collective-permute-start(bf16[128,512]{1,0:T(8,128)(2,1)S(1)} %copy-done.5), channel_id=1, source_target_pairs={{0,3},{1,2},{2,1},{3,0},{4,7},{5,6},{6,5},{7,4},{8,11},{9,10},{10,... | collective-permute-start | bytes 393224 | tf_op jit(solution)/shard_map/ppermute | solution.py:375
  166.4 6.2 %collective-permute-start.13 = (bf16[128,512]{1,0:T(8,128)(2,1)S(1)}, bf16[128,512]{1,0:T(8,128)(2,1)S(1)}, u32[]{:S(2)}, u32[]{:S(2)}) collective-permute-start(bf16[128,512]{1,0:T(8,128)(2,1)S(1)} %copy-done.4), channel_id=1, source_target_pairs={{0,6},{1,7},{2,4},{3,5},{4,2},{5,3},{6,0},{7,1},{8,14},{9,15},{10,... | collective-permute-start | bytes 393224 | tf_op jit(solution)/shard_map/ppermute | solution.py:375
  167.1 8.2 %collective-permute-start.10 = (bf16[128,512]{1,0:T(8,128)(2,1)S(1)}, bf16[128,512]{1,0:T(8,128)(2,1)S(1)}, u32[]{:S(2)}, u32[]{:S(2)}) collective-permute-start(bf16[128,512]{1,0:T(8,128)(2,1)S(1)} %get-tuple-element.85), channel_id=1, source_target_pairs={{0,6},{1,7},{2,4},{3,5},{4,2},{5,3},{6,0},{7,1},{8,14},{9,15},{10,... | collective-permute-start | bytes 393224 | tf_op jit(solution)/shard_map/ppermute | solution.py:375
  169.1 6.3 %collective-permute-start.12 = (bf16[128,512]{1,0:T(8,128)(2,1)S(1)}, bf16[128,512]{1,0:T(8,128)(2,1)S(1)}, u32[]{:S(2)}, u32[]{:S(2)}) collective-permute-start(bf16[128,512]{1,0:T(8,128)(2,1)S(1)} %get-tuple-element.84), channel_id=1, source_target_pairs={{0,2},{1,3},{2,0},{3,1},{4,6},{5,7},{6,4},{7,5},{8,10},{9,11},{10,... | collective-permute-start | bytes 393224 | tf_op jit(solution)/shard_map/ppermute | solution.py:375
  (13 other events, 245.7 us)

commit v5 on v4

--- a/solution.py
+++ b/solution.py
@@ -286,15 +286,34 @@
 def routed_gradients_kernel(
     heads, helpers, pos, routed, key, value, slots, key_own, value_own, out, *rest
 ):
-    *pieces, key_acc, value_acc, mixed, probs = rest
+    *pieces, key_acc, value_acc, key_got, value_got, staged, mixed, probs, sems = rest
     _, blocks, capacity, _ = routed.shape
     group = helpers * capacity
     count = WIDE_TILE // group
-    key_acc[...] = key_own[...]
-    value_acc[...] = value_own[...]
+    steps = blocks // count
+    key_copy = pltpu.make_async_copy(key_own, key_got, sems.at[0])
+    value_copy = pltpu.make_async_copy(value_own, value_got, sems.at[1])
+    key_copy.start()
+    value_copy.start()
     turned = [key[:, cols_of(head)].T for head in range(heads)]
 
+    def sending(tile):
+        return pltpu.make_async_copy(
+            staged.at[tile % 2],
+            out.at[:, pl.ds(tile * count, count)],
+            sems.at[2 + tile % 2],
+        )
+
+    key_acc[...] = jnp.zeros(key_acc.shape, F32)
+    value_acc[...] = jnp.zeros(value_acc.shape, F32)
+
     def body(tile, _):
+        slot = tile % 2
+
+        @pl.when(tile >= 2)
+        def _():
+            sending(tile - 2).wait()
+
         for head in range(heads):
             hc = cols_of(head)
             q = routed_tile(routed, tile, count, head_cols(head, heads, 0))
@@ -308,21 +327,26 @@
             key_acc[hc, :] += dot(q.T, low[...], 1, 1)
             query_new = (dot(turned[head], low[...], 1, 0) * SCALING).T
             for a in range(count):
-                out[:, tile * count + a, :, hc] = (
+                staged[slot, :, a, :, hc] = (
                     query_new[a * group : (a + 1) * group]
                     .reshape(helpers, capacity, HEAD_DIM)
                     .astype(BF16)
                 )
+        sending(tile).start()
         return 0
 
-    lax.fori_loop(0, blocks // count, body, 0)
+    lax.fori_loop(0, steps, body, 0)
+    key_copy.wait()
+    value_copy.wait()
     width = key_acc.shape[0]
     share = key_acc.shape[1] // helpers
     for k in range(helpers):
         at = pl.ds(pl.multiple_of((pos[1] ^ k) * share, share), share)
         piece = piece_ref(pieces, k)
-        piece[:, 0:width] = (key_acc[:, at] * SCALING).T.astype(BF16)
-        piece[:, width : 2 * width] = value_acc[:, at].T.astype(BF16)
+        piece[0:width, :] = ((key_acc[:, at] + key_got[:, at]) * SCALING).astype(BF16)
+        piece[width : 2 * width, :] = (value_acc[:, at] + value_got[:, at]).astype(BF16)
+    for tile in range(max(0, steps - 2), steps):
+        sending(tile).wait()
 
 
 def place_kernel(helpers, pos, *refs):
@@ -331,8 +355,8 @@
     width = key_out.shape[1] // helpers
     for k in range(helpers):
         cols = pl.ds(pl.multiple_of((pos[1] ^ k) * width, width), width)
-        key_out[:, cols] = pieces[k][:, 0:width]
-        value_out[:, cols] = pieces[k][:, width : 2 * width]
+        key_out[:, cols] = pieces[k][0:width, :].astype(F32).T.astype(BF16)
+        value_out[:, cols] = pieces[k][width : 2 * width, :].astype(F32).T.astype(BF16)
 
 
 def finish_kernel(helpers, pos, picker, returned, *refs):
@@ -386,13 +410,17 @@
     return [received[k] for k in range(helpers)]
 
 
-def call(kernel, outputs, operands, position=None, scratch=(), flops=0, fast=99):
+def call(kernel, outputs, operands, position=None, scratch=(), flops=0, fast=99, hand_in=(), hand_out=()):
     vmem = pl.BlockSpec(memory_space=pltpu.VMEM)
     operands = [
         pltpu.with_memory_space_constraint(x, pltpu.VMEM if n < fast else pltpu.HBM)
         for n, x in enumerate(operands)
     ]
-    specs = [vmem] * len(operands)
+    hand = pl.BlockSpec(memory_space=pltpu.HBM)
+    specs = [hand if n in hand_in else vmem for n in range(len(operands))]
+    out_specs = None
+    if hand_out:
+        out_specs = [hand if n in hand_out else vmem for n in range(len(outputs))]
     if position is not None:
         operands = [position] + list(operands)
         specs = [pl.BlockSpec(memory_space=pltpu.SMEM)] + specs
@@ -400,6 +428,7 @@
         kernel,
         out_shape=outputs,
         in_specs=specs,
+        **({"out_specs": out_specs} if out_specs else {}),
         scratch_shapes=scratch,
         compiler_params=pltpu.CompilerParams(vmem_limit_bytes=VMEM_BYTES),
         cost_estimate=pl.CostEstimate(flops=flops, bytes_accessed=0, transcendentals=0),
@@ -480,12 +509,17 @@
 
     terms, *pieces = call(
         functools.partial(routed_gradients_kernel, heads, helpers),
-        [pltpu.HBM((helpers, blocks, CAPACITY, width), BF16)] + piece_shapes((share, 2 * width), BF16, pltpu.HBM),
+        [pltpu.HBM((helpers, blocks, CAPACITY, width), BF16)] + piece_shapes((2 * width, share), BF16, pltpu.HBM),
         [routed, key, value, spread, key_own, value_own],
         position,
-        [pltpu.VMEM((width, length), F32)] * 2 + [pltpu.VMEM((heads, length, WIDE_TILE), BF16)] * 2,
+        [pltpu.VMEM((width, length), F32)] * 4
+        + [pltpu.VMEM((2, helpers, WIDE_TILE // group, CAPACITY, width), BF16)]
+        + [pltpu.VMEM((heads, length, WIDE_TILE), BF16)] * 2
+        + [pltpu.SemaphoreType.DMA((4,))],
         flops=5 * pairs,
         fast=4,
+        hand_in=(4, 5),
+        hand_out=(0,),
     )
     returned = swap(terms.reshape(blocks * helpers, CAPACITY, width), everyone)
     returned = returned.reshape(helpers, blocks, CAPACITY, width)
@@ -498,7 +532,6 @@
         [picker, returned, *query_own],
         position,
     )
-    *pieces, query_grad = lax.optimization_barrier((*pieces, query_grad))
     key_grad, value_grad = call(
         functools.partial(place_kernel, helpers),
         [shape((share, features), BF16)] * 2,

time: 178 us -> 172 us (0.966)
  waiting for transfers between devices: 63.6 us -> 52.4 us
  starting transfers between devices: 59.5 us -> 65.1 us
    ppermute x21, waiting for transfers between devices: 40.8 us -> 29.6 us  [send(): return lax.ppermute(array, 'help', [(i, i ^ k) for i in range(helpers)])]
    ppermute x21, starting transfers between devices: 24.2 us -> 29.9 us  [send(): return lax.ppermute(array, 'help', [(i, i ^ k) for i in range(helpers)])]
  transfers between devices with their start and end apart: 25 -> 25, of which waited for: 10 -> 10; matrix products, arithmetic and copies ran while one was open for 6% -> 7% of each run, Pallas kernels for 6% -> 7%
where the time goes in v5:
time: 172 us; the launch traced here: 171 us
  starting transfers between devices  65.1 us (38%)
  waiting for transfers between devices  52.4 us (30%)
  Pallas kernels  41.1 us (24%)
  local copies, waits for them, and re-layouts  11.4 us (7%)
    pallas_call x8, Pallas kernels, call(): pl.pallas_call(kernel, out_shape=outputs, in_specs=specs, **{'out_specs':...  41.1 us
    all_to_all x4, starting transfers between devices, swap(): return lax.all_to_all(array, axes, split_axis=0, concat_axis=0, tiled=True)  35.3 us
    ppermute x21, starting transfers between devices, send(): return lax.ppermute(array, 'help', [(i, i ^ k) for i in range(helpers)])  29.9 us
    ppermute x21, waiting for transfers between devices, send(): return lax.ppermute(array, 'help', [(i, i ^ k) for i in range(helpers)])  29.6 us
    all_to_all x4, waiting for transfers between devices, swap(): return lax.all_to_all(array, axes, split_axis=0, concat_axis=0, tiled=True)  22.8 us
    unnamed x30, local copies, waits for them, and re-layouts  5.88 us
  transfers between devices with their start and end apart: 25, of which 10 were waited for; matrix products, arithmetic and copies ran while one was open for 7% of the time, Pallas kernels for 7%

profile of v5, /device:TPU:1, one launch (start us, length us, event | category | flops | bytes accessed | tf_op | source)
XLA Modules:
  0.0 171.0 jit_solution(7366569423948987327)
XLA Ops:
  0.7 3.7 %shard_map.76 = (bf16[8,32,8,512]{3,2,1,0:T(8,128)(2,1)}, bf16[128,256]{1,0:T(8,128)(2,1)S(1)}, bf16[144,512]{1,0:T(8,128)(2,1)S(1)}, bf16[144,512]{1,0:T(8,128)...) custom-call(s32[2]{0:T(128)S(1)} %pad_add_fusion.pos, ...), custom_call_target="tpu_custom_call" | custom-call | flops 268435456 | tf_op jit(solution)/shard_map/pallas_call | solution.py:427
  4.5 15.6 %all-to-all-start = ((bf16[256,8,512]{2,1,0:T(8,128)(2,1)}), bf16[256,8,512]{2,1,0:T(8,128)(2,1)S(1)}, u32[]{:S(2)}, u32[]{:S(2)}) async-start(bf16[256,8,512]{2,1,0:T(8,128)(2,1)} %bitcast.53), calls=%async_computation | async-start | bytes 4194304 | tf_op jit(solution)/shard_map/all_to_all | solution.py:439
  20.1 2.2 %collective-permute-start = (bf16[144,512]{1,0:T(8,128)(2,1)}, bf16[144,512]{1,0:T(8,128)(2,1)}, u32[]{:S(2)}, u32[]{:S(2)}) collective-permute-start(bf16[144,512]{1,0:T(8,128)(2,1)} %get-tuple-element.36), channel_id=1, source_target_pairs={{0,1},{1,0},{2,3},{3,2},{4,5},{5,4},{6,7},{7,6},{8,9},{9,8},{10,11... | collective-permute-start | bytes 442376 | tf_op jit(solution)/shard_map/ppermute | solution.py:399
  24.0 2.7 %collective-permute-start.4 = (bf16[2,144,512]{2,1,0:T(8,128)(2,1)}, bf16[2,144,512]{2,1,0:T(8,128)(2,1)}, u32[]{:S(2)}, u32[]{:S(2)}) collective-permute-start(bf16[2,144,512]{2,1,0:T(8,128)(2,1)} %get-tuple-element.39), channel_id=1, source_target_pairs={{0,7},{1,6},{2,5},{3,4},{4,3},{5,2},{6,1},{7,0},{8,15},{9,14},{10,... | collective-permute-start | bytes 884744 | tf_op jit(solution)/shard_map/ppermute | solution.py:399
  30.3 12.8 %collective-permute-done.4 = bf16[2,144,512]{2,1,0:T(8,128)(2,1)} collective-permute-done((bf16[2,144,512]{2,1,0:T(8,128)(2,1)}, bf16[2,144,512]{2,1,0:T(8,128)(2,1)}, u32[]{:S(2)}, u32[]{:S(2)}) %collective-permute-start.4) | collective-permute-done | bytes 294944 | tf_op jit(solution)/shard_map/ppermute | solution.py:399
  48.6 6.3 %collective-permute-done.3 = bf16[144,512]{1,0:T(8,128)(2,1)S(1)} collective-permute-done((bf16[144,512]{1,0:T(8,128)(2,1)S(1)}, bf16[144,512]{1,0:T(8,128)(2,1)S(1)}, u32[]{:S(2)}, u32[]{:S(2)}) %collective-permute-start.3) | collective-permute-done | bytes 147488 | tf_op jit(solution)/shard_map/ppermute | solution.py:399
  56.9 16.8 %all-to-all-done = bf16[256,8,512]{2,1,0:T(8,128)(2,1)S(1)} async-done(((bf16[256,8,512]{2,1,0:T(8,128)(2,1)}), bf16[256,8,512]{2,1,0:T(8,128)(2,1)S(1)}, u32[]{:S(2)}, u32[]{:S(2)}) %all-to-all-start) | async-done | bytes 2097184 | tf_op jit(solution)/shard_map/all_to_all | solution.py:439
  73.8 7.6 %shard_map.78 = f32[32,2,128]{2,1,0:T(2,128)} custom-call(bf16[8,32,8,512]{3,2,1,0:T(8,128)(2,1)S(1)} %bitcast.51, bf16[1024,256]{1,0:T(8,128)(2,1)S(1)} %get-tuple-element.74.key, bf16[1024,256]{1,0:T(8,128)(2,1)S(1)} %get-tuple-element.73.value), custom_call_target="tpu_custom_call" | custom-call | flops 2147483648 | tf_op jit(solution)/shard_map/pallas_call | solution.py:427
  81.4 3.9 %all-to-all-start.1 = ((f32[32,2,128]{2,1,0:T(2,128)}), f32[32,2,128]{2,1,0:T(2,128)S(1)}, u32[]{:S(2)}, u32[]{:S(2)}) async-start(f32[32,2,128]{2,1,0:T(2,128)} %shard_map.78), calls=%async_computation.1 | async-start | bytes 65536 | tf_op jit(solution)/shard_map/all_to_all | solution.py:439
  86.8 3.1 %shard_map.77.stats = f32[8,1024]{1,0:T(8,128)S(1)} custom-call(s32[2]{0:T(128)S(1)} %pad_add_fusion.pos, bf16[8,144,512]{2,1,0:T(8,128)(2,1)} %slice_dynamic-update-slice_fusion.own, bf16[1024,256]{1,0:T(8,128)(2,1)S(1)} %get-tuple-element.74.key, bf16[1024,256]{1,0:T(8,128)(2,1)S(1)} %get-tuple-element.73.value), custom_call_target="tpu_custom_call" | custom-call | flops 536870912 | tf_op jit(solution)/shard_map/pallas_call | solution.py:427
  89.9 4.0 %all-to-all-done.1.got = f32[32,2,128]{2,1,0:T(2,128)S(1)} async-done(((f32[32,2,128]{2,1,0:T(2,128)}), f32[32,2,128]{2,1,0:T(2,128)S(1)}, u32[]{:S(2)}, u32[]{:S(2)}) %all-to-all-start.1) | async-done | bytes 32800 | tf_op jit(solution)/shard_map/all_to_all | solution.py:439
  93.9 2.1 %shard_map.79 = (f32[4,1024]{1,0:T(4,128)S(1)}, f32[32,2,128]{2,1,0:T(2,128)}) custom-call(f32[8,1024]{1,0:T(8,128)S(1)} %shard_map.77.stats, f32[32,2,128]{2,1,0:T(2,128)S(1)} %all-to-all-done.1.got), custom_call_target="tpu_custom_call" | custom-call | flops 134217728 | tf_op jit(solution)/shard_map/pallas_call | solution.py:427
  96.0 5.4 %all-to-all-start.2 = ((f32[32,2,128]{2,1,0:T(2,128)}), f32[32,2,128]{2,1,0:T(2,128)S(1)}, u32[]{:S(2)}, u32[]{:S(2)}) async-start(f32[32,2,128]{2,1,0:T(2,128)} %get-tuple-element.41), calls=%async_computation.2 | async-start | bytes 65536 | tf_op jit(solution)/shard_map/all_to_all | solution.py:439
  101.4 6.5 %shard_map.80 = (f32[256,1024]{1,0:T(8,128)}, f32[256,1024]{1,0:T(8,128)}, bf16[128,256]{1,0:T(8,128)(2,1)}, bf16[128,256]{1,0:T(8,128)(2,1)}, bf16[128,256]{1,0...) custom-call(s32[2]{0:T(128)S(1)} %pad_add_fusion.pos, ...), custom_call_target="tpu_custom_call" | custom-call | flops 2147483648 | tf_op jit(solution)/shard_map/pallas_call | solution.py:427
  108.0 2.0 %all-to-all-done.2.slots = f32[32,2,128]{2,1,0:T(2,128)S(1)} async-done(((f32[32,2,128]{2,1,0:T(2,128)}), f32[32,2,128]{2,1,0:T(2,128)S(1)}, u32[]{:S(2)}, u32[]{:S(2)}) %all-to-all-start.2) | async-done | bytes 32800 | tf_op jit(solution)/shard_map/all_to_all | solution.py:439
  109.9 14.5 %shard_map.81 = (bf16[8,32,8,256]{3,2,1,0:T(8,128)(2,1)}, bf16[512,128]{1,0:T(8,128)(2,1)}, bf16[512,128]{1,0:T(8,128)(2,1)}, bf16[512,128]{1,0:T(8,128)(2,1)}, ...) custom-call(s32[2]{0:T(128)S(1)} %pad_add_fusion.pos, ...), custom_call_target="tpu_custom_call" | custom-call | flops 5368709120 | tf_op jit(solution)/shard_map/pallas_call | solution.py:427
  124.5 10.3 %all-to-all-start.3 = ((bf16[256,8,256]{2,1,0:T(8,128)(2,1)}), bf16[256,8,256]{2,1,0:T(8,128)(2,1)S(1)}, u32[]{:S(2)}, u32[]{:S(2)}) async-start(bf16[256,8,256]{2,1,0:T(8,128)(2,1)} %bitcast.54), calls=%async_computation.3 | async-start | bytes 2097152 | tf_op jit(solution)/shard_map/all_to_all | solution.py:439
  136.5 3.4 %collective-permute-start.11 = (bf16[2,128,256]{2,1,0:T(8,128)(2,1)S(1)}, bf16[2,128,256]{2,1,0:T(8,128)(2,1)S(1)}, u32[]{:S(2)}, u32[]{:S(2)}) collective-permute-start(bf16[2,128,256]{2,1,0:T(8,128)(2,1)S(1)} %copy-done.6), channel_id=1, source_target_pairs={{0,7},{1,6},{2,5},{3,4},{4,3},{5,2},{6,1},{7,0},{8,15},{9,14},{10,... | collective-permute-start | bytes 393224 | tf_op jit(solution)/shard_map/ppermute | solution.py:399
  140.6 5.5 %collective-permute-start.18 = (bf16[2,512,128]{2,1,0:T(8,128)(2,1)S(1)}, bf16[2,512,128]{2,1,0:T(8,128)(2,1)S(1)}, u32[]{:S(2)}, u32[]{:S(2)}) collective-permute-start(bf16[2,512,128]{2,1,0:T(8,128)(2,1)S(1)} %copy-done.2), channel_id=1, source_target_pairs={{0,7},{1,6},{2,5},{3,4},{4,3},{5,2},{6,1},{7,0},{8,15},{9,14},{10,... | collective-permute-start | bytes 786440 | tf_op jit(solution)/shard_map/ppermute | solution.py:399
  146.1 4.7 %collective-permute-done.15 = bf16[2,512,128]{2,1,0:T(8,128)(2,1)S(1)} collective-permute-done((bf16[2,512,128]{2,1,0:T(8,128)(2,1)S(1)}, bf16[2,512,128]{2,1,0:T(8,128)(2,1)S(1)}, u32[]{:S(2)}, u32[]{:S(2)}) %collective-permute-start.15) | collective-permute-done | bytes 262176 | tf_op jit(solution)/shard_map/ppermute | solution.py:399
  150.7 2.6 %collective-permute-start.20 = (bf16[512,128]{1,0:T(8,128)(2,1)S(1)}, bf16[512,128]{1,0:T(8,128)(2,1)S(1)}, u32[]{:S(2)}, u32[]{:S(2)}) collective-permute-start(bf16[512,128]{1,0:T(8,128)(2,1)S(1)} %copy-done.4), channel_id=1, source_target_pairs={{0,6},{1,7},{2,4},{3,5},{4,2},{5,3},{6,0},{7,1},{8,14},{9,15},{10,... | collective-permute-start | bytes 393224 | tf_op jit(solution)/shard_map/ppermute | solution.py:399
  153.4 2.9 %collective-permute-done.18 = bf16[2,512,128]{2,1,0:T(8,128)(2,1)S(1)} collective-permute-done((bf16[2,512,128]{2,1,0:T(8,128)(2,1)S(1)}, bf16[2,512,128]{2,1,0:T(8,128)(2,1)S(1)}, u32[]{:S(2)}, u32[]{:S(2)}) %collective-permute-start.18) | collective-permute-done | bytes 262176 | tf_op jit(solution)/shard_map/ppermute | solution.py:399
  156.2 3.5 %collective-permute-start.17 = (bf16[512,128]{1,0:T(8,128)(2,1)S(1)}, bf16[512,128]{1,0:T(8,128)(2,1)S(1)}, u32[]{:S(2)}, u32[]{:S(2)}) collective-permute-start(bf16[512,128]{1,0:T(8,128)(2,1)S(1)} %get-tuple-element.67), channel_id=1, source_target_pairs={{0,6},{1,7},{2,4},{3,5},{4,2},{5,3},{6,0},{7,1},{8,14},{9,15},{10,... | collective-permute-start | bytes 393224 | tf_op jit(solution)/shard_map/ppermute | solution.py:399
  166.1 1.9 %shard_map.83 = (bf16[128,2048]{1,0:T(8,128)(2,1)}, bf16[128,2048]{1,0:T(8,128)(2,1)}) custom-call(s32[2]{0:T(128)S(1)} %pad_add_fusion.pos, bf16[512,128]{1,0:T(8,128)(2,1)S(1)} %copy-done, bf16[512,128]{1,0:T(8,128)(2,1)S(1)} %collective-permute-done.14.refs_1_, bf16[512,128]{1,0:T(8,128)(2,1)S(1)} %get-tuple-element.68.refs_2_, ...), custom_call_target="tpu_custom_call" | custom-call | tf_op jit(solution)/shard_map/pallas_call | solution.py:427
  (73 shorter events, 26.1 us)
Async XLA Ops:
  4.5 69.3 %all-to-all-start = ((bf16[256,8,512]{2,1,0:T(8,128)(2,1)}), bf16[256,8,512]{2,1,0:T(8,128)(2,1)S(1)}, u32[]{:S(2)}, u32[]{:S(2)}) async-start(bf16[256,8,512]{2,1,0:T(8,128)(2,1)} %bitcast.53), calls=%async_computation | async-start | bytes 4194304 | tf_op jit(solution)/shard_map/all_to_all | solution.py:439
  20.1 8.6 %collective-permute-start = (bf16[144,512]{1,0:T(8,128)(2,1)}, bf16[144,512]{1,0:T(8,128)(2,1)}, u32[]{:S(2)}, u32[]{:S(2)}) collective-permute-start(bf16[144,512]{1,0:T(8,128)(2,1)} %get-tuple-element.36), channel_id=1, source_target_pairs={{0,1},{1,0},{2,3},{3,2},{4,5},{5,4},{6,7},{7,6},{8,9},{9,8},{10,11... | collective-permute-start | bytes 442376 | tf_op jit(solution)/shard_map/ppermute | solution.py:399
  22.3 24.7 %collective-permute-start.2 = (bf16[144,512]{1,0:T(8,128)(2,1)}, bf16[144,512]{1,0:T(8,128)(2,1)}, u32[]{:S(2)}, u32[]{:S(2)}) collective-permute-start(bf16[144,512]{1,0:T(8,128)(2,1)} %get-tuple-element.38), channel_id=1, source_target_pairs={{0,3},{1,2},{2,1},{3,0},{4,7},{5,6},{6,5},{7,4},{8,11},{9,10},{10,... | collective-permute-start | bytes 442376 | tf_op jit(solution)/shard_map/ppermute | solution.py:399
  22.3 33.9 %collective-permute-start.6 = (bf16[144,512]{1,0:T(8,128)(2,1)S(1)}, bf16[144,512]{1,0:T(8,128)(2,1)S(1)}, u32[]{:S(2)}, u32[]{:S(2)}) collective-permute-start(bf16[144,512]{1,0:T(8,128)(2,1)S(1)} %get-tuple-element.40), channel_id=1, source_target_pairs={{0,6},{1,7},{2,4},{3,5},{4,2},{5,3},{6,0},{7,1},{8,14},{9,15},{10,... | collective-permute-start | bytes 442376 | tf_op jit(solution)/shard_map/ppermute | solution.py:399
  23.7 20.9 %collective-permute-start.1 = (bf16[2,144,512]{2,1,0:T(8,128)(2,1)}, bf16[2,144,512]{2,1,0:T(8,128)(2,1)}, u32[]{:S(2)}, u32[]{:S(2)}) collective-permute-start(bf16[2,144,512]{2,1,0:T(8,128)(2,1)} %get-tuple-element.37), channel_id=1, source_target_pairs={{0,2},{1,3},{2,0},{3,1},{4,6},{5,7},{6,4},{7,5},{8,10},{9,11},{10,... | collective-permute-start | bytes 884744 | tf_op jit(solution)/shard_map/ppermute | solution.py:399
  24.0 19.0 %collective-permute-start.4 = (bf16[2,144,512]{2,1,0:T(8,128)(2,1)}, bf16[2,144,512]{2,1,0:T(8,128)(2,1)}, u32[]{:S(2)}, u32[]{:S(2)}) collective-permute-start(bf16[2,144,512]{2,1,0:T(8,128)(2,1)} %get-tuple-element.39), channel_id=1, source_target_pairs={{0,7},{1,6},{2,5},{3,4},{4,3},{5,2},{6,1},{7,0},{8,15},{9,14},{10,... | collective-permute-start | bytes 884744 | tf_op jit(solution)/shard_map/ppermute | solution.py:399
  44.0 11.6 %collective-permute-start.5 = (bf16[144,512]{1,0:T(8,128)(2,1)S(1)}, bf16[144,512]{1,0:T(8,128)(2,1)S(1)}, u32[]{:S(2)}, u32[]{:S(2)}) collective-permute-start(bf16[144,512]{1,0:T(8,128)(2,1)S(1)} %slice_bitcast_fusion), channel_id=1, source_target_pairs={{0,2},{1,3},{2,0},{3,1},{4,6},{5,7},{6,4},{7,5},{8,10},{9,11},{10,... | collective-permute-start | bytes 442376 | tf_op jit(solution)/shard_map/ppermute | solution.py:399
  46.3 8.7 %collective-permute-start.3 = (bf16[144,512]{1,0:T(8,128)(2,1)S(1)}, bf16[144,512]{1,0:T(8,128)(2,1)S(1)}, u32[]{:S(2)}, u32[]{:S(2)}) collective-permute-start(bf16[144,512]{1,0:T(8,128)(2,1)S(1)} %get-tuple-element.63), channel_id=1, source_target_pairs={{0,6},{1,7},{2,4},{3,5},{4,2},{5,3},{6,0},{7,1},{8,14},{9,15},{10,... | collective-permute-start | bytes 442376 | tf_op jit(solution)/shard_map/ppermute | solution.py:399
  81.4 12.5 %all-to-all-start.1 = ((f32[32,2,128]{2,1,0:T(2,128)}), f32[32,2,128]{2,1,0:T(2,128)S(1)}, u32[]{:S(2)}, u32[]{:S(2)}) async-start(f32[32,2,128]{2,1,0:T(2,128)} %shard_map.78), calls=%async_computation.1 | async-start | bytes 65536 | tf_op jit(solution)/shard_map/all_to_all | solution.py:439
  96.0 13.9 %all-to-all-start.2 = ((f32[32,2,128]{2,1,0:T(2,128)}), f32[32,2,128]{2,1,0:T(2,128)S(1)}, u32[]{:S(2)}, u32[]{:S(2)}) async-start(f32[32,2,128]{2,1,0:T(2,128)} %get-tuple-element.41), calls=%async_computation.2 | async-start | bytes 65536 | tf_op jit(solution)/shard_map/all_to_all | solution.py:439
  124.5 44.8 %all-to-all-start.3 = ((bf16[256,8,256]{2,1,0:T(8,128)(2,1)}), bf16[256,8,256]{2,1,0:T(8,128)(2,1)S(1)}, u32[]{:S(2)}, u32[]{:S(2)}) async-start(bf16[256,8,256]{2,1,0:T(8,128)(2,1)} %bitcast.54), calls=%async_computation.3 | async-start | bytes 2097152 | tf_op jit(solution)/shard_map/all_to_all | solution.py:439
  134.9 5.7 %collective-permute-start.8 = (bf16[2,128,256]{2,1,0:T(8,128)(2,1)S(1)}, bf16[2,128,256]{2,1,0:T(8,128)(2,1)S(1)}, u32[]{:S(2)}, u32[]{:S(2)}) collective-permute-start(bf16[2,128,256]{2,1,0:T(8,128)(2,1)S(1)} %copy-done.8), channel_id=1, source_target_pairs={{0,2},{1,3},{2,0},{3,1},{4,6},{5,7},{6,4},{7,5},{8,10},{9,11},{10,... | collective-permute-start | bytes 393224 | tf_op jit(solution)/shard_map/ppermute | solution.py:399
  136.4 14.4 %collective-permute-start.15 = (bf16[2,512,128]{2,1,0:T(8,128)(2,1)S(1)}, bf16[2,512,128]{2,1,0:T(8,128)(2,1)S(1)}, u32[]{:S(2)}, u32[]{:S(2)}) collective-permute-start(bf16[2,512,128]{2,1,0:T(8,128)(2,1)S(1)} %copy-done.3), channel_id=1, source_target_pairs={{0,2},{1,3},{2,0},{3,1},{4,6},{5,7},{6,4},{7,5},{8,10},{9,11},{10,... | collective-permute-start | bytes 786440 | tf_op jit(solution)/shard_map/ppermute | solution.py:399
  136.5 23.3 %collective-permute-start.11 = (bf16[2,128,256]{2,1,0:T(8,128)(2,1)S(1)}, bf16[2,128,256]{2,1,0:T(8,128)(2,1)S(1)}, u32[]{:S(2)}, u32[]{:S(2)}) collective-permute-start(bf16[2,128,256]{2,1,0:T(8,128)(2,1)S(1)} %copy-done.6), channel_id=1, source_target_pairs={{0,7},{1,6},{2,5},{3,4},{4,3},{5,2},{6,1},{7,0},{8,15},{9,14},{10,... | collective-permute-start | bytes 393224 | tf_op jit(solution)/shard_map/ppermute | solution.py:399
  139.9 20.1 %collective-permute-start.14 = (bf16[512,128]{1,0:T(8,128)(2,1)S(1)}, bf16[512,128]{1,0:T(8,128)(2,1)S(1)}, u32[]{:S(2)}, u32[]{:S(2)}) collective-permute-start(bf16[512,128]{1,0:T(8,128)(2,1)S(1)} %copy-done.7), channel_id=1, source_target_pairs={{0,1},{1,0},{2,3},{3,2},{4,5},{5,4},{6,7},{7,6},{8,9},{9,8},{10,11... | collective-permute-start | bytes 393224 | tf_op jit(solution)/shard_map/ppermute | solution.py:399
  139.9 20.9 %collective-permute-start.16 = (bf16[512,128]{1,0:T(8,128)(2,1)S(1)}, bf16[512,128]{1,0:T(8,128)(2,1)S(1)}, u32[]{:S(2)}, u32[]{:S(2)}) collective-permute-start(bf16[512,128]{1,0:T(8,128)(2,1)S(1)} %copy-done.5), channel_id=1, source_target_pairs={{0,3},{1,2},{2,1},{3,0},{4,7},{5,6},{6,5},{7,4},{8,11},{9,10},{10,... | collective-permute-start | bytes 393224 | tf_op jit(solution)/shard_map/ppermute | solution.py:399
  140.6 15.7 %collective-permute-start.18 = (bf16[2,512,128]{2,1,0:T(8,128)(2,1)S(1)}, bf16[2,512,128]{2,1,0:T(8,128)(2,1)S(1)}, u32[]{:S(2)}, u32[]{:S(2)}) collective-permute-start(bf16[2,512,128]{2,1,0:T(8,128)(2,1)S(1)} %copy-done.2), channel_id=1, source_target_pairs={{0,7},{1,6},{2,5},{3,4},{4,3},{5,2},{6,1},{7,0},{8,15},{9,14},{10,... | collective-permute-start | bytes 786440 | tf_op jit(solution)/shard_map/ppermute | solution.py:399
  150.7 11.8 %collective-permute-start.20 = (bf16[512,128]{1,0:T(8,128)(2,1)S(1)}, bf16[512,128]{1,0:T(8,128)(2,1)S(1)}, u32[]{:S(2)}, u32[]{:S(2)}) collective-permute-start(bf16[512,128]{1,0:T(8,128)(2,1)S(1)} %copy-done.4), channel_id=1, source_target_pairs={{0,6},{1,7},{2,4},{3,5},{4,2},{5,3},{6,0},{7,1},{8,14},{9,15},{10,... | collective-permute-start | bytes 393224 | tf_op jit(solution)/shard_map/ppermute | solution.py:399
  156.2 8.3 %collective-permute-start.17 = (bf16[512,128]{1,0:T(8,128)(2,1)S(1)}, bf16[512,128]{1,0:T(8,128)(2,1)S(1)}, u32[]{:S(2)}, u32[]{:S(2)}) collective-permute-start(bf16[512,128]{1,0:T(8,128)(2,1)S(1)} %get-tuple-element.67), channel_id=1, source_target_pairs={{0,6},{1,7},{2,4},{3,5},{4,2},{5,3},{6,0},{7,1},{8,14},{9,15},{10,... | collective-permute-start | bytes 393224 | tf_op jit(solution)/shard_map/ppermute | solution.py:399
  159.8 6.2 %collective-permute-start.19 = (bf16[512,128]{1,0:T(8,128)(2,1)S(1)}, bf16[512,128]{1,0:T(8,128)(2,1)S(1)}, u32[]{:S(2)}, u32[]{:S(2)}) collective-permute-start(bf16[512,128]{1,0:T(8,128)(2,1)S(1)} %get-tuple-element.66), channel_id=1, source_target_pairs={{0,2},{1,3},{2,0},{3,1},{4,6},{5,7},{6,4},{7,5},{8,10},{9,11},{10,... | collective-permute-start | bytes 393224 | tf_op jit(solution)/shard_map/ppermute | solution.py:399
  160.0 8.0 %collective-permute-start.7 = (bf16[128,256]{1,0:T(8,128)(2,1)S(1)}, bf16[128,256]{1,0:T(8,128)(2,1)S(1)}, u32[]{:S(2)}, u32[]{:S(2)}) collective-permute-start(bf16[128,256]{1,0:T(8,128)(2,1)S(1)} %copy-done.11), channel_id=1, source_target_pairs={{0,1},{1,0},{2,3},{3,2},{4,5},{5,4},{6,7},{7,6},{8,9},{9,8},{10,11... | collective-permute-start | bytes 196616 | tf_op jit(solution)/shard_map/ppermute | solution.py:399
  160.8 7.1 %collective-permute-start.9 = (bf16[128,256]{1,0:T(8,128)(2,1)S(1)}, bf16[128,256]{1,0:T(8,128)(2,1)S(1)}, u32[]{:S(2)}, u32[]{:S(2)}) collective-permute-start(bf16[128,256]{1,0:T(8,128)(2,1)S(1)} %copy-done.10), channel_id=1, source_target_pairs={{0,3},{1,2},{2,1},{3,0},{4,7},{5,6},{6,5},{7,4},{8,11},{9,10},{10,... | collective-permute-start | bytes 196616 | tf_op jit(solution)/shard_map/ppermute | solution.py:399
  162.6 5.4 %collective-permute-start.13 = (bf16[128,256]{1,0:T(8,128)(2,1)S(1)}, bf16[128,256]{1,0:T(8,128)(2,1)S(1)}, u32[]{:S(2)}, u32[]{:S(2)}) collective-permute-start(bf16[128,256]{1,0:T(8,128)(2,1)S(1)} %copy-done.9), channel_id=1, source_target_pairs={{0,6},{1,7},{2,4},{3,5},{4,2},{5,3},{6,0},{7,1},{8,14},{9,15},{10,... | collective-permute-start | bytes 196616 | tf_op jit(solution)/shard_map/ppermute | solution.py:399
  164.5 4.8 %collective-permute-start.10 = (bf16[128,256]{1,0:T(8,128)(2,1)S(1)}, bf16[128,256]{1,0:T(8,128)(2,1)S(1)}, u32[]{:S(2)}, u32[]{:S(2)}) collective-permute-start(bf16[128,256]{1,0:T(8,128)(2,1)S(1)} %get-tuple-element.71), channel_id=1, source_target_pairs={{0,6},{1,7},{2,4},{3,5},{4,2},{5,3},{6,0},{7,1},{8,14},{9,15},{10,... | collective-permute-start | bytes 196616 | tf_op jit(solution)/shard_map/ppermute | solution.py:399
  (13 other events, 239.2 us)

commit v6 on v5

--- a/solution.py
+++ b/solution.py
@@ -32,11 +32,12 @@
     )
 
 
-def pack_kernel(blocks, helpers, pos, choice, query, grad, sent, picker_out, *own):
+def pack_kernel(
+    blocks, helpers, pos, choice, query, grad, sent, picker_out, info_out, staged, sems
+):
     rows = query.shape[0]
     width = query.shape[1] // helpers
     center = pos[0]
-    helper = pos[1]
     slots = blocks * CAPACITY
     targets = []
     matches = []
@@ -56,22 +57,32 @@
         places.append(p)
         code = jnp.where(targets[r] >= 0, targets[r] * CAPACITY + p.astype(jnp.int32), -1)
         picker = picker + jnp.where(iota((slots, rows), 0) == code, 1.0, 0.0)
-    picker_out[...] = picker.T.astype(BF16)
     low = picker.astype(BF16)
+    copies = []
     for d in range(helpers):
         for n, source in enumerate((query, grad)):
             got = dot(low, source[:, d * width : (d + 1) * width], 1, 0)
-            sent[d, :, :, n * width : (n + 1) * width] = got.reshape(
+            staged[d, :, :, n * width : (n + 1) * width] = got.reshape(
                 blocks, CAPACITY, width
             ).astype(BF16)
+        copies.append(pltpu.make_async_copy(staged.at[d], sent.at[d], sems.at[d]))
+        copies[-1].start()
+    picker_out[...] = picker.T.astype(BF16)
     info = jnp.concatenate([t.astype(F32) for t in targets] + places, axis=1)
-    info = jnp.broadcast_to(info, (INFO, info.shape[1])).astype(BF16)
+    info_out[...] = jnp.broadcast_to(info, (INFO, info.shape[1])).astype(BF16)
+    for copy in copies:
+        copy.wait()
+
+
+def pack_own_kernel(helpers, pos, query, grad, info, *own):
+    rows = query.shape[0]
+    width = query.shape[1] // helpers
     for k in range(helpers):
-        cols = pl.ds(pl.multiple_of((helper ^ k) * width, width), width)
+        cols = pl.ds(pl.multiple_of((pos[1] ^ k) * width, width), width)
         piece = piece_ref(own, k)
         piece[0:rows, 0:width] = query[:, cols]
         piece[0:rows, width : 2 * width] = grad[:, cols]
-        piece[rows : rows + INFO, :] = info
+        piece[rows : rows + INFO, :] = info[...]
 
 
 def head_cols(head, heads, which):
@@ -456,13 +467,28 @@
     fast = pltpu.VMEM
     everyone = ("help", "ctx")
 
-    sent, picker, *pieces = call(
+    sent, picker, info = call(
         functools.partial(pack_kernel, blocks, helpers),
-        [pltpu.HBM((helpers, blocks, CAPACITY, 2 * width), BF16), shape((rows, slots), BF16)]
-        + piece_shapes((rows + INFO, 2 * width), BF16),
+        [
+            pltpu.HBM((helpers, blocks, CAPACITY, 2 * width), BF16),
+            pltpu.HBM((rows, slots), BF16),
+            pltpu.HBM((INFO, 2 * width), BF16),
+        ],
         [jnp.transpose(block_choice[0]), query_rows[0], output_grad[0]],
         position,
+        [
+            pltpu.VMEM((helpers, blocks, CAPACITY, 2 * width), BF16),
+            pltpu.SemaphoreType.DMA((helpers,)),
+        ],
         flops=2 * rows * slots * features * 2,
+        fast=0,
+        hand_out=(0,),
+    )
+    pieces = call(
+        functools.partial(pack_own_kernel, helpers),
+        piece_shapes((rows + INFO, 2 * width), BF16, pltpu.HBM),
+        [query_rows[0], output_grad[0], info],
+        position,
         fast=0,
     )
     own = jnp.stack(exchange(pieces, helpers))

time: 172 us -> 171 us (level)
  Pallas kernels: 41.1 us -> 43.3 us
  waiting for transfers between devices: 52.4 us -> 50.2 us
    pallas_call x8 -> x9, Pallas kernels: 41.1 us -> 43.3 us  [call(): pl.pallas_call(kernel, out_shape=outputs, in_specs=specs, **{'out_specs':...]
    unnamed x30 -> x26, local copies, waits for them, and re-layouts: 5.88 us -> 7.7 us
  transfers between devices with their start and end apart: 25 -> 25, of which waited for: 10 -> 10; matrix products, arithmetic and copies ran while one was open for 7% -> 7% of each run, Pallas kernels for 7% -> 8%
where the time goes in v6:
time: 171 us; the launch traced here: 170 us
  starting transfers between devices  64.3 us (38%)
  waiting for transfers between devices  50.2 us (29%)
  Pallas kernels  43.3 us (25%)
  local copies, waits for them, and re-layouts  11.4 us (7%)
    pallas_call x9, Pallas kernels, call(): pl.pallas_call(kernel, out_shape=outputs, in_specs=specs, **{'out_specs':...  43.3 us
    all_to_all x4, starting transfers between devices, swap(): return lax.all_to_all(array, axes, split_axis=0, concat_axis=0, tiled=True)  34.5 us
    ppermute x21, starting transfers between devices, send(): return lax.ppermute(array, 'help', [(i, i ^ k) for i in range(helpers)])  29.8 us
    ppermute x21, waiting for transfers between devices, send(): return lax.ppermute(array, 'help', [(i, i ^ k) for i in range(helpers)])  28.9 us
    all_to_all x4, waiting for transfers between devices, swap(): return lax.all_to_all(array, axes, split_axis=0, concat_axis=0, tiled=True)  21.2 us
    unnamed x26, local copies, waits for them, and re-layouts  7.7 us
  transfers between devices with their start and end apart: 25, of which 10 were waited for; matrix products, arithmetic and copies ran while one was open for 7% of the time, Pallas kernels for 8%

profile of v6, /device:TPU:1, one launch (start us, length us, event | category | flops | bytes accessed | tf_op | source)
XLA Modules:
  0.0 170.2 jit_solution(4000002859433160913)
XLA Ops:
  0.7 3.6 %shard_map.76 = (bf16[8,32,8,512]{3,2,1,0:T(8,128)(2,1)}, bf16[128,256]{1,0:T(8,128)(2,1)}, bf16[16,512]{1,0:T(8,128)(2,1)}) custom-call(s32[2]{0:T(128)S(1)} %pad_add_fusion.pos, s32[2,128]{1,0:T(2,128)} %bitcast.60, bf16[128,2048]{1,0:T(8,128)(2,1)} %bitcast.54, bf16[128,2048]{1,0:T(8,128)(2,1)} %bitcast.56), custom_call_target="tpu_custom_call" | custom-call | flops 268435456 | tf_op jit(solution)/shard_map/pallas_call | solution.py:438
  4.4 15.7 %all-to-all-start = ((bf16[256,8,512]{2,1,0:T(8,128)(2,1)}), bf16[256,8,512]{2,1,0:T(8,128)(2,1)S(1)}, u32[]{:S(2)}, u32[]{:S(2)}) async-start(bf16[256,8,512]{2,1,0:T(8,128)(2,1)} %bitcast.53), calls=%async_computation | async-start | bytes 4194304 | tf_op jit(solution)/shard_map/all_to_all | solution.py:450
  20.0 2.4 %shard_map.77 = (bf16[144,512]{1,0:T(8,128)(2,1)}, bf16[144,512]{1,0:T(8,128)(2,1)}, bf16[144,512]{1,0:T(8,128)(2,1)}, bf16[144,512]{1,0:T(8,128)(2,1)}, bf16[2,...) custom-call(s32[2]{0:T(128)S(1)} %pad_add_fusion.pos, bf16[128,2048]{1,0:T(8,128)(2,1)} %bitcast.55, ...), custom_call_target="tpu_custom_call" | custom-call | tf_op jit(solution)/shard_map/pallas_call | solution.py:438
  22.4 2.1 %collective-permute-start = (bf16[144,512]{1,0:T(8,128)(2,1)}, bf16[144,512]{1,0:T(8,128)(2,1)}, u32[]{:S(2)}, u32[]{:S(2)}) collective-permute-start(bf16[144,512]{1,0:T(8,128)(2,1)} %get-tuple-element.38), channel_id=1, source_target_pairs={{0,1},{1,0},{2,3},{3,2},{4,5},{5,4},{6,7},{7,6},{8,9},{9,8},{10,11... | collective-permute-start | bytes 442376 | tf_op jit(solution)/shard_map/ppermute | solution.py:410
  26.2 2.7 %collective-permute-start.4 = (bf16[2,144,512]{2,1,0:T(8,128)(2,1)}, bf16[2,144,512]{2,1,0:T(8,128)(2,1)S(1)}, u32[]{:S(2)}, u32[]{:S(2)}) collective-permute-start(bf16[2,144,512]{2,1,0:T(8,128)(2,1)} %get-tuple-element.41), channel_id=1, source_target_pairs={{0,7},{1,6},{2,5},{3,4},{4,3},{5,2},{6,1},{7,0},{8,15},{9,14},{10,... | collective-permute-start | bytes 884744 | tf_op jit(solution)/shard_map/ppermute | solution.py:410
  33.4 12.2 %collective-permute-done.4 = bf16[2,144,512]{2,1,0:T(8,128)(2,1)S(1)} collective-permute-done((bf16[2,144,512]{2,1,0:T(8,128)(2,1)}, bf16[2,144,512]{2,1,0:T(8,128)(2,1)S(1)}, u32[]{:S(2)}, u32[]{:S(2)}) %collective-permute-start.4) | collective-permute-done | bytes 294944 | tf_op jit(solution)/shard_map/ppermute | solution.py:410
  50.3 6.0 %collective-permute-done.3 = bf16[144,512]{1,0:T(8,128)(2,1)S(1)} collective-permute-done((bf16[144,512]{1,0:T(8,128)(2,1)S(1)}, bf16[144,512]{1,0:T(8,128)(2,1)S(1)}, u32[]{:S(2)}, u32[]{:S(2)}) %collective-permute-start.3) | collective-permute-done | bytes 147488 | tf_op jit(solution)/shard_map/ppermute | solution.py:410
  59.3 14.4 %all-to-all-done = bf16[256,8,512]{2,1,0:T(8,128)(2,1)S(1)} async-done(((bf16[256,8,512]{2,1,0:T(8,128)(2,1)}), bf16[256,8,512]{2,1,0:T(8,128)(2,1)S(1)}, u32[]{:S(2)}, u32[]{:S(2)}) %all-to-all-start) | async-done | bytes 2097184 | tf_op jit(solution)/shard_map/all_to_all | solution.py:450
  73.7 7.6 %shard_map.79 = f32[32,2,128]{2,1,0:T(2,128)} custom-call(bf16[8,32,8,512]{3,2,1,0:T(8,128)(2,1)S(1)} %bitcast.51, bf16[1024,256]{1,0:T(8,128)(2,1)S(1)} %get-tuple-element.76.key, bf16[1024,256]{1,0:T(8,128)(2,1)S(1)} %get-tuple-element.75.value), custom_call_target="tpu_custom_call" | custom-call | flops 2147483648 | tf_op jit(solution)/shard_map/pallas_call | solution.py:438
  81.3 3.9 %all-to-all-start.1 = ((f32[32,2,128]{2,1,0:T(2,128)}), f32[32,2,128]{2,1,0:T(2,128)S(1)}, u32[]{:S(2)}, u32[]{:S(2)}) async-start(f32[32,2,128]{2,1,0:T(2,128)} %shard_map.79), calls=%async_computation.1 | async-start | bytes 65536 | tf_op jit(solution)/shard_map/all_to_all | solution.py:450
  85.8 3.1 %shard_map.78.stats = f32[8,1024]{1,0:T(8,128)S(1)} custom-call(s32[2]{0:T(128)S(1)} %pad_add_fusion.pos, bf16[8,144,512]{2,1,0:T(8,128)(2,1)} %slice_dynamic-update-slice_fusion.own, bf16[1024,256]{1,0:T(8,128)(2,1)S(1)} %get-tuple-element.76.key, bf16[1024,256]{1,0:T(8,128)(2,1)S(1)} %get-tuple-element.75.value), custom_call_target="tpu_custom_call" | custom-call | flops 536870912 | tf_op jit(solution)/shard_map/pallas_call | solution.py:438
  88.9 4.9 %all-to-all-done.1.got = f32[32,2,128]{2,1,0:T(2,128)S(1)} async-done(((f32[32,2,128]{2,1,0:T(2,128)}), f32[32,2,128]{2,1,0:T(2,128)S(1)}, u32[]{:S(2)}, u32[]{:S(2)}) %all-to-all-start.1) | async-done | bytes 32800 | tf_op jit(solution)/shard_map/all_to_all | solution.py:450
  93.8 2.1 %shard_map.80 = (f32[4,1024]{1,0:T(4,128)S(1)}, f32[32,2,128]{2,1,0:T(2,128)}) custom-call(f32[8,1024]{1,0:T(8,128)S(1)} %shard_map.78.stats, f32[32,2,128]{2,1,0:T(2,128)S(1)} %all-to-all-done.1.got), custom_call_target="tpu_custom_call" | custom-call | flops 134217728 | tf_op jit(solution)/shard_map/pallas_call | solution.py:438
  95.9 4.5 %all-to-all-start.2 = ((f32[32,2,128]{2,1,0:T(2,128)}), f32[32,2,128]{2,1,0:T(2,128)S(1)}, u32[]{:S(2)}, u32[]{:S(2)}) async-start(f32[32,2,128]{2,1,0:T(2,128)} %get-tuple-element.43), calls=%async_computation.2 | async-start | bytes 65536 | tf_op jit(solution)/shard_map/all_to_all | solution.py:450
  100.4 6.6 %shard_map.81 = (f32[256,1024]{1,0:T(8,128)}, f32[256,1024]{1,0:T(8,128)}, bf16[128,256]{1,0:T(8,128)(2,1)}, bf16[128,256]{1,0:T(8,128)(2,1)}, bf16[128,256]{1,0...) custom-call(s32[2]{0:T(128)S(1)} %pad_add_fusion.pos, ...), custom_call_target="tpu_custom_call" | custom-call | flops 2147483648 | tf_op jit(solution)/shard_map/pallas_call | solution.py:438
  107.0 2.0 %all-to-all-done.2.slots = f32[32,2,128]{2,1,0:T(2,128)S(1)} async-done(((f32[32,2,128]{2,1,0:T(2,128)}), f32[32,2,128]{2,1,0:T(2,128)S(1)}, u32[]{:S(2)}, u32[]{:S(2)}) %all-to-all-start.2) | async-done | bytes 32800 | tf_op jit(solution)/shard_map/all_to_all | solution.py:450
  108.9 14.5 %shard_map.82 = (bf16[8,32,8,256]{3,2,1,0:T(8,128)(2,1)}, bf16[512,128]{1,0:T(8,128)(2,1)}, bf16[512,128]{1,0:T(8,128)(2,1)}, bf16[512,128]{1,0:T(8,128)(2,1)}, ...) custom-call(s32[2]{0:T(128)S(1)} %pad_add_fusion.pos, ...), custom_call_target="tpu_custom_call" | custom-call | flops 5368709120 | tf_op jit(solution)/shard_map/pallas_call | solution.py:438
  123.5 10.5 %all-to-all-start.3 = ((bf16[256,8,256]{2,1,0:T(8,128)(2,1)}), bf16[256,8,256]{2,1,0:T(8,128)(2,1)S(1)}, u32[]{:S(2)}, u32[]{:S(2)}) async-start(bf16[256,8,256]{2,1,0:T(8,128)(2,1)} %bitcast.58), calls=%async_computation.3 | async-start | bytes 2097152 | tf_op jit(solution)/shard_map/all_to_all | solution.py:450
  135.6 3.4 %collective-permute-start.11 = (bf16[2,128,256]{2,1,0:T(8,128)(2,1)S(1)}, bf16[2,128,256]{2,1,0:T(8,128)(2,1)S(1)}, u32[]{:S(2)}, u32[]{:S(2)}) collective-permute-start(bf16[2,128,256]{2,1,0:T(8,128)(2,1)S(1)} %copy-done.5), channel_id=1, source_target_pairs={{0,7},{1,6},{2,5},{3,4},{4,3},{5,2},{6,1},{7,0},{8,15},{9,14},{10,... | collective-permute-start | bytes 393224 | tf_op jit(solution)/shard_map/ppermute | solution.py:410
  139.7 5.5 %collective-permute-start.18 = (bf16[2,512,128]{2,1,0:T(8,128)(2,1)S(1)}, bf16[2,512,128]{2,1,0:T(8,128)(2,1)S(1)}, u32[]{:S(2)}, u32[]{:S(2)}) collective-permute-start(bf16[2,512,128]{2,1,0:T(8,128)(2,1)S(1)} %copy-done.3), channel_id=1, source_target_pairs={{0,7},{1,6},{2,5},{3,4},{4,3},{5,2},{6,1},{7,0},{8,15},{9,14},{10,... | collective-permute-start | bytes 786440 | tf_op jit(solution)/shard_map/ppermute | solution.py:410
  145.2 4.7 %collective-permute-done.15 = bf16[2,512,128]{2,1,0:T(8,128)(2,1)S(1)} collective-permute-done((bf16[2,512,128]{2,1,0:T(8,128)(2,1)S(1)}, bf16[2,512,128]{2,1,0:T(8,128)(2,1)S(1)}, u32[]{:S(2)}, u32[]{:S(2)}) %collective-permute-start.15) | collective-permute-done | bytes 262176 | tf_op jit(solution)/shard_map/ppermute | solution.py:410
  149.9 2.6 %collective-permute-start.20 = (bf16[512,128]{1,0:T(8,128)(2,1)}, bf16[512,128]{1,0:T(8,128)(2,1)S(1)}, u32[]{:S(2)}, u32[]{:S(2)}) collective-permute-start(bf16[512,128]{1,0:T(8,128)(2,1)} %get-tuple-element.62), channel_id=1, source_target_pairs={{0,6},{1,7},{2,4},{3,5},{4,2},{5,3},{6,0},{7,1},{8,14},{9,15},{10,... | collective-permute-start | bytes 393224 | tf_op jit(solution)/shard_map/ppermute | solution.py:410
  152.5 2.9 %collective-permute-done.18 = bf16[2,512,128]{2,1,0:T(8,128)(2,1)S(1)} collective-permute-done((bf16[2,512,128]{2,1,0:T(8,128)(2,1)S(1)}, bf16[2,512,128]{2,1,0:T(8,128)(2,1)S(1)}, u32[]{:S(2)}, u32[]{:S(2)}) %collective-permute-start.18) | collective-permute-done | bytes 262176 | tf_op jit(solution)/shard_map/ppermute | solution.py:410
  155.4 3.5 %collective-permute-start.17 = (bf16[512,128]{1,0:T(8,128)(2,1)S(1)}, bf16[512,128]{1,0:T(8,128)(2,1)S(1)}, u32[]{:S(2)}, u32[]{:S(2)}) collective-permute-start(bf16[512,128]{1,0:T(8,128)(2,1)S(1)} %get-tuple-element.69), channel_id=1, source_target_pairs={{0,6},{1,7},{2,4},{3,5},{4,2},{5,3},{6,0},{7,1},{8,14},{9,15},{10,... | collective-permute-start | bytes 393224 | tf_op jit(solution)/shard_map/ppermute | solution.py:410
  (70 shorter events, 28.0 us)
Async XLA Ops:
  4.4 69.3 %all-to-all-start = ((bf16[256,8,512]{2,1,0:T(8,128)(2,1)}), bf16[256,8,512]{2,1,0:T(8,128)(2,1)S(1)}, u32[]{:S(2)}, u32[]{:S(2)}) async-start(bf16[256,8,512]{2,1,0:T(8,128)(2,1)} %bitcast.53), calls=%async_computation | async-start | bytes 4194304 | tf_op jit(solution)/shard_map/all_to_all | solution.py:450
  22.4 9.4 %collective-permute-start = (bf16[144,512]{1,0:T(8,128)(2,1)}, bf16[144,512]{1,0:T(8,128)(2,1)}, u32[]{:S(2)}, u32[]{:S(2)}) collective-permute-start(bf16[144,512]{1,0:T(8,128)(2,1)} %get-tuple-element.38), channel_id=1, source_target_pairs={{0,1},{1,0},{2,3},{3,2},{4,5},{5,4},{6,7},{7,6},{8,9},{9,8},{10,11... | collective-permute-start | bytes 442376 | tf_op jit(solution)/shard_map/ppermute | solution.py:410
  24.5 24.2 %collective-permute-start.2 = (bf16[144,512]{1,0:T(8,128)(2,1)}, bf16[144,512]{1,0:T(8,128)(2,1)}, u32[]{:S(2)}, u32[]{:S(2)}) collective-permute-start(bf16[144,512]{1,0:T(8,128)(2,1)} %get-tuple-element.40), channel_id=1, source_target_pairs={{0,3},{1,2},{2,1},{3,0},{4,7},{5,6},{6,5},{7,4},{8,11},{9,10},{10,... | collective-permute-start | bytes 442376 | tf_op jit(solution)/shard_map/ppermute | solution.py:410
  24.5 33.2 %collective-permute-start.6 = (bf16[144,512]{1,0:T(8,128)(2,1)}, bf16[144,512]{1,0:T(8,128)(2,1)}, u32[]{:S(2)}, u32[]{:S(2)}) collective-permute-start(bf16[144,512]{1,0:T(8,128)(2,1)} %get-tuple-element.42), channel_id=1, source_target_pairs={{0,6},{1,7},{2,4},{3,5},{4,2},{5,3},{6,0},{7,1},{8,14},{9,15},{10,... | collective-permute-start | bytes 442376 | tf_op jit(solution)/shard_map/ppermute | solution.py:410
  25.9 20.0 %collective-permute-start.1 = (bf16[2,144,512]{2,1,0:T(8,128)(2,1)}, bf16[2,144,512]{2,1,0:T(8,128)(2,1)}, u32[]{:S(2)}, u32[]{:S(2)}) collective-permute-start(bf16[2,144,512]{2,1,0:T(8,128)(2,1)} %get-tuple-element.39), channel_id=1, source_target_pairs={{0,2},{1,3},{2,0},{3,1},{4,6},{5,7},{6,4},{7,5},{8,10},{9,11},{10,... | collective-permute-start | bytes 884744 | tf_op jit(solution)/shard_map/ppermute | solution.py:410
  26.2 19.3 %collective-permute-start.4 = (bf16[2,144,512]{2,1,0:T(8,128)(2,1)}, bf16[2,144,512]{2,1,0:T(8,128)(2,1)S(1)}, u32[]{:S(2)}, u32[]{:S(2)}) collective-permute-start(bf16[2,144,512]{2,1,0:T(8,128)(2,1)} %get-tuple-element.41), channel_id=1, source_target_pairs={{0,7},{1,6},{2,5},{3,4},{4,3},{5,2},{6,1},{7,0},{8,15},{9,14},{10,... | collective-permute-start | bytes 884744 | tf_op jit(solution)/shard_map/ppermute | solution.py:410
  45.5 11.5 %collective-permute-start.5 = (bf16[144,512]{1,0:T(8,128)(2,1)S(1)}, bf16[144,512]{1,0:T(8,128)(2,1)S(1)}, u32[]{:S(2)}, u32[]{:S(2)}) collective-permute-start(bf16[144,512]{1,0:T(8,128)(2,1)S(1)} %slice_bitcast_fusion), channel_id=1, source_target_pairs={{0,2},{1,3},{2,0},{3,1},{4,6},{5,7},{6,4},{7,5},{8,10},{9,11},{10,... | collective-permute-start | bytes 442376 | tf_op jit(solution)/shard_map/ppermute | solution.py:410
  47.5 8.8 %collective-permute-start.3 = (bf16[144,512]{1,0:T(8,128)(2,1)S(1)}, bf16[144,512]{1,0:T(8,128)(2,1)S(1)}, u32[]{:S(2)}, u32[]{:S(2)}) collective-permute-start(bf16[144,512]{1,0:T(8,128)(2,1)S(1)} %get-tuple-element.65), channel_id=1, source_target_pairs={{0,6},{1,7},{2,4},{3,5},{4,2},{5,3},{6,0},{7,1},{8,14},{9,15},{10,... | collective-permute-start | bytes 442376 | tf_op jit(solution)/shard_map/ppermute | solution.py:410
  81.3 12.5 %all-to-all-start.1 = ((f32[32,2,128]{2,1,0:T(2,128)}), f32[32,2,128]{2,1,0:T(2,128)S(1)}, u32[]{:S(2)}, u32[]{:S(2)}) async-start(f32[32,2,128]{2,1,0:T(2,128)} %shard_map.79), calls=%async_computation.1 | async-start | bytes 65536 | tf_op jit(solution)/shard_map/all_to_all | solution.py:450
  95.9 13.0 %all-to-all-start.2 = ((f32[32,2,128]{2,1,0:T(2,128)}), f32[32,2,128]{2,1,0:T(2,128)S(1)}, u32[]{:S(2)}, u32[]{:S(2)}) async-start(f32[32,2,128]{2,1,0:T(2,128)} %get-tuple-element.43), calls=%async_computation.2 | async-start | bytes 65536 | tf_op jit(solution)/shard_map/all_to_all | solution.py:450
  123.5 45.0 %all-to-all-start.3 = ((bf16[256,8,256]{2,1,0:T(8,128)(2,1)}), bf16[256,8,256]{2,1,0:T(8,128)(2,1)S(1)}, u32[]{:S(2)}, u32[]{:S(2)}) async-start(bf16[256,8,256]{2,1,0:T(8,128)(2,1)} %bitcast.58), calls=%async_computation.3 | async-start | bytes 2097152 | tf_op jit(solution)/shard_map/all_to_all | solution.py:450
  134.1 5.7 %collective-permute-start.8 = (bf16[2,128,256]{2,1,0:T(8,128)(2,1)S(1)}, bf16[2,128,256]{2,1,0:T(8,128)(2,1)S(1)}, u32[]{:S(2)}, u32[]{:S(2)}) collective-permute-start(bf16[2,128,256]{2,1,0:T(8,128)(2,1)S(1)} %copy-done.6), channel_id=1, source_target_pairs={{0,2},{1,3},{2,0},{3,1},{4,6},{5,7},{6,4},{7,5},{8,10},{9,11},{10,... | collective-permute-start | bytes 393224 | tf_op jit(solution)/shard_map/ppermute | solution.py:410
  135.5 14.4 %collective-permute-start.15 = (bf16[2,512,128]{2,1,0:T(8,128)(2,1)S(1)}, bf16[2,512,128]{2,1,0:T(8,128)(2,1)S(1)}, u32[]{:S(2)}, u32[]{:S(2)}) collective-permute-start(bf16[2,512,128]{2,1,0:T(8,128)(2,1)S(1)} %copy-done.4), channel_id=1, source_target_pairs={{0,2},{1,3},{2,0},{3,1},{4,6},{5,7},{6,4},{7,5},{8,10},{9,11},{10,... | collective-permute-start | bytes 786440 | tf_op jit(solution)/shard_map/ppermute | solution.py:410
  135.6 23.3 %collective-permute-start.11 = (bf16[2,128,256]{2,1,0:T(8,128)(2,1)S(1)}, bf16[2,128,256]{2,1,0:T(8,128)(2,1)S(1)}, u32[]{:S(2)}, u32[]{:S(2)}) collective-permute-start(bf16[2,128,256]{2,1,0:T(8,128)(2,1)S(1)} %copy-done.5), channel_id=1, source_target_pairs={{0,7},{1,6},{2,5},{3,4},{4,3},{5,2},{6,1},{7,0},{8,15},{9,14},{10,... | collective-permute-start | bytes 393224 | tf_op jit(solution)/shard_map/ppermute | solution.py:410
  139.0 20.1 %collective-permute-start.14 = (bf16[512,128]{1,0:T(8,128)(2,1)}, bf16[512,128]{1,0:T(8,128)(2,1)S(1)}, u32[]{:S(2)}, u32[]{:S(2)}) collective-permute-start(bf16[512,128]{1,0:T(8,128)(2,1)} %get-tuple-element.58), channel_id=1, source_target_pairs={{0,1},{1,0},{2,3},{3,2},{4,5},{5,4},{6,7},{7,6},{8,9},{9,8},{10,11... | collective-permute-start | bytes 393224 | tf_op jit(solution)/shard_map/ppermute | solution.py:410
  139.0 20.9 %collective-permute-start.16 = (bf16[512,128]{1,0:T(8,128)(2,1)}, bf16[512,128]{1,0:T(8,128)(2,1)S(1)}, u32[]{:S(2)}, u32[]{:S(2)}) collective-permute-start(bf16[512,128]{1,0:T(8,128)(2,1)} %get-tuple-element.60), channel_id=1, source_target_pairs={{0,3},{1,2},{2,1},{3,0},{4,7},{5,6},{6,5},{7,4},{8,11},{9,10},{10,... | collective-permute-start | bytes 393224 | tf_op jit(solution)/shard_map/ppermute | solution.py:410
  139.7 15.7 %collective-permute-start.18 = (bf16[2,512,128]{2,1,0:T(8,128)(2,1)S(1)}, bf16[2,512,128]{2,1,0:T(8,128)(2,1)S(1)}, u32[]{:S(2)}, u32[]{:S(2)}) collective-permute-start(bf16[2,512,128]{2,1,0:T(8,128)(2,1)S(1)} %copy-done.3), channel_id=1, source_target_pairs={{0,7},{1,6},{2,5},{3,4},{4,3},{5,2},{6,1},{7,0},{8,15},{9,14},{10,... | collective-permute-start | bytes 786440 | tf_op jit(solution)/shard_map/ppermute | solution.py:410
  149.9 11.8 %collective-permute-start.20 = (bf16[512,128]{1,0:T(8,128)(2,1)}, bf16[512,128]{1,0:T(8,128)(2,1)S(1)}, u32[]{:S(2)}, u32[]{:S(2)}) collective-permute-start(bf16[512,128]{1,0:T(8,128)(2,1)} %get-tuple-element.62), channel_id=1, source_target_pairs={{0,6},{1,7},{2,4},{3,5},{4,2},{5,3},{6,0},{7,1},{8,14},{9,15},{10,... | collective-permute-start | bytes 393224 | tf_op jit(solution)/shard_map/ppermute | solution.py:410
  155.4 8.3 %collective-permute-start.17 = (bf16[512,128]{1,0:T(8,128)(2,1)S(1)}, bf16[512,128]{1,0:T(8,128)(2,1)S(1)}, u32[]{:S(2)}, u32[]{:S(2)}) collective-permute-start(bf16[512,128]{1,0:T(8,128)(2,1)S(1)} %get-tuple-element.69), channel_id=1, source_target_pairs={{0,6},{1,7},{2,4},{3,5},{4,2},{5,3},{6,0},{7,1},{8,14},{9,15},{10,... | collective-permute-start | bytes 393224 | tf_op jit(solution)/shard_map/ppermute | solution.py:410
  159.0 6.2 %collective-permute-start.19 = (bf16[512,128]{1,0:T(8,128)(2,1)S(1)}, bf16[512,128]{1,0:T(8,128)(2,1)S(1)}, u32[]{:S(2)}, u32[]{:S(2)}) collective-permute-start(bf16[512,128]{1,0:T(8,128)(2,1)S(1)} %get-tuple-element.68), channel_id=1, source_target_pairs={{0,2},{1,3},{2,0},{3,1},{4,6},{5,7},{6,4},{7,5},{8,10},{9,11},{10,... | collective-permute-start | bytes 393224 | tf_op jit(solution)/shard_map/ppermute | solution.py:410
  159.1 8.0 %collective-permute-start.7 = (bf16[128,256]{1,0:T(8,128)(2,1)S(1)}, bf16[128,256]{1,0:T(8,128)(2,1)S(1)}, u32[]{:S(2)}, u32[]{:S(2)}) collective-permute-start(bf16[128,256]{1,0:T(8,128)(2,1)S(1)} %copy-done.9), channel_id=1, source_target_pairs={{0,1},{1,0},{2,3},{3,2},{4,5},{5,4},{6,7},{7,6},{8,9},{9,8},{10,11... | collective-permute-start | bytes 196616 | tf_op jit(solution)/shard_map/ppermute | solution.py:410
  160.0 7.1 %collective-permute-start.9 = (bf16[128,256]{1,0:T(8,128)(2,1)S(1)}, bf16[128,256]{1,0:T(8,128)(2,1)S(1)}, u32[]{:S(2)}, u32[]{:S(2)}) collective-permute-start(bf16[128,256]{1,0:T(8,128)(2,1)S(1)} %copy-done.8), channel_id=1, source_target_pairs={{0,3},{1,2},{2,1},{3,0},{4,7},{5,6},{6,5},{7,4},{8,11},{9,10},{10,... | collective-permute-start | bytes 196616 | tf_op jit(solution)/shard_map/ppermute | solution.py:410
  161.7 5.4 %collective-permute-start.13 = (bf16[128,256]{1,0:T(8,128)(2,1)S(1)}, bf16[128,256]{1,0:T(8,128)(2,1)S(1)}, u32[]{:S(2)}, u32[]{:S(2)}) collective-permute-start(bf16[128,256]{1,0:T(8,128)(2,1)S(1)} %copy-done.7), channel_id=1, source_target_pairs={{0,6},{1,7},{2,4},{3,5},{4,2},{5,3},{6,0},{7,1},{8,14},{9,15},{10,... | collective-permute-start | bytes 196616 | tf_op jit(solution)/shard_map/ppermute | solution.py:410
  163.6 4.8 %collective-permute-start.10 = (bf16[128,256]{1,0:T(8,128)(2,1)S(1)}, bf16[128,256]{1,0:T(8,128)(2,1)S(1)}, u32[]{:S(2)}, u32[]{:S(2)}) collective-permute-start(bf16[128,256]{1,0:T(8,128)(2,1)S(1)} %get-tuple-element.73), channel_id=1, source_target_pairs={{0,6},{1,7},{2,4},{3,5},{4,2},{5,3},{6,0},{7,1},{8,14},{9,15},{10,... | collective-permute-start | bytes 196616 | tf_op jit(solution)/shard_map/ppermute | solution.py:410
  (11 other events, 201.4 us)

commit v7 on v6

--- a/solution.py
+++ b/solution.py
@@ -371,17 +371,20 @@
 
 
 def finish_kernel(helpers, pos, picker, returned, *refs):
-    pieces = refs[:helpers]
-    out = refs[helpers]
+    *pieces, out, staged, sems = refs
     width = out.shape[1] // helpers
     slots = picker.shape[1]
+    copies = []
     for k in range(helpers):
         d = pos[1] ^ k
         cols = pl.ds(pl.multiple_of(d * width, width), width)
         terms = returned[d].astype(F32).reshape(slots, width).astype(BF16)
-        out[:, cols] = (dot(picker[...], terms, 1, 0) + pieces[k][...].astype(F32)).astype(
-            BF16
-        )
+        total = dot(picker[...], terms, 1, 0) + pieces[k][...].astype(F32)
+        staged[k] = total.astype(BF16)
+        copies.append(pltpu.make_async_copy(staged.at[k], out.at[:, cols], sems.at[k]))
+        copies[-1].start()
+    for copy in copies:
+        copy.wait()
 
 
 DIRECT = (1, 3, 6)
@@ -552,11 +555,13 @@
 
     pieces = exchange(pieces, helpers)
 
-    query_grad = call(
+    (query_grad,) = call(
         functools.partial(finish_kernel, helpers),
-        shape((rows, features), BF16),
+        [pltpu.HBM((rows, features), BF16)],
         [picker, returned, *query_own],
         position,
+        [pltpu.VMEM((helpers, rows, width), BF16), pltpu.SemaphoreType.DMA((helpers,))],
+        hand_out=(0,),
     )
     key_grad, value_grad = call(
         functools.partial(place_kernel, helpers),

time: 171 us -> 171 us (level)
  no operation moved by 1% of the time
where the time goes in v7:
time: 171 us; the launch traced here: 170 us
  starting transfers between devices  64.3 us (38%)
  waiting for transfers between devices  50.2 us (29%)
  Pallas kernels  43.3 us (25%)
  local copies, waits for them, and re-layouts  11.4 us (7%)
    pallas_call x9, Pallas kernels, call(): pl.pallas_call(kernel, out_shape=outputs, in_specs=specs, **{'out_specs':...  43.3 us
    all_to_all x4, starting transfers between devices, swap(): return lax.all_to_all(array, axes, split_axis=0, concat_axis=0, tiled=True)  34.5 us
    ppermute x21, starting transfers between devices, send(): return lax.ppermute(array, 'help', [(i, i ^ k) for i in range(helpers)])  29.8 us
    ppermute x21, waiting for transfers between devices, send(): return lax.ppermute(array, 'help', [(i, i ^ k) for i in range(helpers)])  28.9 us
    all_to_all x4, waiting for transfers between devices, swap(): return lax.all_to_all(array, axes, split_axis=0, concat_axis=0, tiled=True)  21.2 us
    unnamed x26, local copies, waits for them, and re-layouts  7.7 us
  transfers between devices with their start and end apart: 25, of which 10 were waited for; matrix products, arithmetic and copies ran while one was open for 7% of the time, Pallas kernels for 8%

profile of v7, /device:TPU:1, one launch (start us, length us, event | category | flops | bytes accessed | tf_op | source)
XLA Modules:
  0.0 170.3 jit_solution(11732063174857484133)
XLA Ops:
  0.7 3.6 %shard_map.76 = (bf16[8,32,8,512]{3,2,1,0:T(8,128)(2,1)}, bf16[128,256]{1,0:T(8,128)(2,1)}, bf16[16,512]{1,0:T(8,128)(2,1)}) custom-call(s32[2]{0:T(128)S(1)} %pad_add_fusion.pos, s32[2,128]{1,0:T(2,128)} %bitcast.60, bf16[128,2048]{1,0:T(8,128)(2,1)} %bitcast.54, bf16[128,2048]{1,0:T(8,128)(2,1)} %bitcast.56), custom_call_target="tpu_custom_call" | custom-call | flops 268435456 | tf_op jit(solution)/shard_map/pallas_call | solution.py:441
  4.4 15.7 %all-to-all-start = ((bf16[256,8,512]{2,1,0:T(8,128)(2,1)}), bf16[256,8,512]{2,1,0:T(8,128)(2,1)S(1)}, u32[]{:S(2)}, u32[]{:S(2)}) async-start(bf16[256,8,512]{2,1,0:T(8,128)(2,1)} %bitcast.53), calls=%async_computation | async-start | bytes 4194304 | tf_op jit(solution)/shard_map/all_to_all | solution.py:453
  20.0 2.4 %shard_map.77 = (bf16[144,512]{1,0:T(8,128)(2,1)}, bf16[144,512]{1,0:T(8,128)(2,1)}, bf16[144,512]{1,0:T(8,128)(2,1)}, bf16[144,512]{1,0:T(8,128)(2,1)}, bf16[2,...) custom-call(s32[2]{0:T(128)S(1)} %pad_add_fusion.pos, bf16[128,2048]{1,0:T(8,128)(2,1)} %bitcast.55, ...), custom_call_target="tpu_custom_call" | custom-call | tf_op jit(solution)/shard_map/pallas_call | solution.py:441
  22.4 2.1 %collective-permute-start = (bf16[144,512]{1,0:T(8,128)(2,1)}, bf16[144,512]{1,0:T(8,128)(2,1)}, u32[]{:S(2)}, u32[]{:S(2)}) collective-permute-start(bf16[144,512]{1,0:T(8,128)(2,1)} %get-tuple-element.38), channel_id=1, source_target_pairs={{0,1},{1,0},{2,3},{3,2},{4,5},{5,4},{6,7},{7,6},{8,9},{9,8},{10,11... | collective-permute-start | bytes 442376 | tf_op jit(solution)/shard_map/ppermute | solution.py:413
  26.2 2.7 %collective-permute-start.4 = (bf16[2,144,512]{2,1,0:T(8,128)(2,1)}, bf16[2,144,512]{2,1,0:T(8,128)(2,1)S(1)}, u32[]{:S(2)}, u32[]{:S(2)}) collective-permute-start(bf16[2,144,512]{2,1,0:T(8,128)(2,1)} %get-tuple-element.41), channel_id=1, source_target_pairs={{0,7},{1,6},{2,5},{3,4},{4,3},{5,2},{6,1},{7,0},{8,15},{9,14},{10,... | collective-permute-start | bytes 884744 | tf_op jit(solution)/shard_map/ppermute | solution.py:413
  33.4 12.2 %collective-permute-done.4 = bf16[2,144,512]{2,1,0:T(8,128)(2,1)S(1)} collective-permute-done((bf16[2,144,512]{2,1,0:T(8,128)(2,1)}, bf16[2,144,512]{2,1,0:T(8,128)(2,1)S(1)}, u32[]{:S(2)}, u32[]{:S(2)}) %collective-permute-start.4) | collective-permute-done | bytes 294944 | tf_op jit(solution)/shard_map/ppermute | solution.py:413
  50.3 6.0 %collective-permute-done.3 = bf16[144,512]{1,0:T(8,128)(2,1)S(1)} collective-permute-done((bf16[144,512]{1,0:T(8,128)(2,1)S(1)}, bf16[144,512]{1,0:T(8,128)(2,1)S(1)}, u32[]{:S(2)}, u32[]{:S(2)}) %collective-permute-start.3) | collective-permute-done | bytes 147488 | tf_op jit(solution)/shard_map/ppermute | solution.py:413
  59.3 14.4 %all-to-all-done = bf16[256,8,512]{2,1,0:T(8,128)(2,1)S(1)} async-done(((bf16[256,8,512]{2,1,0:T(8,128)(2,1)}), bf16[256,8,512]{2,1,0:T(8,128)(2,1)S(1)}, u32[]{:S(2)}, u32[]{:S(2)}) %all-to-all-start) | async-done | bytes 2097184 | tf_op jit(solution)/shard_map/all_to_all | solution.py:453
  73.7 7.6 %shard_map.79 = f32[32,2,128]{2,1,0:T(2,128)} custom-call(bf16[8,32,8,512]{3,2,1,0:T(8,128)(2,1)S(1)} %bitcast.51, bf16[1024,256]{1,0:T(8,128)(2,1)S(1)} %get-tuple-element.76.key, bf16[1024,256]{1,0:T(8,128)(2,1)S(1)} %get-tuple-element.75.value), custom_call_target="tpu_custom_call" | custom-call | flops 2147483648 | tf_op jit(solution)/shard_map/pallas_call | solution.py:441
  81.3 3.9 %all-to-all-start.1 = ((f32[32,2,128]{2,1,0:T(2,128)}), f32[32,2,128]{2,1,0:T(2,128)S(1)}, u32[]{:S(2)}, u32[]{:S(2)}) async-start(f32[32,2,128]{2,1,0:T(2,128)} %shard_map.79), calls=%async_computation.1 | async-start | bytes 65536 | tf_op jit(solution)/shard_map/all_to_all | solution.py:453
  85.8 3.1 %shard_map.78.stats = f32[8,1024]{1,0:T(8,128)S(1)} custom-call(s32[2]{0:T(128)S(1)} %pad_add_fusion.pos, bf16[8,144,512]{2,1,0:T(8,128)(2,1)} %slice_dynamic-update-slice_fusion.own, bf16[1024,256]{1,0:T(8,128)(2,1)S(1)} %get-tuple-element.76.key, bf16[1024,256]{1,0:T(8,128)(2,1)S(1)} %get-tuple-element.75.value), custom_call_target="tpu_custom_call" | custom-call | flops 536870912 | tf_op jit(solution)/shard_map/pallas_call | solution.py:441
  88.9 4.9 %all-to-all-done.1.got = f32[32,2,128]{2,1,0:T(2,128)S(1)} async-done(((f32[32,2,128]{2,1,0:T(2,128)}), f32[32,2,128]{2,1,0:T(2,128)S(1)}, u32[]{:S(2)}, u32[]{:S(2)}) %all-to-all-start.1) | async-done | bytes 32800 | tf_op jit(solution)/shard_map/all_to_all | solution.py:453
  93.8 2.1 %shard_map.80 = (f32[4,1024]{1,0:T(4,128)S(1)}, f32[32,2,128]{2,1,0:T(2,128)}) custom-call(f32[8,1024]{1,0:T(8,128)S(1)} %shard_map.78.stats, f32[32,2,128]{2,1,0:T(2,128)S(1)} %all-to-all-done.1.got), custom_call_target="tpu_custom_call" | custom-call | flops 134217728 | tf_op jit(solution)/shard_map/pallas_call | solution.py:441
  95.9 4.5 %all-to-all-start.2 = ((f32[32,2,128]{2,1,0:T(2,128)}), f32[32,2,128]{2,1,0:T(2,128)S(1)}, u32[]{:S(2)}, u32[]{:S(2)}) async-start(f32[32,2,128]{2,1,0:T(2,128)} %get-tuple-element.43), calls=%async_computation.2 | async-start | bytes 65536 | tf_op jit(solution)/shard_map/all_to_all | solution.py:453
  100.4 6.6 %shard_map.81 = (f32[256,1024]{1,0:T(8,128)}, f32[256,1024]{1,0:T(8,128)}, bf16[128,256]{1,0:T(8,128)(2,1)}, bf16[128,256]{1,0:T(8,128)(2,1)}, bf16[128,256]{1,0...) custom-call(s32[2]{0:T(128)S(1)} %pad_add_fusion.pos, ...), custom_call_target="tpu_custom_call" | custom-call | flops 2147483648 | tf_op jit(solution)/shard_map/pallas_call | solution.py:441
  107.0 2.0 %all-to-all-done.2.slots = f32[32,2,128]{2,1,0:T(2,128)S(1)} async-done(((f32[32,2,128]{2,1,0:T(2,128)}), f32[32,2,128]{2,1,0:T(2,128)S(1)}, u32[]{:S(2)}, u32[]{:S(2)}) %all-to-all-start.2) | async-done | bytes 32800 | tf_op jit(solution)/shard_map/all_to_all | solution.py:453
  108.9 14.5 %shard_map.82 = (bf16[8,32,8,256]{3,2,1,0:T(8,128)(2,1)}, bf16[512,128]{1,0:T(8,128)(2,1)}, bf16[512,128]{1,0:T(8,128)(2,1)}, bf16[512,128]{1,0:T(8,128)(2,1)}, ...) custom-call(s32[2]{0:T(128)S(1)} %pad_add_fusion.pos, ...), custom_call_target="tpu_custom_call" | custom-call | flops 5368709120 | tf_op jit(solution)/shard_map/pallas_call | solution.py:441
  123.5 10.5 %all-to-all-start.3 = ((bf16[256,8,256]{2,1,0:T(8,128)(2,1)}), bf16[256,8,256]{2,1,0:T(8,128)(2,1)S(1)}, u32[]{:S(2)}, u32[]{:S(2)}) async-start(bf16[256,8,256]{2,1,0:T(8,128)(2,1)} %bitcast.58), calls=%async_computation.3 | async-start | bytes 2097152 | tf_op jit(solution)/shard_map/all_to_all | solution.py:453
  135.6 3.4 %collective-permute-start.11 = (bf16[2,128,256]{2,1,0:T(8,128)(2,1)S(1)}, bf16[2,128,256]{2,1,0:T(8,128)(2,1)S(1)}, u32[]{:S(2)}, u32[]{:S(2)}) collective-permute-start(bf16[2,128,256]{2,1,0:T(8,128)(2,1)S(1)} %copy-done.5), channel_id=1, source_target_pairs={{0,7},{1,6},{2,5},{3,4},{4,3},{5,2},{6,1},{7,0},{8,15},{9,14},{10,... | collective-permute-start | bytes 393224 | tf_op jit(solution)/shard_map/ppermute | solution.py:413
  139.7 5.5 %collective-permute-start.18 = (bf16[2,512,128]{2,1,0:T(8,128)(2,1)S(1)}, bf16[2,512,128]{2,1,0:T(8,128)(2,1)S(1)}, u32[]{:S(2)}, u32[]{:S(2)}) collective-permute-start(bf16[2,512,128]{2,1,0:T(8,128)(2,1)S(1)} %copy-done.3), channel_id=1, source_target_pairs={{0,7},{1,6},{2,5},{3,4},{4,3},{5,2},{6,1},{7,0},{8,15},{9,14},{10,... | collective-permute-start | bytes 786440 | tf_op jit(solution)/shard_map/ppermute | solution.py:413
  145.2 4.7 %collective-permute-done.15 = bf16[2,512,128]{2,1,0:T(8,128)(2,1)S(1)} collective-permute-done((bf16[2,512,128]{2,1,0:T(8,128)(2,1)S(1)}, bf16[2,512,128]{2,1,0:T(8,128)(2,1)S(1)}, u32[]{:S(2)}, u32[]{:S(2)}) %collective-permute-start.15) | collective-permute-done | bytes 262176 | tf_op jit(solution)/shard_map/ppermute | solution.py:413
  149.9 2.6 %collective-permute-start.20 = (bf16[512,128]{1,0:T(8,128)(2,1)}, bf16[512,128]{1,0:T(8,128)(2,1)S(1)}, u32[]{:S(2)}, u32[]{:S(2)}) collective-permute-start(bf16[512,128]{1,0:T(8,128)(2,1)} %get-tuple-element.62), channel_id=1, source_target_pairs={{0,6},{1,7},{2,4},{3,5},{4,2},{5,3},{6,0},{7,1},{8,14},{9,15},{10,... | collective-permute-start | bytes 393224 | tf_op jit(solution)/shard_map/ppermute | solution.py:413
  152.5 2.9 %collective-permute-done.18 = bf16[2,512,128]{2,1,0:T(8,128)(2,1)S(1)} collective-permute-done((bf16[2,512,128]{2,1,0:T(8,128)(2,1)S(1)}, bf16[2,512,128]{2,1,0:T(8,128)(2,1)S(1)}, u32[]{:S(2)}, u32[]{:S(2)}) %collective-permute-start.18) | collective-permute-done | bytes 262176 | tf_op jit(solution)/shard_map/ppermute | solution.py:413
  155.4 3.5 %collective-permute-start.17 = (bf16[512,128]{1,0:T(8,128)(2,1)S(1)}, bf16[512,128]{1,0:T(8,128)(2,1)S(1)}, u32[]{:S(2)}, u32[]{:S(2)}) collective-permute-start(bf16[512,128]{1,0:T(8,128)(2,1)S(1)} %get-tuple-element.69), channel_id=1, source_target_pairs={{0,6},{1,7},{2,4},{3,5},{4,2},{5,3},{6,0},{7,1},{8,14},{9,15},{10,... | collective-permute-start | bytes 393224 | tf_op jit(solution)/shard_map/ppermute | solution.py:413
  (70 shorter events, 28.0 us)
Async XLA Ops:
  4.4 69.3 %all-to-all-start = ((bf16[256,8,512]{2,1,0:T(8,128)(2,1)}), bf16[256,8,512]{2,1,0:T(8,128)(2,1)S(1)}, u32[]{:S(2)}, u32[]{:S(2)}) async-start(bf16[256,8,512]{2,1,0:T(8,128)(2,1)} %bitcast.53), calls=%async_computation | async-start | bytes 4194304 | tf_op jit(solution)/shard_map/all_to_all | solution.py:453
  22.4 9.4 %collective-permute-start = (bf16[144,512]{1,0:T(8,128)(2,1)}, bf16[144,512]{1,0:T(8,128)(2,1)}, u32[]{:S(2)}, u32[]{:S(2)}) collective-permute-start(bf16[144,512]{1,0:T(8,128)(2,1)} %get-tuple-element.38), channel_id=1, source_target_pairs={{0,1},{1,0},{2,3},{3,2},{4,5},{5,4},{6,7},{7,6},{8,9},{9,8},{10,11... | collective-permute-start | bytes 442376 | tf_op jit(solution)/shard_map/ppermute | solution.py:413
  24.5 24.2 %collective-permute-start.2 = (bf16[144,512]{1,0:T(8,128)(2,1)}, bf16[144,512]{1,0:T(8,128)(2,1)}, u32[]{:S(2)}, u32[]{:S(2)}) collective-permute-start(bf16[144,512]{1,0:T(8,128)(2,1)} %get-tuple-element.40), channel_id=1, source_target_pairs={{0,3},{1,2},{2,1},{3,0},{4,7},{5,6},{6,5},{7,4},{8,11},{9,10},{10,... | collective-permute-start | bytes 442376 | tf_op jit(solution)/shard_map/ppermute | solution.py:413
  24.5 33.2 %collective-permute-start.6 = (bf16[144,512]{1,0:T(8,128)(2,1)}, bf16[144,512]{1,0:T(8,128)(2,1)}, u32[]{:S(2)}, u32[]{:S(2)}) collective-permute-start(bf16[144,512]{1,0:T(8,128)(2,1)} %get-tuple-element.42), channel_id=1, source_target_pairs={{0,6},{1,7},{2,4},{3,5},{4,2},{5,3},{6,0},{7,1},{8,14},{9,15},{10,... | collective-permute-start | bytes 442376 | tf_op jit(solution)/shard_map/ppermute | solution.py:413
  25.9 20.0 %collective-permute-start.1 = (bf16[2,144,512]{2,1,0:T(8,128)(2,1)}, bf16[2,144,512]{2,1,0:T(8,128)(2,1)}, u32[]{:S(2)}, u32[]{:S(2)}) collective-permute-start(bf16[2,144,512]{2,1,0:T(8,128)(2,1)} %get-tuple-element.39), channel_id=1, source_target_pairs={{0,2},{1,3},{2,0},{3,1},{4,6},{5,7},{6,4},{7,5},{8,10},{9,11},{10,... | collective-permute-start | bytes 884744 | tf_op jit(solution)/shard_map/ppermute | solution.py:413
  26.2 19.3 %collective-permute-start.4 = (bf16[2,144,512]{2,1,0:T(8,128)(2,1)}, bf16[2,144,512]{2,1,0:T(8,128)(2,1)S(1)}, u32[]{:S(2)}, u32[]{:S(2)}) collective-permute-start(bf16[2,144,512]{2,1,0:T(8,128)(2,1)} %get-tuple-element.41), channel_id=1, source_target_pairs={{0,7},{1,6},{2,5},{3,4},{4,3},{5,2},{6,1},{7,0},{8,15},{9,14},{10,... | collective-permute-start | bytes 884744 | tf_op jit(solution)/shard_map/ppermute | solution.py:413
  45.5 11.5 %collective-permute-start.5 = (bf16[144,512]{1,0:T(8,128)(2,1)S(1)}, bf16[144,512]{1,0:T(8,128)(2,1)S(1)}, u32[]{:S(2)}, u32[]{:S(2)}) collective-permute-start(bf16[144,512]{1,0:T(8,128)(2,1)S(1)} %slice_bitcast_fusion), channel_id=1, source_target_pairs={{0,2},{1,3},{2,0},{3,1},{4,6},{5,7},{6,4},{7,5},{8,10},{9,11},{10,... | collective-permute-start | bytes 442376 | tf_op jit(solution)/shard_map/ppermute | solution.py:413
  47.5 8.8 %collective-permute-start.3 = (bf16[144,512]{1,0:T(8,128)(2,1)S(1)}, bf16[144,512]{1,0:T(8,128)(2,1)S(1)}, u32[]{:S(2)}, u32[]{:S(2)}) collective-permute-start(bf16[144,512]{1,0:T(8,128)(2,1)S(1)} %get-tuple-element.65), channel_id=1, source_target_pairs={{0,6},{1,7},{2,4},{3,5},{4,2},{5,3},{6,0},{7,1},{8,14},{9,15},{10,... | collective-permute-start | bytes 442376 | tf_op jit(solution)/shard_map/ppermute | solution.py:413
  81.3 12.5 %all-to-all-start.1 = ((f32[32,2,128]{2,1,0:T(2,128)}), f32[32,2,128]{2,1,0:T(2,128)S(1)}, u32[]{:S(2)}, u32[]{:S(2)}) async-start(f32[32,2,128]{2,1,0:T(2,128)} %shard_map.79), calls=%async_computation.1 | async-start | bytes 65536 | tf_op jit(solution)/shard_map/all_to_all | solution.py:453
  95.9 13.0 %all-to-all-start.2 = ((f32[32,2,128]{2,1,0:T(2,128)}), f32[32,2,128]{2,1,0:T(2,128)S(1)}, u32[]{:S(2)}, u32[]{:S(2)}) async-start(f32[32,2,128]{2,1,0:T(2,128)} %get-tuple-element.43), calls=%async_computation.2 | async-start | bytes 65536 | tf_op jit(solution)/shard_map/all_to_all | solution.py:453
  123.5 45.0 %all-to-all-start.3 = ((bf16[256,8,256]{2,1,0:T(8,128)(2,1)}), bf16[256,8,256]{2,1,0:T(8,128)(2,1)S(1)}, u32[]{:S(2)}, u32[]{:S(2)}) async-start(bf16[256,8,256]{2,1,0:T(8,128)(2,1)} %bitcast.58), calls=%async_computation.3 | async-start | bytes 2097152 | tf_op jit(solution)/shard_map/all_to_all | solution.py:453
  134.1 5.7 %collective-permute-start.8 = (bf16[2,128,256]{2,1,0:T(8,128)(2,1)S(1)}, bf16[2,128,256]{2,1,0:T(8,128)(2,1)S(1)}, u32[]{:S(2)}, u32[]{:S(2)}) collective-permute-start(bf16[2,128,256]{2,1,0:T(8,128)(2,1)S(1)} %copy-done.6), channel_id=1, source_target_pairs={{0,2},{1,3},{2,0},{3,1},{4,6},{5,7},{6,4},{7,5},{8,10},{9,11},{10,... | collective-permute-start | bytes 393224 | tf_op jit(solution)/shard_map/ppermute | solution.py:413
  135.5 14.4 %collective-permute-start.15 = (bf16[2,512,128]{2,1,0:T(8,128)(2,1)S(1)}, bf16[2,512,128]{2,1,0:T(8,128)(2,1)S(1)}, u32[]{:S(2)}, u32[]{:S(2)}) collective-permute-start(bf16[2,512,128]{2,1,0:T(8,128)(2,1)S(1)} %copy-done.4), channel_id=1, source_target_pairs={{0,2},{1,3},{2,0},{3,1},{4,6},{5,7},{6,4},{7,5},{8,10},{9,11},{10,... | collective-permute-start | bytes 786440 | tf_op jit(solution)/shard_map/ppermute | solution.py:413
  135.6 23.3 %collective-permute-start.11 = (bf16[2,128,256]{2,1,0:T(8,128)(2,1)S(1)}, bf16[2,128,256]{2,1,0:T(8,128)(2,1)S(1)}, u32[]{:S(2)}, u32[]{:S(2)}) collective-permute-start(bf16[2,128,256]{2,1,0:T(8,128)(2,1)S(1)} %copy-done.5), channel_id=1, source_target_pairs={{0,7},{1,6},{2,5},{3,4},{4,3},{5,2},{6,1},{7,0},{8,15},{9,14},{10,... | collective-permute-start | bytes 393224 | tf_op jit(solution)/shard_map/ppermute | solution.py:413
  139.0 20.1 %collective-permute-start.14 = (bf16[512,128]{1,0:T(8,128)(2,1)}, bf16[512,128]{1,0:T(8,128)(2,1)S(1)}, u32[]{:S(2)}, u32[]{:S(2)}) collective-permute-start(bf16[512,128]{1,0:T(8,128)(2,1)} %get-tuple-element.58), channel_id=1, source_target_pairs={{0,1},{1,0},{2,3},{3,2},{4,5},{5,4},{6,7},{7,6},{8,9},{9,8},{10,11... | collective-permute-start | bytes 393224 | tf_op jit(solution)/shard_map/ppermute | solution.py:413
  139.0 20.9 %collective-permute-start.16 = (bf16[512,128]{1,0:T(8,128)(2,1)}, bf16[512,128]{1,0:T(8,128)(2,1)S(1)}, u32[]{:S(2)}, u32[]{:S(2)}) collective-permute-start(bf16[512,128]{1,0:T(8,128)(2,1)} %get-tuple-element.60), channel_id=1, source_target_pairs={{0,3},{1,2},{2,1},{3,0},{4,7},{5,6},{6,5},{7,4},{8,11},{9,10},{10,... | collective-permute-start | bytes 393224 | tf_op jit(solution)/shard_map/ppermute | solution.py:413
  139.7 15.7 %collective-permute-start.18 = (bf16[2,512,128]{2,1,0:T(8,128)(2,1)S(1)}, bf16[2,512,128]{2,1,0:T(8,128)(2,1)S(1)}, u32[]{:S(2)}, u32[]{:S(2)}) collective-permute-start(bf16[2,512,128]{2,1,0:T(8,128)(2,1)S(1)} %copy-done.3), channel_id=1, source_target_pairs={{0,7},{1,6},{2,5},{3,4},{4,3},{5,2},{6,1},{7,0},{8,15},{9,14},{10,... | collective-permute-start | bytes 786440 | tf_op jit(solution)/shard_map/ppermute | solution.py:413
  149.9 11.8 %collective-permute-start.20 = (bf16[512,128]{1,0:T(8,128)(2,1)}, bf16[512,128]{1,0:T(8,128)(2,1)S(1)}, u32[]{:S(2)}, u32[]{:S(2)}) collective-permute-start(bf16[512,128]{1,0:T(8,128)(2,1)} %get-tuple-element.62), channel_id=1, source_target_pairs={{0,6},{1,7},{2,4},{3,5},{4,2},{5,3},{6,0},{7,1},{8,14},{9,15},{10,... | collective-permute-start | bytes 393224 | tf_op jit(solution)/shard_map/ppermute | solution.py:413
  155.4 8.3 %collective-permute-start.17 = (bf16[512,128]{1,0:T(8,128)(2,1)S(1)}, bf16[512,128]{1,0:T(8,128)(2,1)S(1)}, u32[]{:S(2)}, u32[]{:S(2)}) collective-permute-start(bf16[512,128]{1,0:T(8,128)(2,1)S(1)} %get-tuple-element.69), channel_id=1, source_target_pairs={{0,6},{1,7},{2,4},{3,5},{4,2},{5,3},{6,0},{7,1},{8,14},{9,15},{10,... | collective-permute-start | bytes 393224 | tf_op jit(solution)/shard_map/ppermute | solution.py:413
  159.0 6.2 %collective-permute-start.19 = (bf16[512,128]{1,0:T(8,128)(2,1)S(1)}, bf16[512,128]{1,0:T(8,128)(2,1)S(1)}, u32[]{:S(2)}, u32[]{:S(2)}) collective-permute-start(bf16[512,128]{1,0:T(8,128)(2,1)S(1)} %get-tuple-element.68), channel_id=1, source_target_pairs={{0,2},{1,3},{2,0},{3,1},{4,6},{5,7},{6,4},{7,5},{8,10},{9,11},{10,... | collective-permute-start | bytes 393224 | tf_op jit(solution)/shard_map/ppermute | solution.py:413
  159.1 8.0 %collective-permute-start.7 = (bf16[128,256]{1,0:T(8,128)(2,1)S(1)}, bf16[128,256]{1,0:T(8,128)(2,1)S(1)}, u32[]{:S(2)}, u32[]{:S(2)}) collective-permute-start(bf16[128,256]{1,0:T(8,128)(2,1)S(1)} %copy-done.9), channel_id=1, source_target_pairs={{0,1},{1,0},{2,3},{3,2},{4,5},{5,4},{6,7},{7,6},{8,9},{9,8},{10,11... | collective-permute-start | bytes 196616 | tf_op jit(solution)/shard_map/ppermute | solution.py:413
  160.0 7.1 %collective-permute-start.9 = (bf16[128,256]{1,0:T(8,128)(2,1)S(1)}, bf16[128,256]{1,0:T(8,128)(2,1)S(1)}, u32[]{:S(2)}, u32[]{:S(2)}) collective-permute-start(bf16[128,256]{1,0:T(8,128)(2,1)S(1)} %copy-done.8), channel_id=1, source_target_pairs={{0,3},{1,2},{2,1},{3,0},{4,7},{5,6},{6,5},{7,4},{8,11},{9,10},{10,... | collective-permute-start | bytes 196616 | tf_op jit(solution)/shard_map/ppermute | solution.py:413
  161.7 5.4 %collective-permute-start.13 = (bf16[128,256]{1,0:T(8,128)(2,1)S(1)}, bf16[128,256]{1,0:T(8,128)(2,1)S(1)}, u32[]{:S(2)}, u32[]{:S(2)}) collective-permute-start(bf16[128,256]{1,0:T(8,128)(2,1)S(1)} %copy-done.7), channel_id=1, source_target_pairs={{0,6},{1,7},{2,4},{3,5},{4,2},{5,3},{6,0},{7,1},{8,14},{9,15},{10,... | collective-permute-start | bytes 196616 | tf_op jit(solution)/shard_map/ppermute | solution.py:413
  163.6 4.8 %collective-permute-start.10 = (bf16[128,256]{1,0:T(8,128)(2,1)S(1)}, bf16[128,256]{1,0:T(8,128)(2,1)S(1)}, u32[]{:S(2)}, u32[]{:S(2)}) collective-permute-start(bf16[128,256]{1,0:T(8,128)(2,1)S(1)} %get-tuple-element.73), channel_id=1, source_target_pairs={{0,6},{1,7},{2,4},{3,5},{4,2},{5,3},{6,0},{7,1},{8,14},{9,15},{10,... | collective-permute-start | bytes 196616 | tf_op jit(solution)/shard_map/ppermute | solution.py:413
  (11 other events, 201.4 us)
